TPU v7x, 256 devices: a whole 4x4x8 slice. The times are simulated.
256 devices in a mesh: space: 32 (over y, z_lo, core), scene: 8 (over x, z_hi).
Axes of the slice: x: 4, y: 4, z: 8 (z_hi: 2, z_lo: 4; z = z_hi * 4 + z_lo), core: 2. Of those that a mesh axis runs over, the one named last changes fastest.
Arguments:
- grad_out: bfloat16 [8, 64, 128, 256], P('scene', 'space'), may hold values from -6 to 6
- pre_second: bfloat16 [8, 64, 128, 256], P('scene', 'space'), may hold values from -6 to 6
- pre_first: bfloat16 [8, 64, 128, 256], P('scene', 'space'), may hold values from -6 to 6
- camera_bev: bfloat16 [8, 64, 128, 80], P('scene', 'space'), may hold values from -6 to 6
- lidar_bev: bfloat16 [8, 64, 128, 256], P('scene', 'space'), may hold values from -6 to 6
- weight_a: bfloat16 [256, 3024], replicated, may hold values from -0.109375 to 0.109375
- weight_b: bfloat16 [256, 2304], replicated, may hold values from -0.125 to 0.125
- depth_weights: bfloat16 [8, 118, 4096], P('scene', None, 'space'), may hold values from 0 to 1
- context: bfloat16 [8, 80, 4096], P('scene', None, 'space'), may hold values from -6 to 6
- block_list: int32 [32, 32, 1], P(None, 'space'), may hold values from -1 to 1, as said below
- point_slot: int32 [118, 4096], P(None, 'space'), may hold values from 0 to 4095, as said below
Outputs:
- weight_grad_a: float32 [256, 3024], P('space')
- weight_grad_b: float32 [256, 2304], P('space')
- grad_lidar: bfloat16 [8, 64, 128, 256], P('scene', 'space')
- grad_context: float32 [8, 80, 4096], P('scene', None, 'space')
- grad_depth: float32 [8, 118, 4096], P('scene', None, 'space')
Inputs may be any that keep to these rules, and one draw needn't show every extreme that they name: block_list[d, s, k] is a block of 128 cells of device s's rows owed to frustum owner d, distinct within (d, s), or -1 for an empty slot; live slots come first; every owner has a live slot from itself; in every draw some owner has all 1 slots live from every device. point_slot[d, p] = (s + k) * 128 + q names cell q of the block in a live slot k from device s, for the owner of pixel p.
All inputs are finite; a program needn't handle non-finite values.
Results may differ from a plain program's by a relative error of at most 0.005.
Values may be sent and summed in bfloat16 or wider, within the bound.
No kernel may reach another device: no remote copies, remote signals or barrier semaphores. Data moves between devices by JAX's collectives and lax.ppermute only.
A program may use at most 64 MiB of HBM per device.

v0:
```python
import functools
import math

import jax
import jax.numpy as jnp
from jax import lax
from jax.experimental import pallas as pl
from jax.experimental.pallas import tpu as pltpu
from jax.sharding import PartitionSpec as P


f32 = jnp.float32
bf16 = jnp.bfloat16
NN = (((1,), (0,)), ((), ()))
NT = (((1,), (1,)), ((), ()))


def mm(a, b, dims):
    return lax.dot_general(a, b, dims, preferred_element_type=f32)


def shifted_columns(rows, step, cols):
    if step == 0:
        return rows
    zero = jnp.zeros((1, rows.shape[1]), rows.dtype)
    out = []
    for r in range(rows.shape[0] // cols):
        row = rows[r * cols : (r + 1) * cols]
        out += [row[1:], zero] if step > 0 else [zero, row[:-1]]
    return jnp.concatenate(out, axis=0)


TILE = 128


def load_kernel(*refs):
    count = (len(refs) - 2) // 2
    moves = [pltpu.make_async_copy(refs[k], refs[count + 1 + k], refs[-1].at[k]) for k in range(count)]
    for move in moves:
        move.start()
    for move in moves:
        move.wait()


def local_kernel(dims, own_ref, before_ref, after_ref, first_ref, lid_ref, cam_ref, wa_ref, wb_ref, spot_ref,
                 lidar_ref, blocks_hbm, keep_ref, send_ref,
                 g_ref, a_ref, gt_ref, at_ref, pick_ref, block_sems):
    cols, ch, cam, parts = dims
    lid = lid_ref.shape[2]
    fan = cam + lid
    half = ch // 2
    ext = jnp.concatenate(
        [before_ref[0], before_ref[1], own_ref[0], own_ref[1], after_ref[0], after_ref[1]], axis=0
    ).astype(f32)
    for b in range(3):
        moved = shifted_columns(ext, b - 1, cols)
        g_ref[b] = moved.astype(bf16)
        gt_ref[b] = moved[cols : 5 * cols].T.astype(bf16)
    back = jnp.zeros((4 * cols, ch), f32)
    for a in range(3):
        for b in range(3):
            tap = (3 * (2 - a) + (2 - b)) * ch
            back += mm(g_ref[b, a * cols : (a + 4) * cols, :], wb_ref[:, tap : tap + ch], NN)
    first = jnp.concatenate([before_ref[2], first_ref[0], first_ref[1], after_ref[2]], axis=0).astype(f32)
    grad_a = jnp.where(first > 0, back, 0.0).astype(bf16).astype(f32)
    for b in range(3):
        moved = shifted_columns(grad_a, b - 1, cols)
        a_ref[b] = moved.astype(bf16)
        at_ref[b] = moved.T.astype(bf16)
    lidar = jnp.zeros((2 * cols, lid), f32)
    camera = jnp.zeros((cam, 2 * cols), f32)
    for a in range(3):
        for b in range(3):
            tap = (3 * (2 - a) + (2 - b)) * fan
            rows = a_ref[b, a * cols : (a + 2) * cols, :]
            lidar += mm(rows, wa_ref[tap + cam : tap + fan, :], NT)
            camera += mm(wa_ref[tap : tap + cam, :], rows, NT)
    for r in range(2):
        lidar_ref[r] = lidar[r * cols : (r + 1) * cols].astype(bf16)
    for r in range(2):
        pick_ref[r] = camera[:, r * cols : (r + 1) * cols].astype(bf16)
    picks = [
        pltpu.make_async_copy(pick_ref.at[jnp.where(spot_ref[2 + k] > 0, 1, 0)], blocks_hbm.at[k], block_sems.at[k])
        for k in range(blocks_hbm.shape[0])
    ]
    for pick in picks:
        pick.start()

    second_core = spot_ref[0] > 0
    per_part = keep_ref.shape[2] // TILE

    def put(value, tile):
        halves = value.reshape(ch // 16, 2, 8, value.shape[1])
        even = halves[:, 0].reshape(half, value.shape[1])
        odd = halves[:, 1].reshape(half, value.shape[1])
        mine = jnp.where(second_core, odd, even)
        other = jnp.where(second_core, even, odd).astype(bf16)
        for t in range(value.shape[1] // TILE):
            part, at = divmod(tile + t, per_part)
            part = part ^ spot_ref[1]
            here = slice(at * TILE, (at + 1) * TILE)
            keep_ref[part, :, here] = mine[:, t * TILE : (t + 1) * TILE]
            send_ref[part, :, here] = other[:, t * TILE : (t + 1) * TILE]

    hidden = jnp.maximum(jnp.concatenate([first_ref[0], first_ref[1]], axis=0), 0)
    lidar_in = jnp.concatenate([lid_ref[0], lid_ref[1]], axis=0)
    camera_in = jnp.concatenate([cam_ref[0], cam_ref[1]], axis=1)
    b_tiles, a_tiles = ch // TILE, lid // TILE
    packed = []
    for a in range(3):
        for b in range(3):
            tap = 3 * a + b
            window = slice((2 - a) * cols, (4 - a) * cols)
            put(mm(gt_ref[2 - b, :, window], hidden, NN), tap * b_tiles)
            put(mm(at_ref[2 - b, :, window], lidar_in, NN), 9 * b_tiles + tap * a_tiles)
            packed.append(mm(at_ref[2 - b, :, window], camera_in, NT))
    at = 9 * (b_tiles + a_tiles)
    spare = (parts * per_part - at) * TILE - 9 * cam
    packed.append(jnp.zeros((ch, spare), f32))
    put(jnp.concatenate(packed, axis=1), at)
    for pick in picks:
        pick.wait()


def depth_kernel(blocks_ref, weight_ref, context_ref, slot_ref, gc_ref, gd_ref, wt_ref, st_ref, s_ref, m_ref, d_ref):
    sources, cam, cells_of = blocks_ref.shape
    depth, pix = slot_ref.shape
    wide = st_ref.shape[1]
    wt_ref[...] = jnp.concatenate([weight_ref[...].astype(f32), jnp.zeros((wide - depth, pix), f32)], axis=0).T
    st_ref[...] = jnp.concatenate([slot_ref[...], jnp.full((wide - depth, pix), -1, jnp.int32)], axis=0).T
    context_t = context_ref[...].astype(f32).T.astype(bf16)
    pitch = s_ref.shape[0] // sources
    for s in range(sources):
        s_ref[s * pitch : s * pitch + pix, :] = mm(context_t, blocks_ref[s], NN)
    cells = lax.broadcasted_iota(jnp.int32, (cells_of, wide), 0)
    places = lax.broadcasted_iota(jnp.int32, (sources, wide), 0)
    shift = cells_of.bit_length() - 1

    def pixels(g, carry):
        base = pl.multiple_of(g * 8, 8)
        slots = st_ref[pl.ds(base, 8), :]
        weights = wt_ref[pl.ds(base, 8), :]
        found_rows = []
        for k in range(8):
            slot = slots[k : k + 1]
            at_cell = jnp.where(cells == (slot & (cells_of - 1)), 1.0, 0.0).astype(bf16)
            here = places == (slot >> shift)
            every = pl.ds(base + k, sources, stride=pitch)
            m_ref[every, :] = mm(jnp.where(here, weights[k : k + 1], 0.0).astype(bf16), at_cell, NT)
            found = mm(s_ref[every, :].astype(bf16), at_cell, NN)
            found_rows.append(jnp.sum(jnp.where(here, found, 0.0), axis=0, keepdims=True))
        d_ref[pl.ds(base, 8), :] = jnp.concatenate(found_rows, axis=0)
        return carry

    lax.fori_loop(0, pix // 8, pixels, 0)
    gd_ref[...] = d_ref[...].T[:depth]
    total = jnp.zeros((cam, pix), f32)
    for s in range(sources):
        total += mm(blocks_ref[s], m_ref[s * pitch : s * pitch + pix, :].astype(bf16), NT)
    gc_ref[...] = total


def first_sum(keep_ref, other_ref, a_ref, b_ref):
    rows = a_ref.shape[1]
    for k, (upper, lower) in enumerate([(1, 3), (2, 2)]):
        a_ref[k] = (keep_ref[upper, :rows] + other_ref[upper, :rows].astype(f32)).astype(bf16)
        b_ref[k] = (keep_ref[lower, rows:] + other_ref[lower, rows:].astype(f32)).astype(bf16)


def kept_sum(keep_ref, other_ref, own_ref, next_ref):
    rows = own_ref.shape[0] // 2
    upper, lower = slice(0, rows), slice(rows, 2 * rows)
    own_ref[...] = keep_ref[0] + other_ref[0].astype(f32)
    next_ref[upper] = keep_ref[3, upper] + other_ref[3, upper].astype(f32)
    next_ref[lower] = keep_ref[1, lower] + other_ref[1, lower].astype(f32)


def second_sum(own_ref, next_ref, a_ref, b_ref, out_ref, a_out_ref, b_out_ref):
    rows = a_ref.shape[1]
    upper, lower = slice(0, rows), slice(rows, 2 * rows)
    a_out_ref[...] = (next_ref[upper] + a_ref[1].astype(f32)).astype(bf16)
    b_out_ref[...] = (next_ref[lower] + b_ref[1].astype(f32)).astype(bf16)
    out_ref[upper] = own_ref[upper] + a_ref[0].astype(f32)
    out_ref[lower] = own_ref[lower] + b_ref[0].astype(f32)


def third_sum(own_ref, a_ref, b_ref, out_ref):
    rows = a_ref.shape[0]
    out_ref[:rows] = (own_ref[:rows] + a_ref[...].astype(f32)).astype(bf16)
    out_ref[rows:] = (own_ref[rows:] + b_ref[...].astype(f32)).astype(bf16)


def place_sum(parts_ref, out_ref):
    out_ref[...] = jnp.sum(parts_ref[...].astype(f32), axis=0).astype(bf16)


def pair_sum(one_ref, two_ref, out_ref):
    out_ref[...] = one_ref[...].astype(f32) + two_ref[...].astype(f32)


def last_sum(dims, scale, *refs):
    ch, lid, cam = dims
    *parts, spot_ref, wa_ref, wb_ref, all_ref = refs
    for k, part in enumerate(parts):
        all_ref[k ^ spot_ref[1]] = part[...]
    whole = jnp.concatenate([all_ref[x] for x in range(len(parts))], axis=1) * scale
    wb_ref[...] = whole[:, : 9 * ch]
    pieces = []
    for tap in range(9):
        at = 9 * (ch + lid) + tap * cam
        pieces += [whole[:, at : at + cam], whole[:, 9 * ch + tap * lid : 9 * ch + (tap + 1) * lid]]
    wa_ref[...] = jnp.concatenate(pieces, axis=1)


def call(kernel, outs, scratch, args, specs, flops, traffic, outs_at=None, limit=24):
    return pl.pallas_call(
        kernel,
        out_shape=outs,
        in_specs=specs,
        out_specs=outs_at or [VM] * len(outs),
        scratch_shapes=scratch,
        cost_estimate=pl.CostEstimate(flops=flops, bytes_accessed=traffic, transcendentals=0),
        compiler_params=pltpu.CompilerParams(vmem_limit_bytes=limit << 20),
    )(*[pltpu.with_memory_space_constraint(x, pltpu.HBM) if spec is HB else x for x, spec in zip(args, specs)])


def small(kernel, outs, args):
    outs = [jax.ShapeDtypeStruct(shape, dtype) for shape, dtype in outs]
    traffic = sum(x.size * x.dtype.itemsize for x in (*args, *outs))
    return call(kernel, outs, [], args, [VM] * len(args), traffic, traffic)


VM = pl.BlockSpec(memory_space=pltpu.VMEM)
SM = pl.BlockSpec(memory_space=pltpu.SMEM)
HB = pl.BlockSpec(memory_space=pltpu.HBM)


def neighbours(x, reverse):
    n = lax.axis_size("space")
    pairs = [(i, i + 1) for i in range(n - 1)]
    return lax.ppermute(x, "space", [(j, i) for i, j in pairs] if reverse else pairs)


def exchanged(x, axis, groups):
    return lax.all_to_all(x, axis, 0, 0, axis_index_groups=groups, tiled=True)


def swapped(x, axis, partner):
    return lax.ppermute(x, axis, [(i, partner(i)) for i in range(lax.axis_size(axis))])


def summed_along_x(keep, send):
    _, rows, per_part = keep.shape
    deep = rows // 2
    other = swapped(send, "space", lambda i: i ^ 1)
    a, b = small(first_sum, [((2, deep, per_part), bf16)] * 2, (keep, other))
    a, b = swapped(a, "scene", lambda i: i ^ 2), swapped(b, "scene", lambda i: i ^ 6)
    kept = small(kept_sum, [((2 * deep, per_part), f32)] * 2, (keep, other))
    own, a, b = small(
        second_sum,
        [((2 * deep, per_part), f32), ((deep, per_part), bf16), ((deep, per_part), bf16)],
        (*kept, a, b),
    )
    a, b = swapped(a, "scene", lambda i: i ^ 6), swapped(b, "scene", lambda i: i ^ 2)
    (part,) = small(third_sum, [((2 * deep, per_part), bf16)], (own, a, b))
    return part


def over_scenes(part, spot, dims, scale):
    ch, lid, cam = dims
    (own,) = small(pair_sum, [(part.shape, f32)], (part, swapped(part, "scene", lambda i: i ^ 1)))
    parts = [own] + [swapped(own, "scene", lambda i, k=k: i ^ 2 * k) for k in range(1, 4)]
    return call(
        functools.partial(last_sum, dims, scale),
        [jax.ShapeDtypeStruct((8, 9 * width), f32) for width in (cam + lid, ch)],
        [pltpu.VMEM((len(parts), *own.shape), f32)],
        (*parts, spot),
        [VM] * len(parts) + [SM],
        400_000,
        400_000,
    )


def shards(
    grad_out, pre_second, pre_first, camera_bev, lidar_bev, weight_a, weight_b,
    depth_weights, context, block_list, point_slot,
):
    _, rows, cols, ch = grad_out.shape
    cam, lid = camera_bev.shape[-1], lidar_bev.shape[-1]
    space, scenes = lax.axis_size("space"), lax.axis_size("scene")
    pix = point_slot.shape[1]
    place = space // 2
    reach = scenes // 2
    scale = 1.0 / math.sqrt(rows * cols * space * scenes)
    first = pre_first[0]
    grad_b = jnp.where(pre_second[0] > 0, grad_out[0], jnp.zeros((), bf16))
    before = neighbours(jnp.concatenate([grad_b, first[-1:]]), False)
    after = neighbours(jnp.concatenate([grad_b, first[:1]]), True)
    camera = jnp.swapaxes(camera_bev[0], 1, 2)
    spot = jnp.concatenate(
        [(lax.axis_index("space") & 1).reshape(1), (lax.axis_index("scene") >> 1).reshape(1), block_list[:, 0, 0]]
    )

    tiles = 9 * (ch + lid) // TILE + -(-9 * cam // TILE)
    per_part = -(-tiles // reach) * TILE
    shape = jax.ShapeDtypeStruct
    own_data = (first, lidar_bev[0], camera, weight_a.T, weight_b)
    loaded = call(
        load_kernel,
        [pltpu.VMEM(x.shape, x.dtype) for x in own_data],
        [pltpu.SemaphoreType.DMA((len(own_data),))],
        (*own_data, spot),
        [HB] * len(own_data) + [SM],
        2_000_000,
        3_000_000,
    )
    lidar, blocks, keep, send = call(
        functools.partial(local_kernel, (cols, ch, cam, reach)),
        [
            shape((rows, cols, lid), bf16),
            pltpu.HBM((space, cam, cols), bf16),
            shape((reach, ch // 2, per_part), f32),
            shape((reach, ch // 2, per_part), bf16),
        ],
        [
            pltpu.VMEM((3, 6 * cols, ch), bf16),
            pltpu.VMEM((3, 4 * cols, ch), bf16),
            pltpu.VMEM((3, ch, 4 * cols), bf16),
            pltpu.VMEM((3, ch, 4 * cols), bf16),
            pltpu.VMEM((2, cam, cols), bf16),
            pltpu.SemaphoreType.DMA((space,)),
        ],
        (grad_b, before, after, *loaded, spot),
        [VM] * 8 + [SM],
        1_800_000_000,
        12_000_000,
        outs_at=[VM, HB, VM, VM],
    )
    incoming = exchanged(blocks, "space", None)
    part = summed_along_x(keep, send)
    incoming, part = lax.optimization_barrier((incoming, part))
    along_yz = exchanged(
        part.reshape(place, 8, per_part), "space", [[2 * i + c for i in range(place)] for c in range(2)]
    )
    grad_context, grad_depth = call(
        depth_kernel,
        [shape((cam, pix), f32), shape(point_slot.shape, f32)],
        [
            pltpu.VMEM((pix, 128), f32),
            pltpu.VMEM((pix, 128), jnp.int32),
            pltpu.VMEM((space * (pix + 8), cols), f32),
            pltpu.VMEM((space * (pix + 8), cols), f32),
            pltpu.VMEM((pix, 128), f32),
        ],
        (incoming, depth_weights[0], context[0], point_slot),
        [VM] * 4,
        2_000_000_000,
        2_000_000,
    )
    along_yz, grad_context, grad_depth = lax.optimization_barrier((along_yz, grad_context, grad_depth))
    (part,) = small(place_sum, [((8, per_part), bf16)], (along_yz,))
    grad_wa, grad_wb = over_scenes(part, spot, (ch, lid, cam), scale)
    return grad_wa, grad_wb, lidar[None], grad_context[None], grad_depth[None]


def solution(mesh):
    field = P("scene", "space", None, None)
    pixels = P("scene", None, "space")
    return jax.shard_map(
        shards,
        mesh=mesh,
        in_specs=(field,) * 5 + (P(), P(), pixels, pixels, P(None, "space", None), P(None, "space")),
        out_specs=(P("space", None), P("space", None), field, pixels, pixels),
        check_vma=False,
    )
```

profile of v0, /device:TPU:2, one launch (start us, length us, event | category | flops | bytes accessed | tf_op | source)
XLA Modules:
  0.0 87.2 jit_solution(3493415505270081039)
XLA Ops:
  1.5 1.0 %fusion.own_ref = bf16[2,128,256]{2,1,0:T(8,128)(2,1)S(1)} fusion(bf16[1,2,128,256]{3,2,1,0:T(8,128)(2,1)} %param.11, bf16[1,2,128,256]{3,2,1,0:T(8,128)(2,1)} %param.12), kind=kLoop, calls=%fused_computation.3 | loop fusion | flops 131072 | bytes 393216 | tf_op jit(solution)/shard_map/jit(_where)/select_n | solution.py:296
  2.5 1.3 %collective-permute-start.1 = (bf16[3,128,256]{2,1,0:T(8,128)(2,1)S(1)}, bf16[3,128,256]{2,1,0:T(8,128)(2,1)S(1)}, u32[]{:S(2)}, u32[]{:S(2)}) collective-permute-start(bf16[3,128,256]{2,1,0:T(8,128)(2,1)S(1)} %get-tuple-element.60), channel_id=1, source_target_pairs={{8,0},{16,8},{24,16},{32,24},{40,32},{48,40},{56,48},{64,56},{72,6... | collective-permute-start | bytes 589832 | tf_op jit(solution)/shard_map/ppermute | solution.py:241
  3.8 3.0 %collective-permute-start = (bf16[3,128,256]{2,1,0:T(8,128)(2,1)S(1)}, bf16[3,128,256]{2,1,0:T(8,128)(2,1)S(1)}, u32[]{:S(2)}, u32[]{:S(2)}) collective-permute-start(bf16[3,128,256]{2,1,0:T(8,128)(2,1)S(1)} %get-tuple-element.61), channel_id=1, source_target_pairs={{0,8},{8,16},{16,24},{24,32},{32,40},{40,48},{48,56},{56,64},{64,7... | collective-permute-start | bytes 589832 | tf_op jit(solution)/shard_map/ppermute | solution.py:241
  7.6 2.5 %shard_map.146 = (bf16[2,128,256]{2,1,0:T(8,128)(2,1)S(1)}, bf16[2,128,256]{2,1,0:T(8,128)(2,1)S(1)}, bf16[2,80,128]{2,1,0:T(8,128)(2,1)S(1)}, bf16[3024,256]{1,0:T(8,128)(2,1)S(1)}, bf16[256,2304]{1,0:T(8,128)(2,1)S(1)}) custom-call(bf16[2,128,256]{2,1,0:T(8,128)(2,1)} %bitcast.25, bf16[2,128,256]{2,1,0:T(8,128)(2,1)} %bitcast.26, ...), custom_call_target="tpu_custom_call" | custom-call | flops 2000000 | bytes 3000000 | tf_op jit(solution)/shard_map/pallas_call | solution.py:216
  10.2 6.5 %shard_map.147 = (bf16[2,128,256]{2,1,0:T(8,128)(2,1)}, bf16[32,80,128]{2,1,0:T(8,128)(2,1)}, f32[4,128,1408]{2,1,0:T(8,128)S(1)}, bf16[4,128,1408]{2,1,0:T(8,128)(2,1)}) custom-call(bf16[2,128,256]{2,1,0:T(8,128)(2,1)S(1)} %fusion.own_ref, bf16[3,128,256]{2,1,0:T(8,128)(2,1)S(1)} %collective-permute-done.before_ref, ...), custom_call_target="tpu_custom_call" | custom-call | flops 1800000000 | bytes 12000000 | tf_op jit(solution)/shard_map/pallas_call | solution.py:216
  16.6 1.6 %collective-permute-start.2 = (bf16[4,128,1408]{2,1,0:T(8,128)(2,1)}, bf16[4,128,1408]{2,1,0:T(8,128)(2,1)}, u32[]{:S(2)}, u32[]{:S(2)}) collective-permute-start(bf16[4,128,1408]{2,1,0:T(8,128)(2,1)} %get-tuple-element.37), channel_id=1, source_target_pairs={{0,8},{8,0},{16,24},{24,16},{32,40},{40,32},{48,56},{56,48},{64,72... | collective-permute-start | bytes 4325384 | tf_op jit(solution)/shard_map/ppermute | solution.py:249
  18.2 11.5 %all-to-all-start = ((bf16[32,80,128]{2,1,0:T(8,128)(2,1)}), bf16[32,80,128]{2,1,0:T(8,128)(2,1)S(1)}, u32[]{:S(2)}, u32[]{:S(2)}) async-start(bf16[32,80,128]{2,1,0:T(8,128)(2,1)} %get-tuple-element.35), calls=%async_computation | async-start | bytes 1310720 | tf_op jit(solution)/shard_map/all_to_all | solution.py:245
  29.8 1.5 %shard_map.149 = (bf16[2,64,1408]{2,1,0:T(8,128)(2,1)S(1)}, bf16[2,64,1408]{2,1,0:T(8,128)(2,1)S(1)}) custom-call(f32[4,128,1408]{2,1,0:T(8,128)S(1)} %get-tuple-element.36.keep_ref, bf16[4,128,1408]{2,1,0:T(8,128)(2,1)} %collective-permute-done.2.other_ref), custom_call_target="tpu_custom_call" | custom-call | flops 5046272 | bytes 5046272 | tf_op jit(solution)/shard_map/pallas_call | solution.py:216
  31.9 2.2 %collective-permute-start.4 = (bf16[2,64,1408]{2,1,0:T(8,128)(2,1)S(1)}, bf16[2,64,1408]{2,1,0:T(8,128)(2,1)S(1)}, u32[]{:S(2)}, u32[]{:S(2)}) collective-permute-start(bf16[2,64,1408]{2,1,0:T(8,128)(2,1)S(1)} %get-tuple-element.41), channel_id=1, source_target_pairs={{0,6},{1,7},{2,4},{3,5},{4,2},{5,3},{6,0},{7,1},{8,14},{9,15},{10,... | collective-permute-start | bytes 1081352 | tf_op jit(solution)/shard_map/ppermute | solution.py:249
  34.1 1.5 %shard_map.148 = (f32[128,1408]{1,0:T(8,128)S(1)}, f32[128,1408]{1,0:T(8,128)S(1)}) custom-call(f32[4,128,1408]{2,1,0:T(8,128)S(1)} %get-tuple-element.36.keep_ref, bf16[4,128,1408]{2,1,0:T(8,128)(2,1)} %collective-permute-done.2.other_ref), custom_call_target="tpu_custom_call" | custom-call | flops 5767168 | bytes 5767168 | tf_op jit(solution)/shard_map/pallas_call | solution.py:216
  35.6 6.4 %collective-permute-done.3.a_ref = bf16[2,64,1408]{2,1,0:T(8,128)(2,1)S(1)} collective-permute-done((bf16[2,64,1408]{2,1,0:T(8,128)(2,1)S(1)}, bf16[2,64,1408]{2,1,0:T(8,128)(2,1)S(1)}, u32[]{:S(2)}, u32[]{:S(2)}) %collective-permute-start.3) | collective-permute-done | bytes 360480 | tf_op jit(solution)/shard_map/ppermute | solution.py:249
  42.8 1.8 %collective-permute-start.5 = (bf16[64,1408]{1,0:T(8,128)(2,1)S(1)}, bf16[64,1408]{1,0:T(8,128)(2,1)S(1)}, u32[]{:S(2)}, u32[]{:S(2)}) collective-permute-start(bf16[64,1408]{1,0:T(8,128)(2,1)S(1)} %get-tuple-element.43), channel_id=1, source_target_pairs={{0,6},{1,7},{2,4},{3,5},{4,2},{5,3},{6,0},{7,1},{8,14},{9,15},{10,... | collective-permute-start | bytes 540680 | tf_op jit(solution)/shard_map/ppermute | solution.py:249
  44.6 2.6 %collective-permute-start.6 = (bf16[64,1408]{1,0:T(8,128)(2,1)S(1)}, bf16[64,1408]{1,0:T(8,128)(2,1)S(1)}, u32[]{:S(2)}, u32[]{:S(2)}) collective-permute-start(bf16[64,1408]{1,0:T(8,128)(2,1)S(1)} %get-tuple-element.44), channel_id=1, source_target_pairs={{0,2},{1,3},{2,0},{3,1},{4,6},{5,7},{6,4},{7,5},{8,10},{9,11},{10,... | collective-permute-start | bytes 540680 | tf_op jit(solution)/shard_map/ppermute | solution.py:249
  47.3 1.5 %collective-permute-done.5.a_ref = bf16[64,1408]{1,0:T(8,128)(2,1)S(1)} collective-permute-done((bf16[64,1408]{1,0:T(8,128)(2,1)S(1)}, bf16[64,1408]{1,0:T(8,128)(2,1)S(1)}, u32[]{:S(2)}, u32[]{:S(2)}) %collective-permute-start.5) | collective-permute-done | bytes 180256 | tf_op jit(solution)/shard_map/ppermute | solution.py:249
  48.8 2.1 %collective-permute-done.6.b_ref = bf16[64,1408]{1,0:T(8,128)(2,1)S(1)} collective-permute-done((bf16[64,1408]{1,0:T(8,128)(2,1)S(1)}, bf16[64,1408]{1,0:T(8,128)(2,1)S(1)}, u32[]{:S(2)}, u32[]{:S(2)}) %collective-permute-start.6) | collective-permute-done | bytes 180256 | tf_op jit(solution)/shard_map/ppermute | solution.py:249
  51.6 7.2 %all-to-all-start.1 = ((bf16[16,8,1408]{2,1,0:T(8,128)(2,1)}), bf16[16,8,1408]{2,1,0:T(8,128)(2,1)S(1)}, u32[]{:S(2)}, u32[]{:S(2)}) async-start(bf16[16,8,1408]{2,1,0:T(8,128)(2,1)} %bitcast.11), calls=%async_computation.1 | async-start | bytes 720896 | tf_op jit(solution)/shard_map/all_to_all | solution.py:245
  58.8 7.4 %shard_map.152 = (f32[80,128]{1,0:T(8,128)}, f32[118,128]{1,0:T(8,128)S(1)}) custom-call(bf16[32,80,128]{2,1,0:T(8,128)(2,1)S(1)} %all-to-all-done.blocks_ref, bf16[118,128]{1,0:T(8,128)(2,1)S(1)} %bitcast.22, bf16[80,128]{1,0:T(8,128)(2,1)S(1)} %bitcast.23, s32[118,128]{1,0:T(8,128)S(1)} %copy-done), custom_call_target="tpu_custom_call" | custom-call | flops 2000000000 | bytes 2000000 | tf_op jit(solution)/shard_map/pallas_call | solution.py:216
  66.2 3.7 %all-to-all-done.1.parts_ref = bf16[16,8,1408]{2,1,0:T(8,128)(2,1)S(1)} async-done(((bf16[16,8,1408]{2,1,0:T(8,128)(2,1)}), bf16[16,8,1408]{2,1,0:T(8,128)(2,1)S(1)}, u32[]{:S(2)}, u32[]{:S(2)}) %all-to-all-start.1) | async-done | bytes 360480 | tf_op jit(solution)/shard_map/all_to_all | solution.py:245
  70.0 4.6 %collective-permute-start.7 = (bf16[8,1408]{1,0:T(8,128)(2,1)S(1)}, bf16[8,1408]{1,0:T(8,128)(2,1)S(1)}, u32[]{:S(2)}, u32[]{:S(2)}) collective-permute-start(bf16[8,1408]{1,0:T(8,128)(2,1)S(1)} %shard_map.153.one_ref), channel_id=1, source_target_pairs={{0,1},{1,0},{2,3},{3,2},{4,5},{5,4},{6,7},{7,6},{8,9},{9,8},{10,11... | collective-permute-start | bytes 67592 | tf_op jit(solution)/shard_map/ppermute | solution.py:249
  74.6 3.2 %collective-permute-done.7.two_ref = bf16[8,1408]{1,0:T(8,128)(2,1)S(1)} collective-permute-done((bf16[8,1408]{1,0:T(8,128)(2,1)S(1)}, bf16[8,1408]{1,0:T(8,128)(2,1)S(1)}, u32[]{:S(2)}, u32[]{:S(2)}) %collective-permute-start.7) | collective-permute-done | bytes 22560 | tf_op jit(solution)/shard_map/ppermute | solution.py:249
  78.6 3.3 %collective-permute-start.9 = (f32[8,1408]{1,0:T(8,128)S(1)}, f32[8,1408]{1,0:T(8,128)S(1)}, u32[]{:S(2)}, u32[]{:S(2)}) collective-permute-start(f32[8,1408]{1,0:T(8,128)S(1)} %shard_map.154.refs_0_), channel_id=1, source_target_pairs={{0,4},{1,5},{2,6},{3,7},{4,0},{5,1},{6,2},{7,3},{8,12},{9,13},{10,... | collective-permute-start | bytes 135176 | tf_op jit(solution)/shard_map/ppermute | solution.py:249
  82.7 1.5 %collective-permute-done.9.refs_2_ = f32[8,1408]{1,0:T(8,128)S(1)} collective-permute-done((f32[8,1408]{1,0:T(8,128)S(1)}, f32[8,1408]{1,0:T(8,128)S(1)}, u32[]{:S(2)}, u32[]{:S(2)}) %collective-permute-start.9) | collective-permute-done | bytes 45088 | tf_op jit(solution)/shard_map/ppermute | solution.py:249
  84.1 1.8 %collective-permute-done.8.refs_1_ = f32[8,1408]{1,0:T(8,128)S(1)} collective-permute-done((f32[8,1408]{1,0:T(8,128)S(1)}, f32[8,1408]{1,0:T(8,128)S(1)}, u32[]{:S(2)}, u32[]{:S(2)}) %collective-permute-start.8) | collective-permute-done | bytes 45088 | tf_op jit(solution)/shard_map/ppermute | solution.py:249
  85.9 1.3 %shard_map.155 = (f32[8,3024]{1,0:T(8,128)}, f32[8,2304]{1,0:T(8,128)}) custom-call(f32[8,1408]{1,0:T(8,128)S(1)} %shard_map.154.refs_0_, f32[8,1408]{1,0:T(8,128)S(1)} %collective-permute-done.8.refs_1_, f32[8,1408]{1,0:T(8,128)S(1)} %collective-permute-done.9.refs_2_, f32[8,1408]{1,0:T(8,128)S(1)} %collective-permute-done.10.refs_3_, ...), custom_call_target="tpu_custom_call" | custom-call | flops 400000 | bytes 400000 | tf_op jit(solution)/shard_map/pallas_call | solution.py:216
  (23 shorter events, 5.5 us)
Async XLA Ops:
  2.5 7.6 %collective-permute-start.1 = (bf16[3,128,256]{2,1,0:T(8,128)(2,1)S(1)}, bf16[3,128,256]{2,1,0:T(8,128)(2,1)S(1)}, u32[]{:S(2)}, u32[]{:S(2)}) collective-permute-start(bf16[3,128,256]{2,1,0:T(8,128)(2,1)S(1)} %get-tuple-element.60), channel_id=1, source_target_pairs={{8,0},{16,8},{24,16},{32,24},{40,32},{48,40},{56,48},{64,56},{72,6... | collective-permute-start | bytes 589832 | tf_op jit(solution)/shard_map/ppermute | solution.py:241
  3.8 6.3 %collective-permute-start = (bf16[3,128,256]{2,1,0:T(8,128)(2,1)S(1)}, bf16[3,128,256]{2,1,0:T(8,128)(2,1)S(1)}, u32[]{:S(2)}, u32[]{:S(2)}) collective-permute-start(bf16[3,128,256]{2,1,0:T(8,128)(2,1)S(1)} %get-tuple-element.61), channel_id=1, source_target_pairs={{0,8},{8,16},{16,24},{24,32},{32,40},{40,48},{48,56},{56,64},{64,7... | collective-permute-start | bytes 589832 | tf_op jit(solution)/shard_map/ppermute | solution.py:241
  16.6 13.1 %collective-permute-start.2 = (bf16[4,128,1408]{2,1,0:T(8,128)(2,1)}, bf16[4,128,1408]{2,1,0:T(8,128)(2,1)}, u32[]{:S(2)}, u32[]{:S(2)}) collective-permute-start(bf16[4,128,1408]{2,1,0:T(8,128)(2,1)} %get-tuple-element.37), channel_id=1, source_target_pairs={{0,8},{8,0},{16,24},{24,16},{32,40},{40,32},{48,56},{56,48},{64,72... | collective-permute-start | bytes 4325384 | tf_op jit(solution)/shard_map/ppermute | solution.py:249
  18.2 33.4 %all-to-all-start = ((bf16[32,80,128]{2,1,0:T(8,128)(2,1)}), bf16[32,80,128]{2,1,0:T(8,128)(2,1)S(1)}, u32[]{:S(2)}, u32[]{:S(2)}) async-start(bf16[32,80,128]{2,1,0:T(8,128)(2,1)} %get-tuple-element.35), calls=%async_computation | async-start | bytes 1310720 | tf_op jit(solution)/shard_map/all_to_all | solution.py:245
  31.3 10.7 %collective-permute-start.3 = (bf16[2,64,1408]{2,1,0:T(8,128)(2,1)S(1)}, bf16[2,64,1408]{2,1,0:T(8,128)(2,1)S(1)}, u32[]{:S(2)}, u32[]{:S(2)}) collective-permute-start(bf16[2,64,1408]{2,1,0:T(8,128)(2,1)S(1)} %get-tuple-element.40), channel_id=1, source_target_pairs={{0,2},{1,3},{2,0},{3,1},{4,6},{5,7},{6,4},{7,5},{8,10},{9,11},{10,... | collective-permute-start | bytes 1081352 | tf_op jit(solution)/shard_map/ppermute | solution.py:249
  31.9 10.7 %collective-permute-start.4 = (bf16[2,64,1408]{2,1,0:T(8,128)(2,1)S(1)}, bf16[2,64,1408]{2,1,0:T(8,128)(2,1)S(1)}, u32[]{:S(2)}, u32[]{:S(2)}) collective-permute-start(bf16[2,64,1408]{2,1,0:T(8,128)(2,1)S(1)} %get-tuple-element.41), channel_id=1, source_target_pairs={{0,6},{1,7},{2,4},{3,5},{4,2},{5,3},{6,0},{7,1},{8,14},{9,15},{10,... | collective-permute-start | bytes 1081352 | tf_op jit(solution)/shard_map/ppermute | solution.py:249
  42.8 16.0 %copy-start = (s32[118,128]{1,0:T(8,128)S(1)}, s32[118,128]{1,0:T(8,128)}, u32[]{:S(2)}) copy-start(s32[118,128]{1,0:T(8,128)} %slot_ref.1) | copy-start | bytes 181252
  42.8 16.0 %copy-start.1 = (bf16[1,118,128]{2,1,0:T(8,128)(2,1)S(1)}, bf16[1,118,128]{2,1,0:T(8,128)(2,1)}, u32[]{:S(2)}) copy-start(bf16[1,118,128]{2,1,0:T(8,128)(2,1)} %param.18) | copy-start | bytes 90628
  42.8 16.0 %copy-start.2 = (bf16[1,80,128]{2,1,0:T(8,128)(2,1)S(1)}, bf16[1,80,128]{2,1,0:T(8,128)(2,1)}, u32[]{:S(2)}) copy-start(bf16[1,80,128]{2,1,0:T(8,128)(2,1)} %param.19) | copy-start | bytes 61444
  42.8 6.0 %collective-permute-start.5 = (bf16[64,1408]{1,0:T(8,128)(2,1)S(1)}, bf16[64,1408]{1,0:T(8,128)(2,1)S(1)}, u32[]{:S(2)}, u32[]{:S(2)}) collective-permute-start(bf16[64,1408]{1,0:T(8,128)(2,1)S(1)} %get-tuple-element.43), channel_id=1, source_target_pairs={{0,6},{1,7},{2,4},{3,5},{4,2},{5,3},{6,0},{7,1},{8,14},{9,15},{10,... | collective-permute-start | bytes 540680 | tf_op jit(solution)/shard_map/ppermute | solution.py:249
  44.6 6.2 %collective-permute-start.6 = (bf16[64,1408]{1,0:T(8,128)(2,1)S(1)}, bf16[64,1408]{1,0:T(8,128)(2,1)S(1)}, u32[]{:S(2)}, u32[]{:S(2)}) collective-permute-start(bf16[64,1408]{1,0:T(8,128)(2,1)S(1)} %get-tuple-element.44), channel_id=1, source_target_pairs={{0,2},{1,3},{2,0},{3,1},{4,6},{5,7},{6,4},{7,5},{8,10},{9,11},{10,... | collective-permute-start | bytes 540680 | tf_op jit(solution)/shard_map/ppermute | solution.py:249
  51.6 18.3 %all-to-all-start.1 = ((bf16[16,8,1408]{2,1,0:T(8,128)(2,1)}), bf16[16,8,1408]{2,1,0:T(8,128)(2,1)S(1)}, u32[]{:S(2)}, u32[]{:S(2)}) async-start(bf16[16,8,1408]{2,1,0:T(8,128)(2,1)} %bitcast.11), calls=%async_computation.1 | async-start | bytes 720896 | tf_op jit(solution)/shard_map/all_to_all | solution.py:245
  70.0 7.8 %collective-permute-start.7 = (bf16[8,1408]{1,0:T(8,128)(2,1)S(1)}, bf16[8,1408]{1,0:T(8,128)(2,1)S(1)}, u32[]{:S(2)}, u32[]{:S(2)}) collective-permute-start(bf16[8,1408]{1,0:T(8,128)(2,1)S(1)} %shard_map.153.one_ref), channel_id=1, source_target_pairs={{0,1},{1,0},{2,3},{3,2},{4,5},{5,4},{6,7},{7,6},{8,9},{9,8},{10,11... | collective-permute-start | bytes 67592 | tf_op jit(solution)/shard_map/ppermute | solution.py:249
  77.8 4.9 %collective-permute-start.10 = (f32[8,1408]{1,0:T(8,128)S(1)}, f32[8,1408]{1,0:T(8,128)S(1)}, u32[]{:S(2)}, u32[]{:S(2)}) collective-permute-start(f32[8,1408]{1,0:T(8,128)S(1)} %shard_map.154.refs_0_), channel_id=1, source_target_pairs={{0,6},{1,7},{2,4},{3,5},{4,2},{5,3},{6,0},{7,1},{8,14},{9,15},{10,... | collective-permute-start | bytes 135176 | tf_op jit(solution)/shard_map/ppermute | solution.py:249
  78.6 5.6 %collective-permute-start.9 = (f32[8,1408]{1,0:T(8,128)S(1)}, f32[8,1408]{1,0:T(8,128)S(1)}, u32[]{:S(2)}, u32[]{:S(2)}) collective-permute-start(f32[8,1408]{1,0:T(8,128)S(1)} %shard_map.154.refs_0_), channel_id=1, source_target_pairs={{0,4},{1,5},{2,6},{3,7},{4,0},{5,1},{6,2},{7,3},{8,12},{9,13},{10,... | collective-permute-start | bytes 135176 | tf_op jit(solution)/shard_map/ppermute | solution.py:249
  81.8 4.0 %collective-permute-start.8 = (f32[8,1408]{1,0:T(8,128)S(1)}, f32[8,1408]{1,0:T(8,128)S(1)}, u32[]{:S(2)}, u32[]{:S(2)}) collective-permute-start(f32[8,1408]{1,0:T(8,128)S(1)} %shard_map.154.refs_0_), channel_id=1, source_target_pairs={{0,2},{1,3},{2,0},{3,1},{4,6},{5,7},{6,4},{7,5},{8,10},{9,11},{10,... | collective-permute-start | bytes 135176 | tf_op jit(solution)/shard_map/ppermute | solution.py:249
where the time goes:
time: 87.7 us; the launch traced here: 87.2 us
  starting transfers between devices  40.6 us (46%)
  Pallas kernels  21.7 us (25%)
  waiting for transfers between devices  20.7 us (24%)
  other arithmetic  1.75 us (2%)
  local copies, waits for them, and re-layouts  1.59 us (2%)
    pallas_call x10, Pallas kernels, call(): pl.pallas_call(kernel, out_shape=outs, in_specs=specs, out_specs=outs_at...  21.7 us
    all_to_all x2, starting transfers between devices, exchanged(): return lax.all_to_all(x, axis, 0, 0, axis_index_groups=groups, tiled=True)  18.7 us
    ppermute x9, starting transfers between devices, swapped(): lax.ppermute(x, axis, [(i, partner(i)) for i in range(lax.axis_size(axis))])  17.6 us
    ppermute x9, waiting for transfers between devices, swapped(): lax.ppermute(x, axis, [(i, partner(i)) for i in range(lax.axis_size(axis))])  17.1 us
    ppermute x2, starting transfers between devices, neighbours(): lax.ppermute(x, 'space', [(j, i) for i, j in pairs] if reverse else pairs)  4.33 us
    all_to_all x2, waiting for transfers between devices, exchanged(): return lax.all_to_all(x, axis, 0, 0, axis_index_groups=groups, tiled=True)  3.69 us
  transfers between devices with their start and end apart: 13, of which 8 were waited for; matrix products, arithmetic and copies ran while one was open for 2% of the time, Pallas kernels for 16%

commit v1 on v0

--- a/solution.py
+++ b/solution.py
@@ -33,12 +33,37 @@
 TILE = 128
 
 
-def load_kernel(*refs):
-    count = (len(refs) - 2) // 2
-    moves = [pltpu.make_async_copy(refs[k], refs[count + 1 + k], refs[-1].at[k]) for k in range(count)]
+def started(sources, targets, sems):
+    moves = [pltpu.make_async_copy(source, target, sems.at[k]) for k, (source, target) in enumerate(zip(sources, targets))]
     for move in moves:
         move.start()
-    for move in moves:
+    return moves
+
+
+def passed(grad_ref, second_ref):
+    return jnp.where(second_ref[...].astype(f32) > 0, grad_ref[...].astype(f32), 0.0).astype(bf16)
+
+
+def halo_kernel(grad_hbm, second_hbm, first_hbm, down_ref, up_ref, grad_ref, second_ref, first_ref, sems):
+    for move in started((grad_hbm, second_hbm, first_hbm), (grad_ref, second_ref, first_ref), sems):
+        move.wait()
+    rows = first_ref.shape[0]
+    grad_b = passed(grad_ref, second_ref)
+    down_ref[:rows] = grad_b
+    up_ref[:rows] = grad_b
+    down_ref[rows] = first_ref[rows - 1]
+    up_ref[rows] = first_ref[0]
+
+
+def load_kernel(*refs):
+    count = (len(refs) - 3) // 2
+    sources, own_ref, targets = refs[:count], refs[count + 1], refs[count + 2 : -3]
+    grad_ref, second_ref, sems = refs[-3:]
+    moves = started(sources, (grad_ref, second_ref, *targets), sems)
+    moves[0].wait()
+    moves[1].wait()
+    own_ref[...] = passed(grad_ref, second_ref)
+    for move in moves[2:]:
         move.wait()
 
 
@@ -55,7 +80,7 @@
     for b in range(3):
         moved = shifted_columns(ext, b - 1, cols)
         g_ref[b] = moved.astype(bf16)
-        gt_ref[b] = moved[cols : 5 * cols].T.astype(bf16)
+        gt_ref[b] = moved[cols : 5 * cols].astype(bf16).T
     back = jnp.zeros((4 * cols, ch), f32)
     for a in range(3):
         for b in range(3):
@@ -66,7 +91,7 @@
     for b in range(3):
         moved = shifted_columns(grad_a, b - 1, cols)
         a_ref[b] = moved.astype(bf16)
-        at_ref[b] = moved.T.astype(bf16)
+        at_ref[b] = moved.astype(bf16).T
     lidar = jnp.zeros((2 * cols, lid), f32)
     camera = jnp.zeros((cam, 2 * cols), f32)
     for a in range(3):
@@ -293,9 +318,17 @@
     reach = scenes // 2
     scale = 1.0 / math.sqrt(rows * cols * space * scenes)
     first = pre_first[0]
-    grad_b = jnp.where(pre_second[0] > 0, grad_out[0], jnp.zeros((), bf16))
-    before = neighbours(jnp.concatenate([grad_b, first[-1:]]), False)
-    after = neighbours(jnp.concatenate([grad_b, first[:1]]), True)
+    shape = jax.ShapeDtypeStruct
+    down, up = call(
+        halo_kernel,
+        [shape((k, cols, ch), bf16) for k in (rows + 1, rows + 1)],
+        [pltpu.VMEM(first.shape, bf16)] * 3 + [pltpu.SemaphoreType.DMA((3,))],
+        (grad_out[0], pre_second[0], first),
+        [HB] * 3,
+        1_000_000,
+        1_000_000,
+    )
+    before, after = neighbours(down, False), neighbours(up, True)
     camera = jnp.swapaxes(camera_bev[0], 1, 2)
     spot = jnp.concatenate(
         [(lax.axis_index("space") & 1).reshape(1), (lax.axis_index("scene") >> 1).reshape(1), block_list[:, 0, 0]]
@@ -303,16 +336,15 @@
 
     tiles = 9 * (ch + lid) // TILE + -(-9 * cam // TILE)
     per_part = -(-tiles // reach) * TILE
-    shape = jax.ShapeDtypeStruct
     own_data = (first, lidar_bev[0], camera, weight_a.T, weight_b)
-    loaded = call(
+    grad_b, *loaded = call(
         load_kernel,
-        [pltpu.VMEM(x.shape, x.dtype) for x in own_data],
-        [pltpu.SemaphoreType.DMA((len(own_data),))],
-        (*own_data, spot),
-        [HB] * len(own_data) + [SM],
+        [pltpu.VMEM(x.shape, x.dtype) for x in (first, *own_data)],
+        [pltpu.VMEM(first.shape, bf16)] * 2 + [pltpu.SemaphoreType.DMA((2 + len(own_data),))],
+        (grad_out[0], pre_second[0], *own_data, spot),
+        [HB] * (2 + len(own_data)) + [SM],
         2_000_000,
-        3_000_000,
+        3_500_000,
     )
     lidar, blocks, keep, send = call(
         functools.partial(local_kernel, (cols, ch, cam, reach)),

time: 87.7 us -> 88 us (level)
  starting transfers between devices: 40.6 us -> 42.8 us
  Pallas kernels: 21.7 us -> 23 us
  other arithmetic: 1.75 us -> 0.73 us
  waiting for transfers between devices: 20.7 us -> 19.7 us
  local copies, waits for them, and re-layouts: 1.59 us -> 0.7 us
    ppermute x9, starting transfers between devices: 17.6 us -> 23.7 us  [swapped(): lax.ppermute(x, axis, [(i, partner(i)) for i in range(lax.axis_size(axis))])]
    all_to_all x2, starting transfers between devices: 18.7 us -> 16 us  [exchanged(): return lax.all_to_all(x, axis, 0, 0, axis_index_groups=groups, tiled=True)]
    ppermute x9, waiting for transfers between devices: 17.1 us -> 15.6 us  [swapped(): lax.ppermute(x, axis, [(i, partner(i)) for i in range(lax.axis_size(axis))])]
    ppermute x2, starting transfers between devices: 4.33 us -> 3.04 us  [neighbours(): lax.ppermute(x, 'space', [(j, i) for i, j in pairs] if reverse else pairs)]
    pallas_call x10 -> x11, Pallas kernels: 21.7 us -> 23 us  [call(): pl.pallas_call(kernel, out_shape=outs, in_specs=specs, out_specs=outs_at...]
    select_n x1 -> x0, other arithmetic: 0.99 us -> none  [shards(): grad_b = jnp.where(pre_second[0] > 0, grad_out[0], jnp.zeros((), bf16))]
    slice x1 -> x0, local copies, waits for them, and re-layouts: 0.88 us -> none  [shards(): after = neighbours(jnp.concatenate([grad_b, first[:1]]), True)]
  transfers between devices with their start and end apart: 13 -> 13, of which waited for: 8 -> 9; matrix products, arithmetic and copies ran while one was open for 2% -> 2% of each run, Pallas kernels for 16% -> 16%
where the time goes in v1:
time: 88 us; the launch traced here: 87.6 us
  starting transfers between devices  42.8 us (49%)
  Pallas kernels  23 us (26%)
  waiting for transfers between devices  19.7 us (22%)
    ppermute x9, starting transfers between devices, swapped(): lax.ppermute(x, axis, [(i, partner(i)) for i in range(lax.axis_size(axis))])  23.7 us
    pallas_call x11, Pallas kernels, call(): pl.pallas_call(kernel, out_shape=outs, in_specs=specs, out_specs=outs_at...  23 us
    all_to_all x2, starting transfers between devices, exchanged(): return lax.all_to_all(x, axis, 0, 0, axis_index_groups=groups, tiled=True)  16 us
    ppermute x9, waiting for transfers between devices, swapped(): lax.ppermute(x, axis, [(i, partner(i)) for i in range(lax.axis_size(axis))])  15.6 us
    all_to_all x2, waiting for transfers between devices, exchanged(): return lax.all_to_all(x, axis, 0, 0, axis_index_groups=groups, tiled=True)  3.68 us
    ppermute x2, starting transfers between devices, neighbours(): lax.ppermute(x, 'space', [(j, i) for i, j in pairs] if reverse else pairs)  3.04 us
  transfers between devices with their start and end apart: 13, of which 9 were waited for; matrix products, arithmetic and copies ran while one was open for 2% of the time, Pallas kernels for 16%

profile of v1, /device:TPU:2, one launch (start us, length us, event | category | flops | bytes accessed | tf_op | source)
XLA Modules:
  0.0 87.6 jit_solution(4939186944438470607)
XLA Ops:
  0.6 1.1 %shard_map.147 = (bf16[3,128,256]{2,1,0:T(8,128)(2,1)S(1)}, bf16[3,128,256]{2,1,0:T(8,128)(2,1)S(1)}) custom-call(bf16[2,128,256]{2,1,0:T(8,128)(2,1)} %bitcast.21, bf16[2,128,256]{2,1,0:T(8,128)(2,1)} %bitcast.23, bf16[2,128,256]{2,1,0:T(8,128)(2,1)} %bitcast.25), custom_call_target="tpu_custom_call" | custom-call | flops 1000000 | bytes 1000000 | tf_op jit(solution)/shard_map/pallas_call | solution.py:241
  1.7 1.8 %collective-permute-start = (bf16[3,128,256]{2,1,0:T(8,128)(2,1)S(1)}, bf16[3,128,256]{2,1,0:T(8,128)(2,1)S(1)}, u32[]{:S(2)}, u32[]{:S(2)}) collective-permute-start(bf16[3,128,256]{2,1,0:T(8,128)(2,1)S(1)} %get-tuple-element.34), channel_id=1, source_target_pairs={{0,8},{8,16},{16,24},{24,32},{32,40},{40,48},{48,56},{56,64},{64,7... | collective-permute-start | bytes 589832 | tf_op jit(solution)/shard_map/ppermute | solution.py:266
  3.5 1.3 %collective-permute-start.1 = (bf16[3,128,256]{2,1,0:T(8,128)(2,1)S(1)}, bf16[3,128,256]{2,1,0:T(8,128)(2,1)S(1)}, u32[]{:S(2)}, u32[]{:S(2)}) collective-permute-start(bf16[3,128,256]{2,1,0:T(8,128)(2,1)S(1)} %get-tuple-element.35), channel_id=1, source_target_pairs={{8,0},{16,8},{24,16},{32,24},{40,32},{48,40},{56,48},{64,56},{72,6... | collective-permute-start | bytes 589832 | tf_op jit(solution)/shard_map/ppermute | solution.py:266
  5.5 2.6 %shard_map.146 = (bf16[2,128,256]{2,1,0:T(8,128)(2,1)S(1)}, bf16[2,128,256]{2,1,0:T(8,128)(2,1)S(1)}, bf16[2,128,256]{2,1,0:T(8,128)(2,1)S(1)}, bf16[2,80,128]{2...) custom-call(bf16[2,128,256]{2,1,0:T(8,128)(2,1)} %bitcast.22, ...), custom_call_target="tpu_custom_call" | custom-call | flops 2000000 | bytes 3500000 | tf_op jit(solution)/shard_map/pallas_call | solution.py:241
  8.5 6.5 %shard_map.148 = (bf16[2,128,256]{2,1,0:T(8,128)(2,1)}, bf16[32,80,128]{2,1,0:T(8,128)(2,1)}, f32[4,128,1408]{2,1,0:T(8,128)S(1)}, bf16[4,128,1408]{2,1,0:T(8,128)(2,1)}) custom-call(bf16[2,128,256]{2,1,0:T(8,128)(2,1)S(1)} %get-tuple-element.33.own_ref, bf16[3,128,256]{2,1,0:T(8,128)(2,1)S(1)} %collective-permute-done.before_ref, ...), custom_call_target="tpu_custom_call" | custom-call | flops 1800000000 | bytes 12000000 | tf_op jit(solution)/shard_map/pallas_call | solution.py:241
  15.0 5.0 %collective-permute-start.2 = (bf16[4,128,1408]{2,1,0:T(8,128)(2,1)}, bf16[4,128,1408]{2,1,0:T(8,128)(2,1)}, u32[]{:S(2)}, u32[]{:S(2)}) collective-permute-start(bf16[4,128,1408]{2,1,0:T(8,128)(2,1)} %get-tuple-element.43), channel_id=1, source_target_pairs={{0,8},{8,0},{16,24},{24,16},{32,40},{40,32},{48,56},{56,48},{64,72... | collective-permute-start | bytes 4325384 | tf_op jit(solution)/shard_map/ppermute | solution.py:274
  20.1 8.8 %all-to-all-start = ((bf16[32,80,128]{2,1,0:T(8,128)(2,1)}), bf16[32,80,128]{2,1,0:T(8,128)(2,1)S(1)}, u32[]{:S(2)}, u32[]{:S(2)}) async-start(bf16[32,80,128]{2,1,0:T(8,128)(2,1)} %get-tuple-element.41), calls=%async_computation | async-start | bytes 1310720 | tf_op jit(solution)/shard_map/all_to_all | solution.py:270
  28.9 1.5 %shard_map.150 = (bf16[2,64,1408]{2,1,0:T(8,128)(2,1)S(1)}, bf16[2,64,1408]{2,1,0:T(8,128)(2,1)S(1)}) custom-call(f32[4,128,1408]{2,1,0:T(8,128)S(1)} %get-tuple-element.42.keep_ref, bf16[4,128,1408]{2,1,0:T(8,128)(2,1)} %collective-permute-done.2.other_ref), custom_call_target="tpu_custom_call" | custom-call | flops 5046272 | bytes 5046272 | tf_op jit(solution)/shard_map/pallas_call | solution.py:241
  31.1 2.2 %collective-permute-start.4 = (bf16[2,64,1408]{2,1,0:T(8,128)(2,1)S(1)}, bf16[2,64,1408]{2,1,0:T(8,128)(2,1)S(1)}, u32[]{:S(2)}, u32[]{:S(2)}) collective-permute-start(bf16[2,64,1408]{2,1,0:T(8,128)(2,1)S(1)} %get-tuple-element.47), channel_id=1, source_target_pairs={{0,6},{1,7},{2,4},{3,5},{4,2},{5,3},{6,0},{7,1},{8,14},{9,15},{10,... | collective-permute-start | bytes 1081352 | tf_op jit(solution)/shard_map/ppermute | solution.py:274
  33.2 1.5 %shard_map.149 = (f32[128,1408]{1,0:T(8,128)S(1)}, f32[128,1408]{1,0:T(8,128)S(1)}) custom-call(f32[4,128,1408]{2,1,0:T(8,128)S(1)} %get-tuple-element.42.keep_ref, bf16[4,128,1408]{2,1,0:T(8,128)(2,1)} %collective-permute-done.2.other_ref), custom_call_target="tpu_custom_call" | custom-call | flops 5767168 | bytes 5767168 | tf_op jit(solution)/shard_map/pallas_call | solution.py:241
  34.7 6.4 %collective-permute-done.3.a_ref = bf16[2,64,1408]{2,1,0:T(8,128)(2,1)S(1)} collective-permute-done((bf16[2,64,1408]{2,1,0:T(8,128)(2,1)S(1)}, bf16[2,64,1408]{2,1,0:T(8,128)(2,1)S(1)}, u32[]{:S(2)}, u32[]{:S(2)}) %collective-permute-start.3) | collective-permute-done | bytes 360480 | tf_op jit(solution)/shard_map/ppermute | solution.py:274
  41.9 1.8 %collective-permute-start.5 = (bf16[64,1408]{1,0:T(8,128)(2,1)S(1)}, bf16[64,1408]{1,0:T(8,128)(2,1)S(1)}, u32[]{:S(2)}, u32[]{:S(2)}) collective-permute-start(bf16[64,1408]{1,0:T(8,128)(2,1)S(1)} %get-tuple-element.49), channel_id=1, source_target_pairs={{0,6},{1,7},{2,4},{3,5},{4,2},{5,3},{6,0},{7,1},{8,14},{9,15},{10,... | collective-permute-start | bytes 540680 | tf_op jit(solution)/shard_map/ppermute | solution.py:274
  43.8 2.6 %collective-permute-start.6 = (bf16[64,1408]{1,0:T(8,128)(2,1)S(1)}, bf16[64,1408]{1,0:T(8,128)(2,1)S(1)}, u32[]{:S(2)}, u32[]{:S(2)}) collective-permute-start(bf16[64,1408]{1,0:T(8,128)(2,1)S(1)} %get-tuple-element.50), channel_id=1, source_target_pairs={{0,2},{1,3},{2,0},{3,1},{4,6},{5,7},{6,4},{7,5},{8,10},{9,11},{10,... | collective-permute-start | bytes 540680 | tf_op jit(solution)/shard_map/ppermute | solution.py:274
  46.4 1.5 %collective-permute-done.5.a_ref = bf16[64,1408]{1,0:T(8,128)(2,1)S(1)} collective-permute-done((bf16[64,1408]{1,0:T(8,128)(2,1)S(1)}, bf16[64,1408]{1,0:T(8,128)(2,1)S(1)}, u32[]{:S(2)}, u32[]{:S(2)}) %collective-permute-start.5) | collective-permute-done | bytes 180256 | tf_op jit(solution)/shard_map/ppermute | solution.py:274
  47.9 2.1 %collective-permute-done.6.b_ref = bf16[64,1408]{1,0:T(8,128)(2,1)S(1)} collective-permute-done((bf16[64,1408]{1,0:T(8,128)(2,1)S(1)}, bf16[64,1408]{1,0:T(8,128)(2,1)S(1)}, u32[]{:S(2)}, u32[]{:S(2)}) %collective-permute-start.6) | collective-permute-done | bytes 180256 | tf_op jit(solution)/shard_map/ppermute | solution.py:274
  50.8 7.2 %all-to-all-start.1 = ((bf16[16,8,1408]{2,1,0:T(8,128)(2,1)}), bf16[16,8,1408]{2,1,0:T(8,128)(2,1)S(1)}, u32[]{:S(2)}, u32[]{:S(2)}) async-start(bf16[16,8,1408]{2,1,0:T(8,128)(2,1)} %bitcast.10), calls=%async_computation.1 | async-start | bytes 720896 | tf_op jit(solution)/shard_map/all_to_all | solution.py:270
  58.0 7.4 %shard_map.153 = (f32[80,128]{1,0:T(8,128)}, f32[118,128]{1,0:T(8,128)S(1)}) custom-call(bf16[32,80,128]{2,1,0:T(8,128)(2,1)S(1)} %all-to-all-done.blocks_ref, bf16[118,128]{1,0:T(8,128)(2,1)S(1)} %bitcast.18, bf16[80,128]{1,0:T(8,128)(2,1)S(1)} %bitcast.19, s32[118,128]{1,0:T(8,128)S(1)} %copy-done), custom_call_target="tpu_custom_call" | custom-call | flops 2000000000 | bytes 2000000 | tf_op jit(solution)/shard_map/pallas_call | solution.py:241
  65.4 3.7 %all-to-all-done.1.parts_ref = bf16[16,8,1408]{2,1,0:T(8,128)(2,1)S(1)} async-done(((bf16[16,8,1408]{2,1,0:T(8,128)(2,1)}), bf16[16,8,1408]{2,1,0:T(8,128)(2,1)S(1)}, u32[]{:S(2)}, u32[]{:S(2)}) %all-to-all-start.1) | async-done | bytes 360480 | tf_op jit(solution)/shard_map/all_to_all | solution.py:270
  69.1 7.3 %collective-permute-start.7 = (bf16[8,1408]{1,0:T(8,128)(2,1)S(1)}, bf16[8,1408]{1,0:T(8,128)(2,1)S(1)}, u32[]{:S(2)}, u32[]{:S(2)}) collective-permute-start(bf16[8,1408]{1,0:T(8,128)(2,1)S(1)} %shard_map.154.one_ref), channel_id=1, source_target_pairs={{0,1},{1,0},{2,3},{3,2},{4,5},{5,4},{6,7},{7,6},{8,9},{9,8},{10,11... | collective-permute-start | bytes 67592 | tf_op jit(solution)/shard_map/ppermute | solution.py:274
  76.4 1.8 %collective-permute-done.7.two_ref = bf16[8,1408]{1,0:T(8,128)(2,1)S(1)} collective-permute-done((bf16[8,1408]{1,0:T(8,128)(2,1)S(1)}, bf16[8,1408]{1,0:T(8,128)(2,1)S(1)}, u32[]{:S(2)}, u32[]{:S(2)}) %collective-permute-start.7) | collective-permute-done | bytes 22560 | tf_op jit(solution)/shard_map/ppermute | solution.py:274
  79.2 3.1 %collective-permute-start.9 = (f32[8,1408]{1,0:T(8,128)S(1)}, f32[8,1408]{1,0:T(8,128)S(1)}, u32[]{:S(2)}, u32[]{:S(2)}) collective-permute-start(f32[8,1408]{1,0:T(8,128)S(1)} %shard_map.155.refs_0_), channel_id=1, source_target_pairs={{0,4},{1,5},{2,6},{3,7},{4,0},{5,1},{6,2},{7,3},{8,12},{9,13},{10,... | collective-permute-start | bytes 135176 | tf_op jit(solution)/shard_map/ppermute | solution.py:274
  83.1 1.7 %collective-permute-done.9.refs_2_ = f32[8,1408]{1,0:T(8,128)S(1)} collective-permute-done((f32[8,1408]{1,0:T(8,128)S(1)}, f32[8,1408]{1,0:T(8,128)S(1)}, u32[]{:S(2)}, u32[]{:S(2)}) %collective-permute-start.9) | collective-permute-done | bytes 45088 | tf_op jit(solution)/shard_map/ppermute | solution.py:274
  84.8 1.6 %collective-permute-done.8.refs_1_ = f32[8,1408]{1,0:T(8,128)S(1)} collective-permute-done((f32[8,1408]{1,0:T(8,128)S(1)}, f32[8,1408]{1,0:T(8,128)S(1)}, u32[]{:S(2)}, u32[]{:S(2)}) %collective-permute-start.8) | collective-permute-done | bytes 45088 | tf_op jit(solution)/shard_map/ppermute | solution.py:274
  86.3 1.3 %shard_map.156 = (f32[8,3024]{1,0:T(8,128)}, f32[8,2304]{1,0:T(8,128)}) custom-call(f32[8,1408]{1,0:T(8,128)S(1)} %shard_map.155.refs_0_, f32[8,1408]{1,0:T(8,128)S(1)} %collective-permute-done.8.refs_1_, f32[8,1408]{1,0:T(8,128)S(1)} %collective-permute-done.9.refs_2_, f32[8,1408]{1,0:T(8,128)S(1)} %collective-permute-done.10.refs_3_, ...), custom_call_target="tpu_custom_call" | custom-call | flops 400000 | bytes 400000 | tf_op jit(solution)/shard_map/pallas_call | solution.py:241
  (21 shorter events, 5.2 us)
Async XLA Ops:
  1.7 6.4 %collective-permute-start = (bf16[3,128,256]{2,1,0:T(8,128)(2,1)S(1)}, bf16[3,128,256]{2,1,0:T(8,128)(2,1)S(1)}, u32[]{:S(2)}, u32[]{:S(2)}) collective-permute-start(bf16[3,128,256]{2,1,0:T(8,128)(2,1)S(1)} %get-tuple-element.34), channel_id=1, source_target_pairs={{0,8},{8,16},{16,24},{24,32},{32,40},{40,48},{48,56},{56,64},{64,7... | collective-permute-start | bytes 589832 | tf_op jit(solution)/shard_map/ppermute | solution.py:266
  3.5 5.0 %collective-permute-start.1 = (bf16[3,128,256]{2,1,0:T(8,128)(2,1)S(1)}, bf16[3,128,256]{2,1,0:T(8,128)(2,1)S(1)}, u32[]{:S(2)}, u32[]{:S(2)}) collective-permute-start(bf16[3,128,256]{2,1,0:T(8,128)(2,1)S(1)} %get-tuple-element.35), channel_id=1, source_target_pairs={{8,0},{16,8},{24,16},{32,24},{40,32},{48,40},{56,48},{64,56},{72,6... | collective-permute-start | bytes 589832 | tf_op jit(solution)/shard_map/ppermute | solution.py:266
  15.0 13.9 %collective-permute-start.2 = (bf16[4,128,1408]{2,1,0:T(8,128)(2,1)}, bf16[4,128,1408]{2,1,0:T(8,128)(2,1)}, u32[]{:S(2)}, u32[]{:S(2)}) collective-permute-start(bf16[4,128,1408]{2,1,0:T(8,128)(2,1)} %get-tuple-element.43), channel_id=1, source_target_pairs={{0,8},{8,0},{16,24},{24,16},{32,40},{40,32},{48,56},{56,48},{64,72... | collective-permute-start | bytes 4325384 | tf_op jit(solution)/shard_map/ppermute | solution.py:274
  20.1 30.7 %all-to-all-start = ((bf16[32,80,128]{2,1,0:T(8,128)(2,1)}), bf16[32,80,128]{2,1,0:T(8,128)(2,1)S(1)}, u32[]{:S(2)}, u32[]{:S(2)}) async-start(bf16[32,80,128]{2,1,0:T(8,128)(2,1)} %get-tuple-element.41), calls=%async_computation | async-start | bytes 1310720 | tf_op jit(solution)/shard_map/all_to_all | solution.py:270
  30.4 10.7 %collective-permute-start.3 = (bf16[2,64,1408]{2,1,0:T(8,128)(2,1)S(1)}, bf16[2,64,1408]{2,1,0:T(8,128)(2,1)S(1)}, u32[]{:S(2)}, u32[]{:S(2)}) collective-permute-start(bf16[2,64,1408]{2,1,0:T(8,128)(2,1)S(1)} %get-tuple-element.46), channel_id=1, source_target_pairs={{0,2},{1,3},{2,0},{3,1},{4,6},{5,7},{6,4},{7,5},{8,10},{9,11},{10,... | collective-permute-start | bytes 1081352 | tf_op jit(solution)/shard_map/ppermute | solution.py:274
  31.1 10.7 %collective-permute-start.4 = (bf16[2,64,1408]{2,1,0:T(8,128)(2,1)S(1)}, bf16[2,64,1408]{2,1,0:T(8,128)(2,1)S(1)}, u32[]{:S(2)}, u32[]{:S(2)}) collective-permute-start(bf16[2,64,1408]{2,1,0:T(8,128)(2,1)S(1)} %get-tuple-element.47), channel_id=1, source_target_pairs={{0,6},{1,7},{2,4},{3,5},{4,2},{5,3},{6,0},{7,1},{8,14},{9,15},{10,... | collective-permute-start | bytes 1081352 | tf_op jit(solution)/shard_map/ppermute | solution.py:274
  41.9 16.0 %copy-start = (s32[118,128]{1,0:T(8,128)S(1)}, s32[118,128]{1,0:T(8,128)}, u32[]{:S(2)}) copy-start(s32[118,128]{1,0:T(8,128)} %slot_ref.1) | copy-start | bytes 181252
  41.9 16.0 %copy-start.1 = (bf16[1,118,128]{2,1,0:T(8,128)(2,1)S(1)}, bf16[1,118,128]{2,1,0:T(8,128)(2,1)}, u32[]{:S(2)}) copy-start(bf16[1,118,128]{2,1,0:T(8,128)(2,1)} %param.18) | copy-start | bytes 90628
  41.9 16.0 %copy-start.2 = (bf16[1,80,128]{2,1,0:T(8,128)(2,1)S(1)}, bf16[1,80,128]{2,1,0:T(8,128)(2,1)}, u32[]{:S(2)}) copy-start(bf16[1,80,128]{2,1,0:T(8,128)(2,1)} %param.19) | copy-start | bytes 61444
  41.9 6.0 %collective-permute-start.5 = (bf16[64,1408]{1,0:T(8,128)(2,1)S(1)}, bf16[64,1408]{1,0:T(8,128)(2,1)S(1)}, u32[]{:S(2)}, u32[]{:S(2)}) collective-permute-start(bf16[64,1408]{1,0:T(8,128)(2,1)S(1)} %get-tuple-element.49), channel_id=1, source_target_pairs={{0,6},{1,7},{2,4},{3,5},{4,2},{5,3},{6,0},{7,1},{8,14},{9,15},{10,... | collective-permute-start | bytes 540680 | tf_op jit(solution)/shard_map/ppermute | solution.py:274
  43.8 6.2 %collective-permute-start.6 = (bf16[64,1408]{1,0:T(8,128)(2,1)S(1)}, bf16[64,1408]{1,0:T(8,128)(2,1)S(1)}, u32[]{:S(2)}, u32[]{:S(2)}) collective-permute-start(bf16[64,1408]{1,0:T(8,128)(2,1)S(1)} %get-tuple-element.50), channel_id=1, source_target_pairs={{0,2},{1,3},{2,0},{3,1},{4,6},{5,7},{6,4},{7,5},{8,10},{9,11},{10,... | collective-permute-start | bytes 540680 | tf_op jit(solution)/shard_map/ppermute | solution.py:274
  50.8 18.3 %all-to-all-start.1 = ((bf16[16,8,1408]{2,1,0:T(8,128)(2,1)}), bf16[16,8,1408]{2,1,0:T(8,128)(2,1)S(1)}, u32[]{:S(2)}, u32[]{:S(2)}) async-start(bf16[16,8,1408]{2,1,0:T(8,128)(2,1)} %bitcast.10), calls=%async_computation.1 | async-start | bytes 720896 | tf_op jit(solution)/shard_map/all_to_all | solution.py:270
  69.1 9.1 %collective-permute-start.7 = (bf16[8,1408]{1,0:T(8,128)(2,1)S(1)}, bf16[8,1408]{1,0:T(8,128)(2,1)S(1)}, u32[]{:S(2)}, u32[]{:S(2)}) collective-permute-start(bf16[8,1408]{1,0:T(8,128)(2,1)S(1)} %shard_map.154.one_ref), channel_id=1, source_target_pairs={{0,1},{1,0},{2,3},{3,2},{4,5},{5,4},{6,7},{7,6},{8,9},{9,8},{10,11... | collective-permute-start | bytes 67592 | tf_op jit(solution)/shard_map/ppermute | solution.py:274
  78.2 4.9 %collective-permute-start.10 = (f32[8,1408]{1,0:T(8,128)S(1)}, f32[8,1408]{1,0:T(8,128)S(1)}, u32[]{:S(2)}, u32[]{:S(2)}) collective-permute-start(f32[8,1408]{1,0:T(8,128)S(1)} %shard_map.155.refs_0_), channel_id=1, source_target_pairs={{0,6},{1,7},{2,4},{3,5},{4,2},{5,3},{6,0},{7,1},{8,14},{9,15},{10,... | collective-permute-start | bytes 135176 | tf_op jit(solution)/shard_map/ppermute | solution.py:274
  79.2 5.6 %collective-permute-start.9 = (f32[8,1408]{1,0:T(8,128)S(1)}, f32[8,1408]{1,0:T(8,128)S(1)}, u32[]{:S(2)}, u32[]{:S(2)}) collective-permute-start(f32[8,1408]{1,0:T(8,128)S(1)} %shard_map.155.refs_0_), channel_id=1, source_target_pairs={{0,4},{1,5},{2,6},{3,7},{4,0},{5,1},{6,2},{7,3},{8,12},{9,13},{10,... | collective-permute-start | bytes 135176 | tf_op jit(solution)/shard_map/ppermute | solution.py:274
  82.3 4.0 %collective-permute-start.8 = (f32[8,1408]{1,0:T(8,128)S(1)}, f32[8,1408]{1,0:T(8,128)S(1)}, u32[]{:S(2)}, u32[]{:S(2)}) collective-permute-start(f32[8,1408]{1,0:T(8,128)S(1)} %shard_map.155.refs_0_), channel_id=1, source_target_pairs={{0,2},{1,3},{2,0},{3,1},{4,6},{5,7},{6,4},{7,5},{8,10},{9,11},{10,... | collective-permute-start | bytes 135176 | tf_op jit(solution)/shard_map/ppermute | solution.py:274

commit v2 on v1

--- a/solution.py
+++ b/solution.py
@@ -68,8 +68,8 @@
 
 
 def local_kernel(dims, own_ref, before_ref, after_ref, first_ref, lid_ref, cam_ref, wa_ref, wb_ref, spot_ref,
-                 lidar_ref, blocks_hbm, keep_ref, send_ref,
-                 g_ref, a_ref, gt_ref, at_ref, pick_ref, block_sems):
+                 lidar_hbm, blocks_hbm, keep_ref, send_hbm,
+                 g_ref, a_ref, gt_ref, at_ref, pick_ref, lidar_ref, send_ref, block_sems, out_sems):
     cols, ch, cam, parts = dims
     lid = lid_ref.shape[2]
     fan = cam + lid
@@ -102,6 +102,8 @@
             camera += mm(wa_ref[tap : tap + cam, :], rows, NT)
     for r in range(2):
         lidar_ref[r] = lidar[r * cols : (r + 1) * cols].astype(bf16)
+    leaving = [pltpu.make_async_copy(lidar_ref, lidar_hbm, out_sems.at[parts])]
+    leaving[0].start()
     for r in range(2):
         pick_ref[r] = camera[:, r * cols : (r + 1) * cols].astype(bf16)
     picks = [
@@ -118,7 +120,7 @@
         halves = value.reshape(ch // 16, 2, 8, value.shape[1])
         even = halves[:, 0].reshape(half, value.shape[1])
         odd = halves[:, 1].reshape(half, value.shape[1])
-        mine = jnp.where(second_core, odd, even)
+        mine = jnp.where(second_core, odd, even).astype(bf16)
         other = jnp.where(second_core, even, odd).astype(bf16)
         for t in range(value.shape[1] // TILE):
             part, at = divmod(tile + t, per_part)
@@ -131,18 +133,29 @@
     lidar_in = jnp.concatenate([lid_ref[0], lid_ref[1]], axis=0)
     camera_in = jnp.concatenate([cam_ref[0], cam_ref[1]], axis=1)
     b_tiles, a_tiles = ch // TILE, lid // TILE
-    packed = []
-    for a in range(3):
-        for b in range(3):
-            tap = 3 * a + b
-            window = slice((2 - a) * cols, (4 - a) * cols)
-            put(mm(gt_ref[2 - b, :, window], hidden, NN), tap * b_tiles)
-            put(mm(at_ref[2 - b, :, window], lidar_in, NN), 9 * b_tiles + tap * a_tiles)
-            packed.append(mm(at_ref[2 - b, :, window], camera_in, NT))
+    windows = [(2 - b, slice((2 - a) * cols, (4 - a) * cols)) for a in range(3) for b in range(3)]
+
+    def leave(first_part, end):
+        for part in range(first_part, end):
+            place = part ^ spot_ref[1]
+            leaving.append(pltpu.make_async_copy(send_ref.at[place], send_hbm.at[place], out_sems.at[part]))
+            leaving[-1].start()
+
+    for tap, (b, window) in enumerate(windows):
+        put(mm(gt_ref[b, :, window], hidden, NN), tap * b_tiles)
+    gone = 9 * b_tiles // per_part
+    leave(0, gone)
+    for tap, (b, window) in enumerate(windows):
+        put(mm(at_ref[b, :, window], lidar_in, NN), 9 * b_tiles + tap * a_tiles)
     at = 9 * (b_tiles + a_tiles)
+    leave(gone, at // per_part)
+    packed = [mm(at_ref[b, :, window], camera_in, NT) for b, window in windows]
     spare = (parts * per_part - at) * TILE - 9 * cam
     packed.append(jnp.zeros((ch, spare), f32))
     put(jnp.concatenate(packed, axis=1), at)
+    leave(at // per_part, parts)
+    for move in leaving:
+        move.wait()
     for pick in picks:
         pick.wait()
 
@@ -185,19 +198,22 @@
     gc_ref[...] = total
 
 
+def added(keep_ref, other_ref, part, rows):
+    return keep_ref[part, rows].astype(f32) + other_ref[part, rows].astype(f32)
+
+
 def first_sum(keep_ref, other_ref, a_ref, b_ref):
     rows = a_ref.shape[1]
     for k, (upper, lower) in enumerate([(1, 3), (2, 2)]):
-        a_ref[k] = (keep_ref[upper, :rows] + other_ref[upper, :rows].astype(f32)).astype(bf16)
-        b_ref[k] = (keep_ref[lower, rows:] + other_ref[lower, rows:].astype(f32)).astype(bf16)
+        a_ref[k] = added(keep_ref, other_ref, upper, slice(0, rows)).astype(bf16)
+        b_ref[k] = added(keep_ref, other_ref, lower, slice(rows, 2 * rows)).astype(bf16)
 
 
 def kept_sum(keep_ref, other_ref, own_ref, next_ref):
     rows = own_ref.shape[0] // 2
-    upper, lower = slice(0, rows), slice(rows, 2 * rows)
-    own_ref[...] = keep_ref[0] + other_ref[0].astype(f32)
-    next_ref[upper] = keep_ref[3, upper] + other_ref[3, upper].astype(f32)
-    next_ref[lower] = keep_ref[1, lower] + other_ref[1, lower].astype(f32)
+    for here, part in [(slice(0, rows), 3), (slice(rows, 2 * rows), 1)]:
+        own_ref[here] = added(keep_ref, other_ref, 0, here)
+        next_ref[here] = added(keep_ref, other_ref, part, here)
 
 
 def second_sum(own_ref, next_ref, a_ref, b_ref, out_ref, a_out_ref, b_out_ref):
@@ -220,15 +236,14 @@
 
 
 def pair_sum(one_ref, two_ref, out_ref):
-    out_ref[...] = one_ref[...].astype(f32) + two_ref[...].astype(f32)
-
-
-def last_sum(dims, scale, *refs):
+    total = one_ref[...].astype(f32) + two_ref[...].astype(f32)
+    for k in range(out_ref.shape[0]):
+        out_ref[k] = total
+
+
+def last_sum(dims, scale, parts_ref, wa_ref, wb_ref):
     ch, lid, cam = dims
-    *parts, spot_ref, wa_ref, wb_ref, all_ref = refs
-    for k, part in enumerate(parts):
-        all_ref[k ^ spot_ref[1]] = part[...]
-    whole = jnp.concatenate([all_ref[x] for x in range(len(parts))], axis=1) * scale
+    whole = jnp.concatenate([parts_ref[x] for x in range(parts_ref.shape[0])], axis=1) * scale
     wb_ref[...] = whole[:, : 9 * ch]
     pieces = []
     for tap in range(9):
@@ -291,18 +306,15 @@
     return part
 
 
-def over_scenes(part, spot, dims, scale):
+def over_scenes(part, dims, scale):
     ch, lid, cam = dims
-    (own,) = small(pair_sum, [(part.shape, f32)], (part, swapped(part, "scene", lambda i: i ^ 1)))
-    parts = [own] + [swapped(own, "scene", lambda i, k=k: i ^ 2 * k) for k in range(1, 4)]
-    return call(
+    reach = lax.axis_size("scene") // 2
+    (spread,) = small(pair_sum, [((reach, *part.shape), f32)], (part, swapped(part, "scene", lambda i: i ^ 1)))
+    parts = exchanged(spread, "scene", [[2 * i + h for i in range(reach)] for h in range(2)])
+    return small(
         functools.partial(last_sum, dims, scale),
-        [jax.ShapeDtypeStruct((8, 9 * width), f32) for width in (cam + lid, ch)],
-        [pltpu.VMEM((len(parts), *own.shape), f32)],
-        (*parts, spot),
-        [VM] * len(parts) + [SM],
-        400_000,
-        400_000,
+        [((part.shape[0], 9 * width), f32) for width in (cam + lid, ch)],
+        (parts,),
     )
 
 
@@ -349,10 +361,10 @@
     lidar, blocks, keep, send = call(
         functools.partial(local_kernel, (cols, ch, cam, reach)),
         [
-            shape((rows, cols, lid), bf16),
+            pltpu.HBM((rows, cols, lid), bf16),
             pltpu.HBM((space, cam, cols), bf16),
-            shape((reach, ch // 2, per_part), f32),
             shape((reach, ch // 2, per_part), bf16),
+            pltpu.HBM((reach, ch // 2, per_part), bf16),
         ],
         [
             pltpu.VMEM((3, 6 * cols, ch), bf16),
@@ -360,13 +372,16 @@
             pltpu.VMEM((3, ch, 4 * cols), bf16),
             pltpu.VMEM((3, ch, 4 * cols), bf16),
             pltpu.VMEM((2, cam, cols), bf16),
+            pltpu.VMEM((rows, cols, lid), bf16),
+            pltpu.VMEM((reach, ch // 2, per_part), bf16),
             pltpu.SemaphoreType.DMA((space,)),
+            pltpu.SemaphoreType.DMA((reach + 1,)),
         ],
         (grad_b, before, after, *loaded, spot),
         [VM] * 8 + [SM],
         1_800_000_000,
         12_000_000,
-        outs_at=[VM, HB, VM, VM],
+        outs_at=[HB, HB, VM, HB],
     )
     incoming = exchanged(blocks, "space", None)
     part = summed_along_x(keep, send)
@@ -391,7 +406,7 @@
     )
     along_yz, grad_context, grad_depth = lax.optimization_barrier((along_yz, grad_context, grad_depth))
     (part,) = small(place_sum, [((8, per_part), bf16)], (along_yz,))
-    grad_wa, grad_wb = over_scenes(part, spot, (ch, lid, cam), scale)
+    grad_wa, grad_wb = over_scenes(part, (ch, lid, cam), scale)
     return grad_wa, grad_wb, lidar[None], grad_context[None], grad_depth[None]
 
 

time: 88 us -> 87.8 us (level)
  Pallas kernels: 23 us -> 19.4 us
  waiting for transfers between devices: 19.7 us -> 21.9 us
  starting transfers between devices: 42.8 us -> 43.8 us
    all_to_all x2 -> x3, starting transfers between devices: 16 us -> 21.2 us  [exchanged(): return lax.all_to_all(x, axis, 0, 0, axis_index_groups=groups, tiled=True)]
    ppermute x9 -> x6, starting transfers between devices: 23.7 us -> 19.5 us  [swapped(): lax.ppermute(x, axis, [(i, partner(i)) for i in range(lax.axis_size(axis))])]
    all_to_all x2 -> x3, waiting for transfers between devices: 3.68 us -> 7.81 us  [exchanged(): return lax.all_to_all(x, axis, 0, 0, axis_index_groups=groups, tiled=True)]
    pallas_call x11, Pallas kernels: 23 us -> 19.4 us  [call(): pl.pallas_call(kernel, out_shape=outs, in_specs=specs, out_specs=outs_at...]
    ppermute x9 -> x6, waiting for transfers between devices: 15.6 us -> 13.8 us  [swapped(): lax.ppermute(x, axis, [(i, partner(i)) for i in range(lax.axis_size(axis))])]
  transfers between devices with their start and end apart: 13 -> 11, of which waited for: 9 -> 8; matrix products, arithmetic and copies ran while one was open for 2% -> 2% of each run, Pallas kernels for 16% -> 13%
where the time goes in v2:
time: 87.8 us; the launch traced here: 87.3 us
  starting transfers between devices  43.8 us (50%)
  waiting for transfers between devices  21.9 us (25%)
  Pallas kernels  19.4 us (22%)
    all_to_all x3, starting transfers between devices, exchanged(): return lax.all_to_all(x, axis, 0, 0, axis_index_groups=groups, tiled=True)  21.2 us
    ppermute x6, starting transfers between devices, swapped(): lax.ppermute(x, axis, [(i, partner(i)) for i in range(lax.axis_size(axis))])  19.5 us
    pallas_call x11, Pallas kernels, call(): pl.pallas_call(kernel, out_shape=outs, in_specs=specs, out_specs=outs_at...  19.4 us
    ppermute x6, waiting for transfers between devices, swapped(): lax.ppermute(x, axis, [(i, partner(i)) for i in range(lax.axis_size(axis))])  13.8 us
    all_to_all x3, waiting for transfers between devices, exchanged(): return lax.all_to_all(x, axis, 0, 0, axis_index_groups=groups, tiled=True)  7.81 us
    ppermute x2, starting transfers between devices, neighbours(): lax.ppermute(x, 'space', [(j, i) for i, j in pairs] if reverse else pairs)  3.04 us
  transfers between devices with their start and end apart: 11, of which 8 were waited for; matrix products, arithmetic and copies ran while one was open for 2% of the time, Pallas kernels for 13%

profile of v2, /device:TPU:2, one launch (start us, length us, event | category | flops | bytes accessed | tf_op | source)
XLA Modules:
  0.0 87.3 jit_solution(2195276485900911852)
XLA Ops:
  0.6 1.1 %shard_map.147 = (bf16[3,128,256]{2,1,0:T(8,128)(2,1)S(1)}, bf16[3,128,256]{2,1,0:T(8,128)(2,1)S(1)}) custom-call(bf16[2,128,256]{2,1,0:T(8,128)(2,1)} %bitcast.21, bf16[2,128,256]{2,1,0:T(8,128)(2,1)} %bitcast.23, bf16[2,128,256]{2,1,0:T(8,128)(2,1)} %bitcast.25), custom_call_target="tpu_custom_call" | custom-call | flops 1000000 | bytes 1000000 | tf_op jit(solution)/shard_map/pallas_call | solution.py:256
  1.7 1.8 %collective-permute-start = (bf16[3,128,256]{2,1,0:T(8,128)(2,1)S(1)}, bf16[3,128,256]{2,1,0:T(8,128)(2,1)S(1)}, u32[]{:S(2)}, u32[]{:S(2)}) collective-permute-start(bf16[3,128,256]{2,1,0:T(8,128)(2,1)S(1)} %get-tuple-element.34), channel_id=1, source_target_pairs={{0,8},{8,16},{16,24},{24,32},{32,40},{40,48},{48,56},{56,64},{64,7... | collective-permute-start | bytes 589832 | tf_op jit(solution)/shard_map/ppermute | solution.py:281
  3.5 1.3 %collective-permute-start.1 = (bf16[3,128,256]{2,1,0:T(8,128)(2,1)S(1)}, bf16[3,128,256]{2,1,0:T(8,128)(2,1)S(1)}, u32[]{:S(2)}, u32[]{:S(2)}) collective-permute-start(bf16[3,128,256]{2,1,0:T(8,128)(2,1)S(1)} %get-tuple-element.35), channel_id=1, source_target_pairs={{8,0},{16,8},{24,16},{32,24},{40,32},{48,40},{56,48},{64,56},{72,6... | collective-permute-start | bytes 589832 | tf_op jit(solution)/shard_map/ppermute | solution.py:281
  4.8 0.7 pad_add_fusion.refs_7_.spot_ref
  5.5 2.6 %shard_map.146 = (bf16[2,128,256]{2,1,0:T(8,128)(2,1)S(1)}, bf16[2,128,256]{2,1,0:T(8,128)(2,1)S(1)}, bf16[2,128,256]{2,1,0:T(8,128)(2,1)S(1)}, bf16[2,80,128]{2...) custom-call(bf16[2,128,256]{2,1,0:T(8,128)(2,1)} %bitcast.22, ...), custom_call_target="tpu_custom_call" | custom-call | flops 2000000 | bytes 3500000 | tf_op jit(solution)/shard_map/pallas_call | solution.py:256
  8.5 5.6 %shard_map.148 = (bf16[2,128,256]{2,1,0:T(8,128)(2,1)}, bf16[32,80,128]{2,1,0:T(8,128)(2,1)}, bf16[4,128,1408]{2,1,0:T(8,128)(2,1)S(1)}, bf16[4,128,1408]{2,1,0:T(8,128)(2,1)}) custom-call(bf16[2,128,256]{2,1,0:T(8,128)(2,1)S(1)} %get-tuple-element.33.own_ref, bf16[3,128,256]{2,1,0:T(8,128)(2,1)S(1)} %collective-permute-done.before_ref, ...), custom_call_target="tpu_custom_call" | custom-call | flops 1800000000 | bytes 12000000 | tf_op jit(solution)/shard_map/pallas_call | solution.py:256
  14.1 5.0 %collective-permute-start.2 = (bf16[4,128,1408]{2,1,0:T(8,128)(2,1)}, bf16[4,128,1408]{2,1,0:T(8,128)(2,1)S(1)}, u32[]{:S(2)}, u32[]{:S(2)}) collective-permute-start(bf16[4,128,1408]{2,1,0:T(8,128)(2,1)} %get-tuple-element.43), channel_id=1, source_target_pairs={{0,8},{8,0},{16,24},{24,16},{32,40},{40,32},{48,56},{56,48},{64,72... | collective-permute-start | bytes 4325384 | tf_op jit(solution)/shard_map/ppermute | solution.py:289
  19.2 8.8 %all-to-all-start = ((bf16[32,80,128]{2,1,0:T(8,128)(2,1)}), bf16[32,80,128]{2,1,0:T(8,128)(2,1)S(1)}, u32[]{:S(2)}, u32[]{:S(2)}) async-start(bf16[32,80,128]{2,1,0:T(8,128)(2,1)} %get-tuple-element.41), calls=%async_computation | async-start | bytes 1310720 | tf_op jit(solution)/shard_map/all_to_all | solution.py:285
  28.8 2.1 %collective-permute-start.4 = (bf16[2,64,1408]{2,1,0:T(8,128)(2,1)S(1)}, bf16[2,64,1408]{2,1,0:T(8,128)(2,1)S(1)}, u32[]{:S(2)}, u32[]{:S(2)}) collective-permute-start(bf16[2,64,1408]{2,1,0:T(8,128)(2,1)S(1)} %get-tuple-element.47), channel_id=1, source_target_pairs={{0,6},{1,7},{2,4},{3,5},{4,2},{5,3},{6,0},{7,1},{8,14},{9,15},{10,... | collective-permute-start | bytes 1081352 | tf_op jit(solution)/shard_map/ppermute | solution.py:289
  31.1 7.8 %collective-permute-done.3.a_ref = bf16[2,64,1408]{2,1,0:T(8,128)(2,1)S(1)} collective-permute-done((bf16[2,64,1408]{2,1,0:T(8,128)(2,1)S(1)}, bf16[2,64,1408]{2,1,0:T(8,128)(2,1)S(1)}, u32[]{:S(2)}, u32[]{:S(2)}) %collective-permute-start.3) | collective-permute-done | bytes 360480 | tf_op jit(solution)/shard_map/ppermute | solution.py:289
  39.7 1.8 %collective-permute-start.5 = (bf16[64,1408]{1,0:T(8,128)(2,1)S(1)}, bf16[64,1408]{1,0:T(8,128)(2,1)S(1)}, u32[]{:S(2)}, u32[]{:S(2)}) collective-permute-start(bf16[64,1408]{1,0:T(8,128)(2,1)S(1)} %get-tuple-element.49), channel_id=1, source_target_pairs={{0,6},{1,7},{2,4},{3,5},{4,2},{5,3},{6,0},{7,1},{8,14},{9,15},{10,... | collective-permute-start | bytes 540680 | tf_op jit(solution)/shard_map/ppermute | solution.py:289
  41.5 2.6 %collective-permute-start.6 = (bf16[64,1408]{1,0:T(8,128)(2,1)S(1)}, bf16[64,1408]{1,0:T(8,128)(2,1)S(1)}, u32[]{:S(2)}, u32[]{:S(2)}) collective-permute-start(bf16[64,1408]{1,0:T(8,128)(2,1)S(1)} %get-tuple-element.50), channel_id=1, source_target_pairs={{0,2},{1,3},{2,0},{3,1},{4,6},{5,7},{6,4},{7,5},{8,10},{9,11},{10,... | collective-permute-start | bytes 540680 | tf_op jit(solution)/shard_map/ppermute | solution.py:289
  44.2 1.5 %collective-permute-done.5.a_ref = bf16[64,1408]{1,0:T(8,128)(2,1)S(1)} collective-permute-done((bf16[64,1408]{1,0:T(8,128)(2,1)S(1)}, bf16[64,1408]{1,0:T(8,128)(2,1)S(1)}, u32[]{:S(2)}, u32[]{:S(2)}) %collective-permute-start.5) | collective-permute-done | bytes 180256 | tf_op jit(solution)/shard_map/ppermute | solution.py:289
  45.7 2.1 %collective-permute-done.6.b_ref = bf16[64,1408]{1,0:T(8,128)(2,1)S(1)} collective-permute-done((bf16[64,1408]{1,0:T(8,128)(2,1)S(1)}, bf16[64,1408]{1,0:T(8,128)(2,1)S(1)}, u32[]{:S(2)}, u32[]{:S(2)}) %collective-permute-start.6) | collective-permute-done | bytes 180256 | tf_op jit(solution)/shard_map/ppermute | solution.py:289
  47.7 0.8 shard_map.152
  48.5 7.2 %all-to-all-start.1 = ((bf16[16,8,1408]{2,1,0:T(8,128)(2,1)}), bf16[16,8,1408]{2,1,0:T(8,128)(2,1)S(1)}, u32[]{:S(2)}, u32[]{:S(2)}) async-start(bf16[16,8,1408]{2,1,0:T(8,128)(2,1)} %bitcast.10), calls=%async_computation.1 | async-start | bytes 720896 | tf_op jit(solution)/shard_map/all_to_all | solution.py:285
  55.7 7.4 %shard_map.153 = (f32[80,128]{1,0:T(8,128)}, f32[118,128]{1,0:T(8,128)S(1)}) custom-call(bf16[32,80,128]{2,1,0:T(8,128)(2,1)S(1)} %all-to-all-done.blocks_ref, bf16[118,128]{1,0:T(8,128)(2,1)S(1)} %bitcast.18, bf16[80,128]{1,0:T(8,128)(2,1)S(1)} %bitcast.19, s32[118,128]{1,0:T(8,128)S(1)} %copy-done), custom_call_target="tpu_custom_call" | custom-call | flops 2000000000 | bytes 2000000 | tf_op jit(solution)/shard_map/pallas_call | solution.py:256
  63.1 3.7 %all-to-all-done.1.parts_ref = bf16[16,8,1408]{2,1,0:T(8,128)(2,1)S(1)} async-done(((bf16[16,8,1408]{2,1,0:T(8,128)(2,1)}), bf16[16,8,1408]{2,1,0:T(8,128)(2,1)S(1)}, u32[]{:S(2)}, u32[]{:S(2)}) %all-to-all-start.1) | async-done | bytes 360480 | tf_op jit(solution)/shard_map/all_to_all | solution.py:285
  66.9 7.3 %collective-permute-start.7 = (bf16[8,1408]{1,0:T(8,128)(2,1)S(1)}, bf16[8,1408]{1,0:T(8,128)(2,1)S(1)}, u32[]{:S(2)}, u32[]{:S(2)}) collective-permute-start(bf16[8,1408]{1,0:T(8,128)(2,1)S(1)} %shard_map.154.one_ref), channel_id=1, source_target_pairs={{0,1},{1,0},{2,3},{3,2},{4,5},{5,4},{6,7},{7,6},{8,9},{9,8},{10,11... | collective-permute-start | bytes 67592 | tf_op jit(solution)/shard_map/ppermute | solution.py:289
  74.2 1.8 %collective-permute-done.7.two_ref = bf16[8,1408]{1,0:T(8,128)(2,1)S(1)} collective-permute-done((bf16[8,1408]{1,0:T(8,128)(2,1)S(1)}, bf16[8,1408]{1,0:T(8,128)(2,1)S(1)}, u32[]{:S(2)}, u32[]{:S(2)}) %collective-permute-start.7) | collective-permute-done | bytes 22560 | tf_op jit(solution)/shard_map/ppermute | solution.py:289
  76.6 5.2 %all-to-all-start.2 = ((f32[4,8,1408]{2,1,0:T(8,128)}), f32[4,8,1408]{2,1,0:T(8,128)S(1)}, u32[]{:S(2)}, u32[]{:S(2)}) async-start(f32[4,8,1408]{2,1,0:T(8,128)} %shard_map.155), calls=%async_computation.2 | async-start | bytes 360448 | tf_op jit(solution)/shard_map/all_to_all | solution.py:285
  81.8 0.7 copy.16
  82.5 4.1 %all-to-all-done.2.parts_ref = f32[4,8,1408]{2,1,0:T(8,128)S(1)} async-done(((f32[4,8,1408]{2,1,0:T(8,128)}), f32[4,8,1408]{2,1,0:T(8,128)S(1)}, u32[]{:S(2)}, u32[]{:S(2)}) %all-to-all-start.2) | async-done | bytes 180256 | tf_op jit(solution)/shard_map/all_to_all | solution.py:285
  86.6 0.7 shard_map.156
  (17 shorter events, 2.8 us)
Async XLA Ops:
  1.7 6.4 %collective-permute-start = (bf16[3,128,256]{2,1,0:T(8,128)(2,1)S(1)}, bf16[3,128,256]{2,1,0:T(8,128)(2,1)S(1)}, u32[]{:S(2)}, u32[]{:S(2)}) collective-permute-start(bf16[3,128,256]{2,1,0:T(8,128)(2,1)S(1)} %get-tuple-element.34), channel_id=1, source_target_pairs={{0,8},{8,16},{16,24},{24,32},{32,40},{40,48},{48,56},{56,64},{64,7... | collective-permute-start | bytes 589832 | tf_op jit(solution)/shard_map/ppermute | solution.py:281
  3.5 5.0 %collective-permute-start.1 = (bf16[3,128,256]{2,1,0:T(8,128)(2,1)S(1)}, bf16[3,128,256]{2,1,0:T(8,128)(2,1)S(1)}, u32[]{:S(2)}, u32[]{:S(2)}) collective-permute-start(bf16[3,128,256]{2,1,0:T(8,128)(2,1)S(1)} %get-tuple-element.35), channel_id=1, source_target_pairs={{8,0},{16,8},{24,16},{32,24},{40,32},{48,40},{56,48},{64,56},{72,6... | collective-permute-start | bytes 589832 | tf_op jit(solution)/shard_map/ppermute | solution.py:281
  14.1 13.9 %collective-permute-start.2 = (bf16[4,128,1408]{2,1,0:T(8,128)(2,1)}, bf16[4,128,1408]{2,1,0:T(8,128)(2,1)S(1)}, u32[]{:S(2)}, u32[]{:S(2)}) collective-permute-start(bf16[4,128,1408]{2,1,0:T(8,128)(2,1)} %get-tuple-element.43), channel_id=1, source_target_pairs={{0,8},{8,0},{16,24},{24,16},{32,40},{40,32},{48,56},{56,48},{64,72... | collective-permute-start | bytes 4325384 | tf_op jit(solution)/shard_map/ppermute | solution.py:289
  19.2 29.4 %all-to-all-start = ((bf16[32,80,128]{2,1,0:T(8,128)(2,1)}), bf16[32,80,128]{2,1,0:T(8,128)(2,1)S(1)}, u32[]{:S(2)}, u32[]{:S(2)}) async-start(bf16[32,80,128]{2,1,0:T(8,128)(2,1)} %get-tuple-element.41), calls=%async_computation | async-start | bytes 1310720 | tf_op jit(solution)/shard_map/all_to_all | solution.py:285
  28.2 10.7 %collective-permute-start.3 = (bf16[2,64,1408]{2,1,0:T(8,128)(2,1)S(1)}, bf16[2,64,1408]{2,1,0:T(8,128)(2,1)S(1)}, u32[]{:S(2)}, u32[]{:S(2)}) collective-permute-start(bf16[2,64,1408]{2,1,0:T(8,128)(2,1)S(1)} %get-tuple-element.46), channel_id=1, source_target_pairs={{0,2},{1,3},{2,0},{3,1},{4,6},{5,7},{6,4},{7,5},{8,10},{9,11},{10,... | collective-permute-start | bytes 1081352 | tf_op jit(solution)/shard_map/ppermute | solution.py:289
  28.8 10.7 %collective-permute-start.4 = (bf16[2,64,1408]{2,1,0:T(8,128)(2,1)S(1)}, bf16[2,64,1408]{2,1,0:T(8,128)(2,1)S(1)}, u32[]{:S(2)}, u32[]{:S(2)}) collective-permute-start(bf16[2,64,1408]{2,1,0:T(8,128)(2,1)S(1)} %get-tuple-element.47), channel_id=1, source_target_pairs={{0,6},{1,7},{2,4},{3,5},{4,2},{5,3},{6,0},{7,1},{8,14},{9,15},{10,... | collective-permute-start | bytes 1081352 | tf_op jit(solution)/shard_map/ppermute | solution.py:289
  39.7 16.0 %copy-start = (s32[118,128]{1,0:T(8,128)S(1)}, s32[118,128]{1,0:T(8,128)}, u32[]{:S(2)}) copy-start(s32[118,128]{1,0:T(8,128)} %slot_ref.1) | copy-start | bytes 181252
  39.7 16.0 %copy-start.1 = (bf16[1,118,128]{2,1,0:T(8,128)(2,1)S(1)}, bf16[1,118,128]{2,1,0:T(8,128)(2,1)}, u32[]{:S(2)}) copy-start(bf16[1,118,128]{2,1,0:T(8,128)(2,1)} %param.18) | copy-start | bytes 90628
  39.7 16.0 %copy-start.2 = (bf16[1,80,128]{2,1,0:T(8,128)(2,1)S(1)}, bf16[1,80,128]{2,1,0:T(8,128)(2,1)}, u32[]{:S(2)}) copy-start(bf16[1,80,128]{2,1,0:T(8,128)(2,1)} %param.19) | copy-start | bytes 61444
  39.7 6.0 %collective-permute-start.5 = (bf16[64,1408]{1,0:T(8,128)(2,1)S(1)}, bf16[64,1408]{1,0:T(8,128)(2,1)S(1)}, u32[]{:S(2)}, u32[]{:S(2)}) collective-permute-start(bf16[64,1408]{1,0:T(8,128)(2,1)S(1)} %get-tuple-element.49), channel_id=1, source_target_pairs={{0,6},{1,7},{2,4},{3,5},{4,2},{5,3},{6,0},{7,1},{8,14},{9,15},{10,... | collective-permute-start | bytes 540680 | tf_op jit(solution)/shard_map/ppermute | solution.py:289
  41.5 6.2 %collective-permute-start.6 = (bf16[64,1408]{1,0:T(8,128)(2,1)S(1)}, bf16[64,1408]{1,0:T(8,128)(2,1)S(1)}, u32[]{:S(2)}, u32[]{:S(2)}) collective-permute-start(bf16[64,1408]{1,0:T(8,128)(2,1)S(1)} %get-tuple-element.50), channel_id=1, source_target_pairs={{0,2},{1,3},{2,0},{3,1},{4,6},{5,7},{6,4},{7,5},{8,10},{9,11},{10,... | collective-permute-start | bytes 540680 | tf_op jit(solution)/shard_map/ppermute | solution.py:289
  48.5 18.3 %all-to-all-start.1 = ((bf16[16,8,1408]{2,1,0:T(8,128)(2,1)}), bf16[16,8,1408]{2,1,0:T(8,128)(2,1)S(1)}, u32[]{:S(2)}, u32[]{:S(2)}) async-start(bf16[16,8,1408]{2,1,0:T(8,128)(2,1)} %bitcast.10), calls=%async_computation.1 | async-start | bytes 720896 | tf_op jit(solution)/shard_map/all_to_all | solution.py:285
  66.9 9.1 %collective-permute-start.7 = (bf16[8,1408]{1,0:T(8,128)(2,1)S(1)}, bf16[8,1408]{1,0:T(8,128)(2,1)S(1)}, u32[]{:S(2)}, u32[]{:S(2)}) collective-permute-start(bf16[8,1408]{1,0:T(8,128)(2,1)S(1)} %shard_map.154.one_ref), channel_id=1, source_target_pairs={{0,1},{1,0},{2,3},{3,2},{4,5},{5,4},{6,7},{7,6},{8,9},{9,8},{10,11... | collective-permute-start | bytes 67592 | tf_op jit(solution)/shard_map/ppermute | solution.py:289
  76.6 10.0 %all-to-all-start.2 = ((f32[4,8,1408]{2,1,0:T(8,128)}), f32[4,8,1408]{2,1,0:T(8,128)S(1)}, u32[]{:S(2)}, u32[]{:S(2)}) async-start(f32[4,8,1408]{2,1,0:T(8,128)} %shard_map.155), calls=%async_computation.2 | async-start | bytes 360448 | tf_op jit(solution)/shard_map/all_to_all | solution.py:285

commit v3 on v2

--- a/solution.py
+++ b/solution.py
@@ -44,15 +44,16 @@
     return jnp.where(second_ref[...].astype(f32) > 0, grad_ref[...].astype(f32), 0.0).astype(bf16)
 
 
-def halo_kernel(grad_hbm, second_hbm, first_hbm, down_ref, up_ref, grad_ref, second_ref, first_ref, sems):
+def halo_kernel(grad_hbm, second_hbm, first_hbm, near_ref, far_ref, grad_ref, second_ref, first_ref, sems):
     for move in started((grad_hbm, second_hbm, first_hbm), (grad_ref, second_ref, first_ref), sems):
         move.wait()
     rows = first_ref.shape[0]
+    odd = lax.axis_index("space") & 1
     grad_b = passed(grad_ref, second_ref)
-    down_ref[:rows] = grad_b
-    up_ref[:rows] = grad_b
-    down_ref[rows] = first_ref[rows - 1]
-    up_ref[rows] = first_ref[0]
+    near_ref[:rows] = grad_b
+    far_ref[:rows] = grad_b
+    near_ref[rows] = first_ref[(rows - 1) * (1 - odd)]
+    far_ref[rows] = first_ref[(rows - 1) * odd]
 
 
 def load_kernel(*refs):
@@ -67,16 +68,20 @@
         move.wait()
 
 
-def local_kernel(dims, own_ref, before_ref, after_ref, first_ref, lid_ref, cam_ref, wa_ref, wb_ref, spot_ref,
+def local_kernel(dims, own_ref, near_ref, far_ref, first_ref, lid_ref, cam_ref, wa_ref, wb_ref, spot_ref,
                  lidar_hbm, blocks_hbm, keep_ref, send_hbm,
                  g_ref, a_ref, gt_ref, at_ref, pick_ref, lidar_ref, send_ref, block_sems, out_sems):
     cols, ch, cam, parts = dims
     lid = lid_ref.shape[2]
     fan = cam + lid
     half = ch // 2
-    ext = jnp.concatenate(
-        [before_ref[0], before_ref[1], own_ref[0], own_ref[1], after_ref[0], after_ref[1]], axis=0
-    ).astype(f32)
+    second_core = spot_ref[0] > 0
+    near = [near_ref[k].astype(f32) for k in range(3)]
+    far = [far_ref[k].astype(f32) for k in range(3)]
+    before = [jnp.where(second_core, n, f) for n, f in zip(near, far)]
+    after = [jnp.where(second_core, f, n) for n, f in zip(near, far)]
+    own = [own_ref[k].astype(f32) for k in range(2)]
+    ext = jnp.concatenate([*before[:2], *own, *after[:2]], axis=0)
     for b in range(3):
         moved = shifted_columns(ext, b - 1, cols)
         g_ref[b] = moved.astype(bf16)
@@ -86,7 +91,7 @@
         for b in range(3):
             tap = (3 * (2 - a) + (2 - b)) * ch
             back += mm(g_ref[b, a * cols : (a + 4) * cols, :], wb_ref[:, tap : tap + ch], NN)
-    first = jnp.concatenate([before_ref[2], first_ref[0], first_ref[1], after_ref[2]], axis=0).astype(f32)
+    first = jnp.concatenate([before[2], first_ref[0].astype(f32), first_ref[1].astype(f32), after[2]], axis=0)
     grad_a = jnp.where(first > 0, back, 0.0).astype(bf16).astype(f32)
     for b in range(3):
         moved = shifted_columns(grad_a, b - 1, cols)
@@ -113,7 +118,6 @@
     for pick in picks:
         pick.start()
 
-    second_core = spot_ref[0] > 0
     per_part = keep_ref.shape[2] // TILE
 
     def put(value, tile):
@@ -236,14 +240,15 @@
 
 
 def pair_sum(one_ref, two_ref, out_ref):
-    total = one_ref[...].astype(f32) + two_ref[...].astype(f32)
-    for k in range(out_ref.shape[0]):
-        out_ref[k] = total
-
-
-def last_sum(dims, scale, parts_ref, wa_ref, wb_ref):
+    out_ref[...] = one_ref[...].astype(f32) + two_ref[...].astype(f32)
+
+
+def last_sum(dims, scale, *refs):
     ch, lid, cam = dims
-    whole = jnp.concatenate([parts_ref[x] for x in range(parts_ref.shape[0])], axis=1) * scale
+    *parts, spot_ref, wa_ref, wb_ref, all_ref = refs
+    for k, part in enumerate(parts):
+        all_ref[k ^ spot_ref[1]] = part[...]
+    whole = jnp.concatenate([all_ref[x] for x in range(len(parts))], axis=1) * scale
     wb_ref[...] = whole[:, : 9 * ch]
     pieces = []
     for tap in range(9):
@@ -273,12 +278,6 @@
 VM = pl.BlockSpec(memory_space=pltpu.VMEM)
 SM = pl.BlockSpec(memory_space=pltpu.SMEM)
 HB = pl.BlockSpec(memory_space=pltpu.HBM)
-
-
-def neighbours(x, reverse):
-    n = lax.axis_size("space")
-    pairs = [(i, i + 1) for i in range(n - 1)]
-    return lax.ppermute(x, "space", [(j, i) for i, j in pairs] if reverse else pairs)
 
 
 def exchanged(x, axis, groups):
@@ -306,15 +305,18 @@
     return part
 
 
-def over_scenes(part, dims, scale):
+def over_scenes(part, spot, dims, scale):
     ch, lid, cam = dims
-    reach = lax.axis_size("scene") // 2
-    (spread,) = small(pair_sum, [((reach, *part.shape), f32)], (part, swapped(part, "scene", lambda i: i ^ 1)))
-    parts = exchanged(spread, "scene", [[2 * i + h for i in range(reach)] for h in range(2)])
-    return small(
+    (own,) = small(pair_sum, [(part.shape, f32)], (part, swapped(part, "scene", lambda i: i ^ 1)))
+    parts = [own] + [swapped(own, "scene", lambda i, k=k: i ^ 2 * k) for k in range(1, 4)]
+    return call(
         functools.partial(last_sum, dims, scale),
-        [((part.shape[0], 9 * width), f32) for width in (cam + lid, ch)],
-        (parts,),
+        [jax.ShapeDtypeStruct((8, 9 * width), f32) for width in (cam + lid, ch)],
+        [pltpu.VMEM((len(parts), *own.shape), f32)],
+        (*parts, spot),
+        [VM] * len(parts) + [SM],
+        400_000,
+        400_000,
     )
 
 
@@ -331,7 +333,7 @@
     scale = 1.0 / math.sqrt(rows * cols * space * scenes)
     first = pre_first[0]
     shape = jax.ShapeDtypeStruct
-    down, up = call(
+    near, far = call(
         halo_kernel,
         [shape((k, cols, ch), bf16) for k in (rows + 1, rows + 1)],
         [pltpu.VMEM(first.shape, bf16)] * 3 + [pltpu.SemaphoreType.DMA((3,))],
@@ -340,7 +342,9 @@
         1_000_000,
         1_000_000,
     )
-    before, after = neighbours(down, False), neighbours(up, True)
+    sides = [(i, i + 1) for i in range(1, space - 1, 2)]
+    far = lax.ppermute(far, "space", sides + [(j, i) for i, j in sides])
+    near = swapped(near, "space", lambda i: i ^ 1)
     camera = jnp.swapaxes(camera_bev[0], 1, 2)
     spot = jnp.concatenate(
         [(lax.axis_index("space") & 1).reshape(1), (lax.axis_index("scene") >> 1).reshape(1), block_list[:, 0, 0]]
@@ -377,7 +381,7 @@
             pltpu.SemaphoreType.DMA((space,)),
             pltpu.SemaphoreType.DMA((reach + 1,)),
         ],
-        (grad_b, before, after, *loaded, spot),
+        (grad_b, near, far, *loaded, spot),
         [VM] * 8 + [SM],
         1_800_000_000,
         12_000_000,
@@ -406,7 +410,7 @@
     )
     along_yz, grad_context, grad_depth = lax.optimization_barrier((along_yz, grad_context, grad_depth))
     (part,) = small(place_sum, [((8, per_part), bf16)], (along_yz,))
-    grad_wa, grad_wb = over_scenes(part, (ch, lid, cam), scale)
+    grad_wa, grad_wb = over_scenes(part, spot, (ch, lid, cam), scale)
     return grad_wa, grad_wb, lidar[None], grad_context[None], grad_depth[None]
 
 

time: 87.8 us -> 83 us (0.945)
  starting transfers between devices: 43.8 us -> 39.4 us
    ppermute x6 -> x10, waiting for transfers between devices: 13.8 us -> 18 us  [swapped(): lax.ppermute(x, axis, [(i, partner(i)) for i in range(lax.axis_size(axis))])]
    all_to_all x3 -> x2, waiting for transfers between devices: 7.81 us -> 3.69 us  [exchanged(): return lax.all_to_all(x, axis, 0, 0, axis_index_groups=groups, tiled=True)]
    all_to_all x3 -> x2, starting transfers between devices: 21.2 us -> 18.8 us  [exchanged(): return lax.all_to_all(x, axis, 0, 0, axis_index_groups=groups, tiled=True)]
    ppermute x2 -> x1, starting transfers between devices: 3.04 us -> 0.67 us  [shards(): far = lax.ppermute(far, 'space', sides + [(j, i) for i, j in sides])]
    ppermute x6 -> x10, starting transfers between devices: 19.5 us -> 20 us  [swapped(): lax.ppermute(x, axis, [(i, partner(i)) for i in range(lax.axis_size(axis))])]
  transfers between devices with their start and end apart: 11 -> 13, of which waited for: 8 -> 8; matrix products, arithmetic and copies ran while one was open for 2% -> 2% of each run, Pallas kernels for 13% -> 14%
where the time goes in v3:
time: 83 us; the launch traced here: 82.7 us
  starting transfers between devices  39.4 us (47%)
  waiting for transfers between devices  21.7 us (26%)
  Pallas kernels  19.3 us (23%)
    ppermute x10, starting transfers between devices, swapped(): lax.ppermute(x, axis, [(i, partner(i)) for i in range(lax.axis_size(axis))])  20 us
    pallas_call x11, Pallas kernels, call(): pl.pallas_call(kernel, out_shape=outs, in_specs=specs, out_specs=outs_at...  19.3 us
    all_to_all x2, starting transfers between devices, exchanged(): return lax.all_to_all(x, axis, 0, 0, axis_index_groups=groups, tiled=True)  18.8 us
    ppermute x10, waiting for transfers between devices, swapped(): lax.ppermute(x, axis, [(i, partner(i)) for i in range(lax.axis_size(axis))])  18 us
    all_to_all x2, waiting for transfers between devices, exchanged(): return lax.all_to_all(x, axis, 0, 0, axis_index_groups=groups, tiled=True)  3.69 us
  transfers between devices with their start and end apart: 13, of which 8 were waited for; matrix products, arithmetic and copies ran while one was open for 2% of the time, Pallas kernels for 14%

profile of v3, /device:TPU:2, one launch (start us, length us, event | category | flops | bytes accessed | tf_op | source)
XLA Modules:
  0.0 82.7 jit_solution(6495728835629194544)
XLA Ops:
  0.6 1.1 %shard_map.147 = (bf16[3,128,256]{2,1,0:T(8,128)(2,1)S(1)}, bf16[3,128,256]{2,1,0:T(8,128)(2,1)S(1)}) custom-call(bf16[2,128,256]{2,1,0:T(8,128)(2,1)} %bitcast.21, bf16[2,128,256]{2,1,0:T(8,128)(2,1)} %bitcast.23, bf16[2,128,256]{2,1,0:T(8,128)(2,1)} %bitcast.25), custom_call_target="tpu_custom_call" | custom-call | flops 1000000 | bytes 1000000 | tf_op jit(solution)/shard_map/pallas_call | solution.py:261
  2.5 0.7 pad_add_fusion.refs_7_.spot_ref.refs_4_
  3.3 2.6 %shard_map.146 = (bf16[2,128,256]{2,1,0:T(8,128)(2,1)S(1)}, bf16[2,128,256]{2,1,0:T(8,128)(2,1)S(1)}, bf16[2,128,256]{2,1,0:T(8,128)(2,1)S(1)}, bf16[2,80,128]{2...) custom-call(bf16[2,128,256]{2,1,0:T(8,128)(2,1)} %bitcast.22, ...), custom_call_target="tpu_custom_call" | custom-call | flops 2000000 | bytes 3500000 | tf_op jit(solution)/shard_map/pallas_call | solution.py:261
  5.9 5.6 %shard_map.148 = (bf16[2,128,256]{2,1,0:T(8,128)(2,1)}, bf16[32,80,128]{2,1,0:T(8,128)(2,1)}, bf16[4,128,1408]{2,1,0:T(8,128)(2,1)S(1)}, bf16[4,128,1408]{2,1,0:T(8,128)(2,1)}) custom-call(bf16[2,128,256]{2,1,0:T(8,128)(2,1)S(1)} %get-tuple-element.33.own_ref, bf16[3,128,256]{2,1,0:T(8,128)(2,1)S(1)} %collective-permute-done.near_ref, ...), custom_call_target="tpu_custom_call" | custom-call | flops 1800000000 | bytes 12000000 | tf_op jit(solution)/shard_map/pallas_call | solution.py:261
  11.5 3.5 %collective-permute-start.2 = (bf16[4,128,1408]{2,1,0:T(8,128)(2,1)}, bf16[4,128,1408]{2,1,0:T(8,128)(2,1)S(1)}, u32[]{:S(2)}, u32[]{:S(2)}) collective-permute-start(bf16[4,128,1408]{2,1,0:T(8,128)(2,1)} %get-tuple-element.43), channel_id=1, source_target_pairs={{0,8},{8,0},{16,24},{24,16},{32,40},{40,32},{48,56},{56,48},{64,72... | collective-permute-start | bytes 4325384 | tf_op jit(solution)/shard_map/ppermute | solution.py:288
  15.0 11.6 %all-to-all-start = ((bf16[32,80,128]{2,1,0:T(8,128)(2,1)}), bf16[32,80,128]{2,1,0:T(8,128)(2,1)S(1)}, u32[]{:S(2)}, u32[]{:S(2)}) async-start(bf16[32,80,128]{2,1,0:T(8,128)(2,1)} %get-tuple-element.41), calls=%async_computation | async-start | bytes 1310720 | tf_op jit(solution)/shard_map/all_to_all | solution.py:284
  27.4 2.2 %collective-permute-start.4 = (bf16[2,64,1408]{2,1,0:T(8,128)(2,1)S(1)}, bf16[2,64,1408]{2,1,0:T(8,128)(2,1)S(1)}, u32[]{:S(2)}, u32[]{:S(2)}) collective-permute-start(bf16[2,64,1408]{2,1,0:T(8,128)(2,1)S(1)} %get-tuple-element.47), channel_id=1, source_target_pairs={{0,6},{1,7},{2,4},{3,5},{4,2},{5,3},{6,0},{7,1},{8,14},{9,15},{10,... | collective-permute-start | bytes 1081352 | tf_op jit(solution)/shard_map/ppermute | solution.py:288
  29.7 7.8 %collective-permute-done.3.a_ref = bf16[2,64,1408]{2,1,0:T(8,128)(2,1)S(1)} collective-permute-done((bf16[2,64,1408]{2,1,0:T(8,128)(2,1)S(1)}, bf16[2,64,1408]{2,1,0:T(8,128)(2,1)S(1)}, u32[]{:S(2)}, u32[]{:S(2)}) %collective-permute-start.3) | collective-permute-done | bytes 360480 | tf_op jit(solution)/shard_map/ppermute | solution.py:288
  38.3 1.8 %collective-permute-start.5 = (bf16[64,1408]{1,0:T(8,128)(2,1)S(1)}, bf16[64,1408]{1,0:T(8,128)(2,1)S(1)}, u32[]{:S(2)}, u32[]{:S(2)}) collective-permute-start(bf16[64,1408]{1,0:T(8,128)(2,1)S(1)} %get-tuple-element.49), channel_id=1, source_target_pairs={{0,6},{1,7},{2,4},{3,5},{4,2},{5,3},{6,0},{7,1},{8,14},{9,15},{10,... | collective-permute-start | bytes 540680 | tf_op jit(solution)/shard_map/ppermute | solution.py:288
  40.1 2.6 %collective-permute-start.6 = (bf16[64,1408]{1,0:T(8,128)(2,1)S(1)}, bf16[64,1408]{1,0:T(8,128)(2,1)S(1)}, u32[]{:S(2)}, u32[]{:S(2)}) collective-permute-start(bf16[64,1408]{1,0:T(8,128)(2,1)S(1)} %get-tuple-element.50), channel_id=1, source_target_pairs={{0,2},{1,3},{2,0},{3,1},{4,6},{5,7},{6,4},{7,5},{8,10},{9,11},{10,... | collective-permute-start | bytes 540680 | tf_op jit(solution)/shard_map/ppermute | solution.py:288
  42.8 1.5 %collective-permute-done.5.a_ref = bf16[64,1408]{1,0:T(8,128)(2,1)S(1)} collective-permute-done((bf16[64,1408]{1,0:T(8,128)(2,1)S(1)}, bf16[64,1408]{1,0:T(8,128)(2,1)S(1)}, u32[]{:S(2)}, u32[]{:S(2)}) %collective-permute-start.5) | collective-permute-done | bytes 180256 | tf_op jit(solution)/shard_map/ppermute | solution.py:288
  44.3 2.1 %collective-permute-done.6.b_ref = bf16[64,1408]{1,0:T(8,128)(2,1)S(1)} collective-permute-done((bf16[64,1408]{1,0:T(8,128)(2,1)S(1)}, bf16[64,1408]{1,0:T(8,128)(2,1)S(1)}, u32[]{:S(2)}, u32[]{:S(2)}) %collective-permute-start.6) | collective-permute-done | bytes 180256 | tf_op jit(solution)/shard_map/ppermute | solution.py:288
  46.3 0.8 shard_map.152
  47.1 7.2 %all-to-all-start.1 = ((bf16[16,8,1408]{2,1,0:T(8,128)(2,1)}), bf16[16,8,1408]{2,1,0:T(8,128)(2,1)S(1)}, u32[]{:S(2)}, u32[]{:S(2)}) async-start(bf16[16,8,1408]{2,1,0:T(8,128)(2,1)} %bitcast.10), calls=%async_computation.1 | async-start | bytes 720896 | tf_op jit(solution)/shard_map/all_to_all | solution.py:284
  54.3 7.4 %shard_map.153 = (f32[80,128]{1,0:T(8,128)}, f32[118,128]{1,0:T(8,128)S(1)}) custom-call(bf16[32,80,128]{2,1,0:T(8,128)(2,1)S(1)} %all-to-all-done.blocks_ref, bf16[118,128]{1,0:T(8,128)(2,1)S(1)} %bitcast.18, bf16[80,128]{1,0:T(8,128)(2,1)S(1)} %bitcast.19, s32[118,128]{1,0:T(8,128)S(1)} %copy-done), custom_call_target="tpu_custom_call" | custom-call | flops 2000000000 | bytes 2000000 | tf_op jit(solution)/shard_map/pallas_call | solution.py:261
  61.8 3.7 %all-to-all-done.1.parts_ref = bf16[16,8,1408]{2,1,0:T(8,128)(2,1)S(1)} async-done(((bf16[16,8,1408]{2,1,0:T(8,128)(2,1)}), bf16[16,8,1408]{2,1,0:T(8,128)(2,1)S(1)}, u32[]{:S(2)}, u32[]{:S(2)}) %all-to-all-start.1) | async-done | bytes 360480 | tf_op jit(solution)/shard_map/all_to_all | solution.py:284
  65.5 5.0 %collective-permute-start.7 = (bf16[8,1408]{1,0:T(8,128)(2,1)S(1)}, bf16[8,1408]{1,0:T(8,128)(2,1)S(1)}, u32[]{:S(2)}, u32[]{:S(2)}) collective-permute-start(bf16[8,1408]{1,0:T(8,128)(2,1)S(1)} %shard_map.154.one_ref), channel_id=1, source_target_pairs={{0,1},{1,0},{2,3},{3,2},{4,5},{5,4},{6,7},{7,6},{8,9},{9,8},{10,11... | collective-permute-start | bytes 67592 | tf_op jit(solution)/shard_map/ppermute | solution.py:288
  70.5 2.8 %collective-permute-done.7.two_ref = bf16[8,1408]{1,0:T(8,128)(2,1)S(1)} collective-permute-done((bf16[8,1408]{1,0:T(8,128)(2,1)S(1)}, bf16[8,1408]{1,0:T(8,128)(2,1)S(1)}, u32[]{:S(2)}, u32[]{:S(2)}) %collective-permute-start.7) | collective-permute-done | bytes 22560 | tf_op jit(solution)/shard_map/ppermute | solution.py:288
  73.3 0.8 collective-permute-start.10
  74.1 3.3 %collective-permute-start.9 = (f32[8,1408]{1,0:T(8,128)S(1)}, f32[8,1408]{1,0:T(8,128)S(1)}, u32[]{:S(2)}, u32[]{:S(2)}) collective-permute-start(f32[8,1408]{1,0:T(8,128)S(1)} %shard_map.155.refs_0_), channel_id=1, source_target_pairs={{0,4},{1,5},{2,6},{3,7},{4,0},{5,1},{6,2},{7,3},{8,12},{9,13},{10,... | collective-permute-start | bytes 135176 | tf_op jit(solution)/shard_map/ppermute | solution.py:288
  77.5 0.7 copy.16
  78.2 1.5 %collective-permute-done.9.refs_2_ = f32[8,1408]{1,0:T(8,128)S(1)} collective-permute-done((f32[8,1408]{1,0:T(8,128)S(1)}, f32[8,1408]{1,0:T(8,128)S(1)}, u32[]{:S(2)}, u32[]{:S(2)}) %collective-permute-start.9) | collective-permute-done | bytes 45088 | tf_op jit(solution)/shard_map/ppermute | solution.py:288
  79.6 1.8 %collective-permute-done.8.refs_1_ = f32[8,1408]{1,0:T(8,128)S(1)} collective-permute-done((f32[8,1408]{1,0:T(8,128)S(1)}, f32[8,1408]{1,0:T(8,128)S(1)}, u32[]{:S(2)}, u32[]{:S(2)}) %collective-permute-start.8) | collective-permute-done | bytes 45088 | tf_op jit(solution)/shard_map/ppermute | solution.py:288
  81.4 1.3 %shard_map.156 = (f32[8,3024]{1,0:T(8,128)}, f32[8,2304]{1,0:T(8,128)}) custom-call(f32[8,1408]{1,0:T(8,128)S(1)} %shard_map.155.refs_0_, f32[8,1408]{1,0:T(8,128)S(1)} %collective-permute-done.8.refs_1_, f32[8,1408]{1,0:T(8,128)S(1)} %collective-permute-done.9.refs_2_, f32[8,1408]{1,0:T(8,128)S(1)} %collective-permute-done.10.refs_3_, ...), custom_call_target="tpu_custom_call" | custom-call | flops 400000 | bytes 400000 | tf_op jit(solution)/shard_map/pallas_call | solution.py:261
  (21 shorter events, 2.7 us)
Async XLA Ops:
  1.7 4.2 %collective-permute-start = (bf16[3,128,256]{2,1,0:T(8,128)(2,1)S(1)}, bf16[3,128,256]{2,1,0:T(8,128)(2,1)S(1)}, u32[]{:S(2)}, u32[]{:S(2)}) collective-permute-start(bf16[3,128,256]{2,1,0:T(8,128)(2,1)S(1)} %get-tuple-element.34), channel_id=1, source_target_pairs={{0,8},{8,0},{16,24},{24,16},{32,40},{40,32},{48,56},{56,48},{64,72... | collective-permute-start | bytes 589832 | tf_op jit(solution)/shard_map/ppermute | solution.py:288
  1.8 4.1 %collective-permute-start.1 = (bf16[3,128,256]{2,1,0:T(8,128)(2,1)S(1)}, bf16[3,128,256]{2,1,0:T(8,128)(2,1)S(1)}, u32[]{:S(2)}, u32[]{:S(2)}) collective-permute-start(bf16[3,128,256]{2,1,0:T(8,128)(2,1)S(1)} %get-tuple-element.35), channel_id=1, source_target_pairs={{8,16},{24,32},{40,48},{56,64},{72,80},{88,96},{104,112},{120,128}... | collective-permute-start | bytes 589832 | tf_op jit(solution)/shard_map/ppermute | solution.py:346
  11.5 15.1 %collective-permute-start.2 = (bf16[4,128,1408]{2,1,0:T(8,128)(2,1)}, bf16[4,128,1408]{2,1,0:T(8,128)(2,1)S(1)}, u32[]{:S(2)}, u32[]{:S(2)}) collective-permute-start(bf16[4,128,1408]{2,1,0:T(8,128)(2,1)} %get-tuple-element.43), channel_id=1, source_target_pairs={{0,8},{8,0},{16,24},{24,16},{32,40},{40,32},{48,56},{56,48},{64,72... | collective-permute-start | bytes 4325384 | tf_op jit(solution)/shard_map/ppermute | solution.py:288
  15.0 32.1 %all-to-all-start = ((bf16[32,80,128]{2,1,0:T(8,128)(2,1)}), bf16[32,80,128]{2,1,0:T(8,128)(2,1)S(1)}, u32[]{:S(2)}, u32[]{:S(2)}) async-start(bf16[32,80,128]{2,1,0:T(8,128)(2,1)} %get-tuple-element.41), calls=%async_computation | async-start | bytes 1310720 | tf_op jit(solution)/shard_map/all_to_all | solution.py:284
  26.8 10.7 %collective-permute-start.3 = (bf16[2,64,1408]{2,1,0:T(8,128)(2,1)S(1)}, bf16[2,64,1408]{2,1,0:T(8,128)(2,1)S(1)}, u32[]{:S(2)}, u32[]{:S(2)}) collective-permute-start(bf16[2,64,1408]{2,1,0:T(8,128)(2,1)S(1)} %get-tuple-element.46), channel_id=1, source_target_pairs={{0,2},{1,3},{2,0},{3,1},{4,6},{5,7},{6,4},{7,5},{8,10},{9,11},{10,... | collective-permute-start | bytes 1081352 | tf_op jit(solution)/shard_map/ppermute | solution.py:288
  27.4 10.7 %collective-permute-start.4 = (bf16[2,64,1408]{2,1,0:T(8,128)(2,1)S(1)}, bf16[2,64,1408]{2,1,0:T(8,128)(2,1)S(1)}, u32[]{:S(2)}, u32[]{:S(2)}) collective-permute-start(bf16[2,64,1408]{2,1,0:T(8,128)(2,1)S(1)} %get-tuple-element.47), channel_id=1, source_target_pairs={{0,6},{1,7},{2,4},{3,5},{4,2},{5,3},{6,0},{7,1},{8,14},{9,15},{10,... | collective-permute-start | bytes 1081352 | tf_op jit(solution)/shard_map/ppermute | solution.py:288
  38.3 16.0 %copy-start = (s32[118,128]{1,0:T(8,128)S(1)}, s32[118,128]{1,0:T(8,128)}, u32[]{:S(2)}) copy-start(s32[118,128]{1,0:T(8,128)} %slot_ref.1) | copy-start | bytes 181252
  38.3 16.0 %copy-start.1 = (bf16[1,118,128]{2,1,0:T(8,128)(2,1)S(1)}, bf16[1,118,128]{2,1,0:T(8,128)(2,1)}, u32[]{:S(2)}) copy-start(bf16[1,118,128]{2,1,0:T(8,128)(2,1)} %param.18) | copy-start | bytes 90628
  38.3 16.0 %copy-start.2 = (bf16[1,80,128]{2,1,0:T(8,128)(2,1)S(1)}, bf16[1,80,128]{2,1,0:T(8,128)(2,1)}, u32[]{:S(2)}) copy-start(bf16[1,80,128]{2,1,0:T(8,128)(2,1)} %param.19) | copy-start | bytes 61444
  38.3 6.0 %collective-permute-start.5 = (bf16[64,1408]{1,0:T(8,128)(2,1)S(1)}, bf16[64,1408]{1,0:T(8,128)(2,1)S(1)}, u32[]{:S(2)}, u32[]{:S(2)}) collective-permute-start(bf16[64,1408]{1,0:T(8,128)(2,1)S(1)} %get-tuple-element.49), channel_id=1, source_target_pairs={{0,6},{1,7},{2,4},{3,5},{4,2},{5,3},{6,0},{7,1},{8,14},{9,15},{10,... | collective-permute-start | bytes 540680 | tf_op jit(solution)/shard_map/ppermute | solution.py:288
  40.1 6.2 %collective-permute-start.6 = (bf16[64,1408]{1,0:T(8,128)(2,1)S(1)}, bf16[64,1408]{1,0:T(8,128)(2,1)S(1)}, u32[]{:S(2)}, u32[]{:S(2)}) collective-permute-start(bf16[64,1408]{1,0:T(8,128)(2,1)S(1)} %get-tuple-element.50), channel_id=1, source_target_pairs={{0,2},{1,3},{2,0},{3,1},{4,6},{5,7},{6,4},{7,5},{8,10},{9,11},{10,... | collective-permute-start | bytes 540680 | tf_op jit(solution)/shard_map/ppermute | solution.py:288
  47.1 18.3 %all-to-all-start.1 = ((bf16[16,8,1408]{2,1,0:T(8,128)(2,1)}), bf16[16,8,1408]{2,1,0:T(8,128)(2,1)S(1)}, u32[]{:S(2)}, u32[]{:S(2)}) async-start(bf16[16,8,1408]{2,1,0:T(8,128)(2,1)} %bitcast.10), calls=%async_computation.1 | async-start | bytes 720896 | tf_op jit(solution)/shard_map/all_to_all | solution.py:284
  65.5 7.8 %collective-permute-start.7 = (bf16[8,1408]{1,0:T(8,128)(2,1)S(1)}, bf16[8,1408]{1,0:T(8,128)(2,1)S(1)}, u32[]{:S(2)}, u32[]{:S(2)}) collective-permute-start(bf16[8,1408]{1,0:T(8,128)(2,1)S(1)} %shard_map.154.one_ref), channel_id=1, source_target_pairs={{0,1},{1,0},{2,3},{3,2},{4,5},{5,4},{6,7},{7,6},{8,9},{9,8},{10,11... | collective-permute-start | bytes 67592 | tf_op jit(solution)/shard_map/ppermute | solution.py:288
  73.3 4.9 %collective-permute-start.10 = (f32[8,1408]{1,0:T(8,128)S(1)}, f32[8,1408]{1,0:T(8,128)S(1)}, u32[]{:S(2)}, u32[]{:S(2)}) collective-permute-start(f32[8,1408]{1,0:T(8,128)S(1)} %shard_map.155.refs_0_), channel_id=1, source_target_pairs={{0,6},{1,7},{2,4},{3,5},{4,2},{5,3},{6,0},{7,1},{8,14},{9,15},{10,... | collective-permute-start | bytes 135176 | tf_op jit(solution)/shard_map/ppermute | solution.py:288
  74.1 5.6 %collective-permute-start.9 = (f32[8,1408]{1,0:T(8,128)S(1)}, f32[8,1408]{1,0:T(8,128)S(1)}, u32[]{:S(2)}, u32[]{:S(2)}) collective-permute-start(f32[8,1408]{1,0:T(8,128)S(1)} %shard_map.155.refs_0_), channel_id=1, source_target_pairs={{0,4},{1,5},{2,6},{3,7},{4,0},{5,1},{6,2},{7,3},{8,12},{9,13},{10,... | collective-permute-start | bytes 135176 | tf_op jit(solution)/shard_map/ppermute | solution.py:288
  77.4 4.0 %collective-permute-start.8 = (f32[8,1408]{1,0:T(8,128)S(1)}, f32[8,1408]{1,0:T(8,128)S(1)}, u32[]{:S(2)}, u32[]{:S(2)}) collective-permute-start(f32[8,1408]{1,0:T(8,128)S(1)} %shard_map.155.refs_0_), channel_id=1, source_target_pairs={{0,2},{1,3},{2,0},{3,1},{4,6},{5,7},{6,4},{7,5},{8,10},{9,11},{10,... | collective-permute-start | bytes 135176 | tf_op jit(solution)/shard_map/ppermute | solution.py:288

commit v4 on v3

--- a/solution.py
+++ b/solution.py
@@ -56,47 +56,71 @@
     far_ref[rows] = first_ref[(rows - 1) * odd]
 
 
-def load_kernel(*refs):
-    count = (len(refs) - 3) // 2
-    sources, own_ref, targets = refs[:count], refs[count + 1], refs[count + 2 : -3]
-    grad_ref, second_ref, sems = refs[-3:]
-    moves = started(sources, (grad_ref, second_ref, *targets), sems)
+def back_weight(wb_ref, a, b):
+    ch = wb_ref.shape[0]
+    tap = (3 * (2 - a) + (2 - b)) * ch
+    return wb_ref[:, tap : tap + ch]
+
+
+def own_kernel(cols, grad_hbm, second_hbm, wb_hbm, start_ref, gt_ref, wb_ref, grad_ref, second_ref, g_ref, sems):
+    moves = started((grad_hbm, second_hbm, wb_hbm), (grad_ref, second_ref, wb_ref), sems)
     moves[0].wait()
     moves[1].wait()
-    own_ref[...] = passed(grad_ref, second_ref)
-    for move in moves[2:]:
-        move.wait()
-
-
-def local_kernel(dims, own_ref, near_ref, far_ref, first_ref, lid_ref, cam_ref, wa_ref, wb_ref, spot_ref,
+    own = passed(grad_ref, second_ref)
+    own = jnp.concatenate([own[0], own[1]], axis=0).astype(f32)
+    for b in range(3):
+        g_ref[b] = shifted_columns(own, b - 1, cols).astype(bf16)
+        gt_ref[b] = g_ref[b].T
+    moves[2].wait()
+    low, middle, high = [
+        sum(mm(g_ref[b], back_weight(wb_ref, a, b), NN) for b in range(3)) for a in (2, 1, 0)
+    ]
+    start_ref[0:cols] = low[:cols]
+    start_ref[cols : 2 * cols] = low[cols:] + middle[:cols]
+    start_ref[2 * cols : 3 * cols] = middle[cols:] + high[:cols]
+    start_ref[3 * cols :] = high[cols:]
+
+
+def local_kernel(dims, near_ref, far_ref, start_ref, gt_own_ref, wb_ref, first_hbm, lid_hbm, cam_hbm, wa_hbm, list_hbm,
                  lidar_hbm, blocks_hbm, keep_ref, send_hbm,
-                 g_ref, a_ref, gt_ref, at_ref, pick_ref, lidar_ref, send_ref, block_sems, out_sems):
+                 gb_ref, ga_ref, a_ref, gt_ref, at_ref, first_ref, lid_ref, cam_ref, wa_ref, list_ref,
+                 pick_ref, lidar_ref, send_ref, block_sems, out_sems, in_sems):
     cols, ch, cam, parts = dims
     lid = lid_ref.shape[2]
     fan = cam + lid
     half = ch // 2
-    second_core = spot_ref[0] > 0
+    moves = started(
+        (first_hbm, wa_hbm, list_hbm, lid_hbm, cam_hbm), (first_ref, wa_ref, list_ref, lid_ref, cam_ref), in_sems
+    )
+    second_core = (lax.axis_index("space") & 1) > 0
+    column_place = lax.axis_index("scene") >> 1
     near = [near_ref[k].astype(f32) for k in range(3)]
     far = [far_ref[k].astype(f32) for k in range(3)]
     before = [jnp.where(second_core, n, f) for n, f in zip(near, far)]
     after = [jnp.where(second_core, f, n) for n, f in zip(near, far)]
-    own = [own_ref[k].astype(f32) for k in range(2)]
-    ext = jnp.concatenate([*before[:2], *own, *after[:2]], axis=0)
+    two_before = jnp.concatenate(before[:2], axis=0)
+    two_after = jnp.concatenate(after[:2], axis=0)
     for b in range(3):
-        moved = shifted_columns(ext, b - 1, cols)
-        g_ref[b] = moved.astype(bf16)
-        gt_ref[b] = moved[cols : 5 * cols].astype(bf16).T
-    back = jnp.zeros((4 * cols, ch), f32)
-    for a in range(3):
-        for b in range(3):
-            tap = (3 * (2 - a) + (2 - b)) * ch
-            back += mm(g_ref[b, a * cols : (a + 4) * cols, :], wb_ref[:, tap : tap + ch], NN)
+        gb_ref[b] = shifted_columns(two_before, b - 1, cols).astype(bf16)
+        ga_ref[b] = shifted_columns(two_after, b - 1, cols).astype(bf16)
+        gt_ref[b, :, :cols] = gb_ref[b, cols:, :].T
+        gt_ref[b, :, cols : 3 * cols] = gt_own_ref[b]
+        gt_ref[b, :, 3 * cols :] = ga_ref[b, :cols, :].T
+    up = sum(mm(gb_ref[b], back_weight(wb_ref, 0, b), NN) for b in range(3))
+    up_edge = sum(mm(gb_ref[b, cols:, :], back_weight(wb_ref, 1, b), NN) for b in range(3))
+    down = sum(mm(ga_ref[b], back_weight(wb_ref, 2, b), NN) for b in range(3))
+    down_edge = sum(mm(ga_ref[b, :cols, :], back_weight(wb_ref, 1, b), NN) for b in range(3))
+    back = start_ref[...] + jnp.concatenate(
+        [up[:cols] + up_edge, up[cols:], down[:cols], down[cols:] + down_edge], axis=0
+    )
+    moves[0].wait()
     first = jnp.concatenate([before[2], first_ref[0].astype(f32), first_ref[1].astype(f32), after[2]], axis=0)
     grad_a = jnp.where(first > 0, back, 0.0).astype(bf16).astype(f32)
     for b in range(3):
         moved = shifted_columns(grad_a, b - 1, cols)
         a_ref[b] = moved.astype(bf16)
         at_ref[b] = moved.astype(bf16).T
+    moves[1].wait()
     lidar = jnp.zeros((2 * cols, lid), f32)
     camera = jnp.zeros((cam, 2 * cols), f32)
     for a in range(3):
@@ -111,13 +135,16 @@
     leaving[0].start()
     for r in range(2):
         pick_ref[r] = camera[:, r * cols : (r + 1) * cols].astype(bf16)
+    moves[2].wait()
     picks = [
-        pltpu.make_async_copy(pick_ref.at[jnp.where(spot_ref[2 + k] > 0, 1, 0)], blocks_hbm.at[k], block_sems.at[k])
+        pltpu.make_async_copy(pick_ref.at[jnp.where(list_ref[k] > 0, 1, 0)], blocks_hbm.at[k], block_sems.at[k])
         for k in range(blocks_hbm.shape[0])
     ]
     for pick in picks:
         pick.start()
 
+    moves[3].wait()
+    moves[4].wait()
     per_part = keep_ref.shape[2] // TILE
 
     def put(value, tile):
@@ -128,7 +155,7 @@
         other = jnp.where(second_core, even, odd).astype(bf16)
         for t in range(value.shape[1] // TILE):
             part, at = divmod(tile + t, per_part)
-            part = part ^ spot_ref[1]
+            part = part ^ column_place
             here = slice(at * TILE, (at + 1) * TILE)
             keep_ref[part, :, here] = mine[:, t * TILE : (t + 1) * TILE]
             send_ref[part, :, here] = other[:, t * TILE : (t + 1) * TILE]
@@ -141,7 +168,7 @@
 
     def leave(first_part, end):
         for part in range(first_part, end):
-            place = part ^ spot_ref[1]
+            place = part ^ column_place
             leaving.append(pltpu.make_async_copy(send_ref.at[place], send_hbm.at[place], out_sems.at[part]))
             leaving[-1].start()
 
@@ -245,9 +272,10 @@
 
 def last_sum(dims, scale, *refs):
     ch, lid, cam = dims
-    *parts, spot_ref, wa_ref, wb_ref, all_ref = refs
+    *parts, wa_ref, wb_ref, all_ref = refs
+    column_place = lax.axis_index("scene") >> 1
     for k, part in enumerate(parts):
-        all_ref[k ^ spot_ref[1]] = part[...]
+        all_ref[k ^ column_place] = part[...]
     whole = jnp.concatenate([all_ref[x] for x in range(len(parts))], axis=1) * scale
     wb_ref[...] = whole[:, : 9 * ch]
     pieces = []
@@ -305,16 +333,18 @@
     return part
 
 
-def over_scenes(part, spot, dims, scale):
+def over_scenes(part, dims, scale):
     ch, lid, cam = dims
     (own,) = small(pair_sum, [(part.shape, f32)], (part, swapped(part, "scene", lambda i: i ^ 1)))
-    parts = [own] + [swapped(own, "scene", lambda i, k=k: i ^ 2 * k) for k in range(1, 4)]
+    parts = [own]
+    for k in range(1, 4):
+        parts.append(swapped(own, "scene", lambda i: i ^ 2 * k))
     return call(
         functools.partial(last_sum, dims, scale),
         [jax.ShapeDtypeStruct((8, 9 * width), f32) for width in (cam + lid, ch)],
         [pltpu.VMEM((len(parts), *own.shape), f32)],
-        (*parts, spot),
-        [VM] * len(parts) + [SM],
+        parts,
+        [VM] * len(parts),
         400_000,
         400_000,
     )
@@ -346,21 +376,25 @@
     far = lax.ppermute(far, "space", sides + [(j, i) for i, j in sides])
     near = swapped(near, "space", lambda i: i ^ 1)
     camera = jnp.swapaxes(camera_bev[0], 1, 2)
-    spot = jnp.concatenate(
-        [(lax.axis_index("space") & 1).reshape(1), (lax.axis_index("scene") >> 1).reshape(1), block_list[:, 0, 0]]
-    )
-
     tiles = 9 * (ch + lid) // TILE + -(-9 * cam // TILE)
     per_part = -(-tiles // reach) * TILE
-    own_data = (first, lidar_bev[0], camera, weight_a.T, weight_b)
-    grad_b, *loaded = call(
-        load_kernel,
-        [pltpu.VMEM(x.shape, x.dtype) for x in (first, *own_data)],
-        [pltpu.VMEM(first.shape, bf16)] * 2 + [pltpu.SemaphoreType.DMA((2 + len(own_data),))],
-        (grad_out[0], pre_second[0], *own_data, spot),
-        [HB] * (2 + len(own_data)) + [SM],
-        2_000_000,
-        3_500_000,
+    start, gt_own, wb = call(
+        functools.partial(own_kernel, cols),
+        [
+            pltpu.VMEM((4 * cols, ch), f32),
+            pltpu.VMEM((3, ch, rows * cols), bf16),
+            pltpu.VMEM(weight_b.shape, bf16),
+        ],
+        [
+            pltpu.VMEM(first.shape, bf16),
+            pltpu.VMEM(first.shape, bf16),
+            pltpu.VMEM((3, rows * cols, ch), bf16),
+            pltpu.SemaphoreType.DMA((3,)),
+        ],
+        (grad_out[0], pre_second[0], weight_b),
+        [HB] * 3,
+        300_000_000,
+        2_500_000,
     )
     lidar, blocks, keep, send = call(
         functools.partial(local_kernel, (cols, ch, cam, reach)),
@@ -371,19 +405,26 @@
             pltpu.HBM((reach, ch // 2, per_part), bf16),
         ],
         [
-            pltpu.VMEM((3, 6 * cols, ch), bf16),
+            pltpu.VMEM((3, 2 * cols, ch), bf16),
+            pltpu.VMEM((3, 2 * cols, ch), bf16),
             pltpu.VMEM((3, 4 * cols, ch), bf16),
             pltpu.VMEM((3, ch, 4 * cols), bf16),
             pltpu.VMEM((3, ch, 4 * cols), bf16),
+            pltpu.VMEM(first.shape, bf16),
+            pltpu.VMEM((rows, cols, lid), bf16),
+            pltpu.VMEM(camera.shape, bf16),
+            pltpu.VMEM(weight_a.shape[::-1], bf16),
+            pltpu.SMEM((space,), jnp.int32),
             pltpu.VMEM((2, cam, cols), bf16),
             pltpu.VMEM((rows, cols, lid), bf16),
             pltpu.VMEM((reach, ch // 2, per_part), bf16),
             pltpu.SemaphoreType.DMA((space,)),
             pltpu.SemaphoreType.DMA((reach + 1,)),
+            pltpu.SemaphoreType.DMA((5,)),
         ],
-        (grad_b, near, far, *loaded, spot),
-        [VM] * 8 + [SM],
-        1_800_000_000,
+        (near, far, start, gt_own, wb, first, lidar_bev[0], camera, weight_a.T, block_list[:, 0, 0]),
+        [VM] * 5 + [HB] * 5,
+        1_500_000_000,
         12_000_000,
         outs_at=[HB, HB, VM, HB],
     )
@@ -410,7 +451,7 @@
     )
     along_yz, grad_context, grad_depth = lax.optimization_barrier((along_yz, grad_context, grad_depth))
     (part,) = small(place_sum, [((8, per_part), bf16)], (along_yz,))
-    grad_wa, grad_wb = over_scenes(part, spot, (ch, lid, cam), scale)
+    grad_wa, grad_wb = over_scenes(part, (ch, lid, cam), scale)
     return grad_wa, grad_wb, lidar[None], grad_context[None], grad_depth[None]
 
 

time: 83 us -> 81.7 us (0.984)
  Pallas kernels: 19.3 us -> 17.3 us
  starting transfers between devices: 39.4 us -> 40.9 us
    pallas_call x11, Pallas kernels: 19.3 us -> 17.3 us  [call(): pl.pallas_call(kernel, out_shape=outs, in_specs=specs, out_specs=outs_at...]
    ppermute x10, starting transfers between devices: 20 us -> 21.4 us  [swapped(): lax.ppermute(x, axis, [(i, partner(i)) for i in range(lax.axis_size(axis))])]
  transfers between devices with their start and end apart: 13 -> 13, of which waited for: 8 -> 8; matrix products, arithmetic and copies ran while one was open for 2% -> 1% of each run, Pallas kernels for 14% -> 13%
where the time goes in v4:
time: 81.7 us; the launch traced here: 81.3 us
  starting transfers between devices  40.9 us (50%)
  waiting for transfers between devices  21.7 us (27%)
  Pallas kernels  17.3 us (21%)
    ppermute x10, starting transfers between devices, swapped(): lax.ppermute(x, axis, [(i, partner(i)) for i in range(lax.axis_size(axis))])  21.4 us
    all_to_all x2, starting transfers between devices, exchanged(): return lax.all_to_all(x, axis, 0, 0, axis_index_groups=groups, tiled=True)  18.8 us
    ppermute x10, waiting for transfers between devices, swapped(): lax.ppermute(x, axis, [(i, partner(i)) for i in range(lax.axis_size(axis))])  18 us
    pallas_call x11, Pallas kernels, call(): pl.pallas_call(kernel, out_shape=outs, in_specs=specs, out_specs=outs_at...  17.3 us
    all_to_all x2, waiting for transfers between devices, exchanged(): return lax.all_to_all(x, axis, 0, 0, axis_index_groups=groups, tiled=True)  3.69 us
  transfers between devices with their start and end apart: 13, of which 8 were waited for; matrix products, arithmetic and copies ran while one was open for 1% of the time, Pallas kernels for 13%

profile of v4, /device:TPU:2, one launch (start us, length us, event | category | flops | bytes accessed | tf_op | source)
XLA Modules:
  0.0 81.3 jit_solution(3787558283293210801)
XLA Ops:
  0.6 1.1 %shard_map.146 = (bf16[3,128,256]{2,1,0:T(8,128)(2,1)S(1)}, bf16[3,128,256]{2,1,0:T(8,128)(2,1)S(1)}) custom-call(bf16[2,128,256]{2,1,0:T(8,128)(2,1)} %bitcast.18, bf16[2,128,256]{2,1,0:T(8,128)(2,1)} %bitcast.20, bf16[2,128,256]{2,1,0:T(8,128)(2,1)} %bitcast.22), custom_call_target="tpu_custom_call" | custom-call | flops 1000000 | bytes 1000000 | tf_op jit(solution)/shard_map/pallas_call | solution.py:289
  1.8 0.7 collective-permute-start.1
  2.5 1.9 %shard_map.147 = (f32[512,256]{1,0:T(8,128)S(1)}, bf16[3,256,256]{2,1,0:T(8,128)(2,1)S(1)}, bf16[256,2304]{1,0:T(8,128)(2,1)S(1)}) custom-call(bf16[2,128,256]{2,1,0:T(8,128)(2,1)} %bitcast.19, bf16[2,128,256]{2,1,0:T(8,128)(2,1)} %bitcast.21, bf16[256,2304]{1,0:T(8,128)(2,1)} %wb_hbm.1), custom_call_target="tpu_custom_call" | custom-call | flops 300000000 | bytes 2500000 | tf_op jit(solution)/shard_map/pallas_call | solution.py:289
  4.5 4.8 %shard_map.148 = (bf16[2,128,256]{2,1,0:T(8,128)(2,1)}, bf16[32,80,128]{2,1,0:T(8,128)(2,1)}, bf16[4,128,1408]{2,1,0:T(8,128)(2,1)S(1)}, bf16[4,128,1408]{2,1,0:T(8,128)(2,1)}) custom-call(bf16[3,128,256]{2,1,0:T(8,128)(2,1)S(1)} %collective-permute-done.near_ref, bf16[3,128,256]{2,1,0:T(8,128)(2,1)S(1)} %collective-permute-done.1.far_ref, ...), custom_call_target="tpu_custom_call" | custom-call | flops 1500000000 | bytes 12000000 | tf_op jit(solution)/shard_map/pallas_call | solution.py:289
  9.3 4.9 %collective-permute-start.2 = (bf16[4,128,1408]{2,1,0:T(8,128)(2,1)}, bf16[4,128,1408]{2,1,0:T(8,128)(2,1)S(1)}, u32[]{:S(2)}, u32[]{:S(2)}) collective-permute-start(bf16[4,128,1408]{2,1,0:T(8,128)(2,1)} %get-tuple-element.37), channel_id=1, source_target_pairs={{0,8},{8,0},{16,24},{24,16},{32,40},{40,32},{48,56},{56,48},{64,72... | collective-permute-start | bytes 4325384 | tf_op jit(solution)/shard_map/ppermute | solution.py:316
  14.2 11.6 %all-to-all-start = ((bf16[32,80,128]{2,1,0:T(8,128)(2,1)}), bf16[32,80,128]{2,1,0:T(8,128)(2,1)S(1)}, u32[]{:S(2)}, u32[]{:S(2)}) async-start(bf16[32,80,128]{2,1,0:T(8,128)(2,1)} %get-tuple-element.35), calls=%async_computation | async-start | bytes 1310720 | tf_op jit(solution)/shard_map/all_to_all | solution.py:312
  26.6 2.2 %collective-permute-start.4 = (bf16[2,64,1408]{2,1,0:T(8,128)(2,1)S(1)}, bf16[2,64,1408]{2,1,0:T(8,128)(2,1)S(1)}, u32[]{:S(2)}, u32[]{:S(2)}) collective-permute-start(bf16[2,64,1408]{2,1,0:T(8,128)(2,1)S(1)} %get-tuple-element.41), channel_id=1, source_target_pairs={{0,6},{1,7},{2,4},{3,5},{4,2},{5,3},{6,0},{7,1},{8,14},{9,15},{10,... | collective-permute-start | bytes 1081352 | tf_op jit(solution)/shard_map/ppermute | solution.py:316
  28.9 7.8 %collective-permute-done.3.a_ref = bf16[2,64,1408]{2,1,0:T(8,128)(2,1)S(1)} collective-permute-done((bf16[2,64,1408]{2,1,0:T(8,128)(2,1)S(1)}, bf16[2,64,1408]{2,1,0:T(8,128)(2,1)S(1)}, u32[]{:S(2)}, u32[]{:S(2)}) %collective-permute-start.3) | collective-permute-done | bytes 360480 | tf_op jit(solution)/shard_map/ppermute | solution.py:316
  37.5 1.8 %collective-permute-start.5 = (bf16[64,1408]{1,0:T(8,128)(2,1)S(1)}, bf16[64,1408]{1,0:T(8,128)(2,1)S(1)}, u32[]{:S(2)}, u32[]{:S(2)}) collective-permute-start(bf16[64,1408]{1,0:T(8,128)(2,1)S(1)} %get-tuple-element.43), channel_id=1, source_target_pairs={{0,6},{1,7},{2,4},{3,5},{4,2},{5,3},{6,0},{7,1},{8,14},{9,15},{10,... | collective-permute-start | bytes 540680 | tf_op jit(solution)/shard_map/ppermute | solution.py:316
  39.3 2.6 %collective-permute-start.6 = (bf16[64,1408]{1,0:T(8,128)(2,1)S(1)}, bf16[64,1408]{1,0:T(8,128)(2,1)S(1)}, u32[]{:S(2)}, u32[]{:S(2)}) collective-permute-start(bf16[64,1408]{1,0:T(8,128)(2,1)S(1)} %get-tuple-element.44), channel_id=1, source_target_pairs={{0,2},{1,3},{2,0},{3,1},{4,6},{5,7},{6,4},{7,5},{8,10},{9,11},{10,... | collective-permute-start | bytes 540680 | tf_op jit(solution)/shard_map/ppermute | solution.py:316
  42.0 1.5 %collective-permute-done.5.a_ref = bf16[64,1408]{1,0:T(8,128)(2,1)S(1)} collective-permute-done((bf16[64,1408]{1,0:T(8,128)(2,1)S(1)}, bf16[64,1408]{1,0:T(8,128)(2,1)S(1)}, u32[]{:S(2)}, u32[]{:S(2)}) %collective-permute-start.5) | collective-permute-done | bytes 180256 | tf_op jit(solution)/shard_map/ppermute | solution.py:316
  43.4 2.1 %collective-permute-done.6.b_ref = bf16[64,1408]{1,0:T(8,128)(2,1)S(1)} collective-permute-done((bf16[64,1408]{1,0:T(8,128)(2,1)S(1)}, bf16[64,1408]{1,0:T(8,128)(2,1)S(1)}, u32[]{:S(2)}, u32[]{:S(2)}) %collective-permute-start.6) | collective-permute-done | bytes 180256 | tf_op jit(solution)/shard_map/ppermute | solution.py:316
  45.5 0.8 shard_map.152
  46.3 7.2 %all-to-all-start.1 = ((bf16[16,8,1408]{2,1,0:T(8,128)(2,1)}), bf16[16,8,1408]{2,1,0:T(8,128)(2,1)S(1)}, u32[]{:S(2)}, u32[]{:S(2)}) async-start(bf16[16,8,1408]{2,1,0:T(8,128)(2,1)} %bitcast.8), calls=%async_computation.1 | async-start | bytes 720896 | tf_op jit(solution)/shard_map/all_to_all | solution.py:312
  53.5 7.4 %shard_map.153 = (f32[80,128]{1,0:T(8,128)}, f32[118,128]{1,0:T(8,128)S(1)}) custom-call(bf16[32,80,128]{2,1,0:T(8,128)(2,1)S(1)} %all-to-all-done.blocks_ref, bf16[118,128]{1,0:T(8,128)(2,1)S(1)} %bitcast.16, bf16[80,128]{1,0:T(8,128)(2,1)S(1)} %bitcast.17, s32[118,128]{1,0:T(8,128)S(1)} %copy-done), custom_call_target="tpu_custom_call" | custom-call | flops 2000000000 | bytes 2000000 | tf_op jit(solution)/shard_map/pallas_call | solution.py:289
  60.9 3.7 %all-to-all-done.1.parts_ref = bf16[16,8,1408]{2,1,0:T(8,128)(2,1)S(1)} async-done(((bf16[16,8,1408]{2,1,0:T(8,128)(2,1)}), bf16[16,8,1408]{2,1,0:T(8,128)(2,1)S(1)}, u32[]{:S(2)}, u32[]{:S(2)}) %all-to-all-start.1) | async-done | bytes 360480 | tf_op jit(solution)/shard_map/all_to_all | solution.py:312
  64.7 5.0 %collective-permute-start.7 = (bf16[8,1408]{1,0:T(8,128)(2,1)S(1)}, bf16[8,1408]{1,0:T(8,128)(2,1)S(1)}, u32[]{:S(2)}, u32[]{:S(2)}) collective-permute-start(bf16[8,1408]{1,0:T(8,128)(2,1)S(1)} %shard_map.154.one_ref), channel_id=1, source_target_pairs={{0,1},{1,0},{2,3},{3,2},{4,5},{5,4},{6,7},{7,6},{8,9},{9,8},{10,11... | collective-permute-start | bytes 67592 | tf_op jit(solution)/shard_map/ppermute | solution.py:316
  69.7 2.8 %collective-permute-done.7.two_ref = bf16[8,1408]{1,0:T(8,128)(2,1)S(1)} collective-permute-done((bf16[8,1408]{1,0:T(8,128)(2,1)S(1)}, bf16[8,1408]{1,0:T(8,128)(2,1)S(1)}, u32[]{:S(2)}, u32[]{:S(2)}) %collective-permute-start.7) | collective-permute-done | bytes 22560 | tf_op jit(solution)/shard_map/ppermute | solution.py:316
  72.5 0.8 collective-permute-start.10
  73.3 3.3 %collective-permute-start.9 = (f32[8,1408]{1,0:T(8,128)S(1)}, f32[8,1408]{1,0:T(8,128)S(1)}, u32[]{:S(2)}, u32[]{:S(2)}) collective-permute-start(f32[8,1408]{1,0:T(8,128)S(1)} %shard_map.155.refs_0_), channel_id=1, source_target_pairs={{0,4},{1,5},{2,6},{3,7},{4,0},{5,1},{6,2},{7,3},{8,12},{9,13},{10,... | collective-permute-start | bytes 135176 | tf_op jit(solution)/shard_map/ppermute | solution.py:316
  76.7 0.7 copy.16
  77.4 1.5 %collective-permute-done.9.refs_2_ = f32[8,1408]{1,0:T(8,128)S(1)} collective-permute-done((f32[8,1408]{1,0:T(8,128)S(1)}, f32[8,1408]{1,0:T(8,128)S(1)}, u32[]{:S(2)}, u32[]{:S(2)}) %collective-permute-start.9) | collective-permute-done | bytes 45088 | tf_op jit(solution)/shard_map/ppermute | solution.py:316
  78.8 1.8 %collective-permute-done.8.refs_1_ = f32[8,1408]{1,0:T(8,128)S(1)} collective-permute-done((f32[8,1408]{1,0:T(8,128)S(1)}, f32[8,1408]{1,0:T(8,128)S(1)}, u32[]{:S(2)}, u32[]{:S(2)}) %collective-permute-start.8) | collective-permute-done | bytes 45088 | tf_op jit(solution)/shard_map/ppermute | solution.py:316
  80.6 0.8 shard_map.156
  (20 shorter events, 2.0 us)
Async XLA Ops:
  1.7 2.7 %collective-permute-start = (bf16[3,128,256]{2,1,0:T(8,128)(2,1)S(1)}, bf16[3,128,256]{2,1,0:T(8,128)(2,1)S(1)}, u32[]{:S(2)}, u32[]{:S(2)}) collective-permute-start(bf16[3,128,256]{2,1,0:T(8,128)(2,1)S(1)} %get-tuple-element.30), channel_id=1, source_target_pairs={{0,8},{8,0},{16,24},{24,16},{32,40},{40,32},{48,56},{56,48},{64,72... | collective-permute-start | bytes 589832 | tf_op jit(solution)/shard_map/ppermute | solution.py:316
  1.8 2.6 %collective-permute-start.1 = (bf16[3,128,256]{2,1,0:T(8,128)(2,1)S(1)}, bf16[3,128,256]{2,1,0:T(8,128)(2,1)S(1)}, u32[]{:S(2)}, u32[]{:S(2)}) collective-permute-start(bf16[3,128,256]{2,1,0:T(8,128)(2,1)S(1)} %get-tuple-element.31), channel_id=1, source_target_pairs={{8,16},{24,32},{40,48},{56,64},{72,80},{88,96},{104,112},{120,128}... | collective-permute-start | bytes 589832 | tf_op jit(solution)/shard_map/ppermute | solution.py:376
  9.3 16.5 %collective-permute-start.2 = (bf16[4,128,1408]{2,1,0:T(8,128)(2,1)}, bf16[4,128,1408]{2,1,0:T(8,128)(2,1)S(1)}, u32[]{:S(2)}, u32[]{:S(2)}) collective-permute-start(bf16[4,128,1408]{2,1,0:T(8,128)(2,1)} %get-tuple-element.37), channel_id=1, source_target_pairs={{0,8},{8,0},{16,24},{24,16},{32,40},{40,32},{48,56},{56,48},{64,72... | collective-permute-start | bytes 4325384 | tf_op jit(solution)/shard_map/ppermute | solution.py:316
  14.2 32.1 %all-to-all-start = ((bf16[32,80,128]{2,1,0:T(8,128)(2,1)}), bf16[32,80,128]{2,1,0:T(8,128)(2,1)S(1)}, u32[]{:S(2)}, u32[]{:S(2)}) async-start(bf16[32,80,128]{2,1,0:T(8,128)(2,1)} %get-tuple-element.35), calls=%async_computation | async-start | bytes 1310720 | tf_op jit(solution)/shard_map/all_to_all | solution.py:312
  26.0 10.7 %collective-permute-start.3 = (bf16[2,64,1408]{2,1,0:T(8,128)(2,1)S(1)}, bf16[2,64,1408]{2,1,0:T(8,128)(2,1)S(1)}, u32[]{:S(2)}, u32[]{:S(2)}) collective-permute-start(bf16[2,64,1408]{2,1,0:T(8,128)(2,1)S(1)} %get-tuple-element.40), channel_id=1, source_target_pairs={{0,2},{1,3},{2,0},{3,1},{4,6},{5,7},{6,4},{7,5},{8,10},{9,11},{10,... | collective-permute-start | bytes 1081352 | tf_op jit(solution)/shard_map/ppermute | solution.py:316
  26.6 10.7 %collective-permute-start.4 = (bf16[2,64,1408]{2,1,0:T(8,128)(2,1)S(1)}, bf16[2,64,1408]{2,1,0:T(8,128)(2,1)S(1)}, u32[]{:S(2)}, u32[]{:S(2)}) collective-permute-start(bf16[2,64,1408]{2,1,0:T(8,128)(2,1)S(1)} %get-tuple-element.41), channel_id=1, source_target_pairs={{0,6},{1,7},{2,4},{3,5},{4,2},{5,3},{6,0},{7,1},{8,14},{9,15},{10,... | collective-permute-start | bytes 1081352 | tf_op jit(solution)/shard_map/ppermute | solution.py:316
  37.4 16.0 %copy-start = (s32[118,128]{1,0:T(8,128)S(1)}, s32[118,128]{1,0:T(8,128)}, u32[]{:S(2)}) copy-start(s32[118,128]{1,0:T(8,128)} %slot_ref.1) | copy-start | bytes 181252
  37.5 16.0 %copy-start.1 = (bf16[1,118,128]{2,1,0:T(8,128)(2,1)S(1)}, bf16[1,118,128]{2,1,0:T(8,128)(2,1)}, u32[]{:S(2)}) copy-start(bf16[1,118,128]{2,1,0:T(8,128)(2,1)} %param.18) | copy-start | bytes 90628
  37.5 16.0 %copy-start.2 = (bf16[1,80,128]{2,1,0:T(8,128)(2,1)S(1)}, bf16[1,80,128]{2,1,0:T(8,128)(2,1)}, u32[]{:S(2)}) copy-start(bf16[1,80,128]{2,1,0:T(8,128)(2,1)} %param.19) | copy-start | bytes 61444
  37.5 6.0 %collective-permute-start.5 = (bf16[64,1408]{1,0:T(8,128)(2,1)S(1)}, bf16[64,1408]{1,0:T(8,128)(2,1)S(1)}, u32[]{:S(2)}, u32[]{:S(2)}) collective-permute-start(bf16[64,1408]{1,0:T(8,128)(2,1)S(1)} %get-tuple-element.43), channel_id=1, source_target_pairs={{0,6},{1,7},{2,4},{3,5},{4,2},{5,3},{6,0},{7,1},{8,14},{9,15},{10,... | collective-permute-start | bytes 540680 | tf_op jit(solution)/shard_map/ppermute | solution.py:316
  39.3 6.2 %collective-permute-start.6 = (bf16[64,1408]{1,0:T(8,128)(2,1)S(1)}, bf16[64,1408]{1,0:T(8,128)(2,1)S(1)}, u32[]{:S(2)}, u32[]{:S(2)}) collective-permute-start(bf16[64,1408]{1,0:T(8,128)(2,1)S(1)} %get-tuple-element.44), channel_id=1, source_target_pairs={{0,2},{1,3},{2,0},{3,1},{4,6},{5,7},{6,4},{7,5},{8,10},{9,11},{10,... | collective-permute-start | bytes 540680 | tf_op jit(solution)/shard_map/ppermute | solution.py:316
  46.3 18.3 %all-to-all-start.1 = ((bf16[16,8,1408]{2,1,0:T(8,128)(2,1)}), bf16[16,8,1408]{2,1,0:T(8,128)(2,1)S(1)}, u32[]{:S(2)}, u32[]{:S(2)}) async-start(bf16[16,8,1408]{2,1,0:T(8,128)(2,1)} %bitcast.8), calls=%async_computation.1 | async-start | bytes 720896 | tf_op jit(solution)/shard_map/all_to_all | solution.py:312
  64.7 7.8 %collective-permute-start.7 = (bf16[8,1408]{1,0:T(8,128)(2,1)S(1)}, bf16[8,1408]{1,0:T(8,128)(2,1)S(1)}, u32[]{:S(2)}, u32[]{:S(2)}) collective-permute-start(bf16[8,1408]{1,0:T(8,128)(2,1)S(1)} %shard_map.154.one_ref), channel_id=1, source_target_pairs={{0,1},{1,0},{2,3},{3,2},{4,5},{5,4},{6,7},{7,6},{8,9},{9,8},{10,11... | collective-permute-start | bytes 67592 | tf_op jit(solution)/shard_map/ppermute | solution.py:316
  72.5 4.9 %collective-permute-start.10 = (f32[8,1408]{1,0:T(8,128)S(1)}, f32[8,1408]{1,0:T(8,128)S(1)}, u32[]{:S(2)}, u32[]{:S(2)}) collective-permute-start(f32[8,1408]{1,0:T(8,128)S(1)} %shard_map.155.refs_0_), channel_id=1, source_target_pairs={{0,6},{1,7},{2,4},{3,5},{4,2},{5,3},{6,0},{7,1},{8,14},{9,15},{10,... | collective-permute-start | bytes 135176 | tf_op jit(solution)/shard_map/ppermute | solution.py:316
  73.3 5.6 %collective-permute-start.9 = (f32[8,1408]{1,0:T(8,128)S(1)}, f32[8,1408]{1,0:T(8,128)S(1)}, u32[]{:S(2)}, u32[]{:S(2)}) collective-permute-start(f32[8,1408]{1,0:T(8,128)S(1)} %shard_map.155.refs_0_), channel_id=1, source_target_pairs={{0,4},{1,5},{2,6},{3,7},{4,0},{5,1},{6,2},{7,3},{8,12},{9,13},{10,... | collective-permute-start | bytes 135176 | tf_op jit(solution)/shard_map/ppermute | solution.py:316
  76.5 4.0 %collective-permute-start.8 = (f32[8,1408]{1,0:T(8,128)S(1)}, f32[8,1408]{1,0:T(8,128)S(1)}, u32[]{:S(2)}, u32[]{:S(2)}) collective-permute-start(f32[8,1408]{1,0:T(8,128)S(1)} %shard_map.155.refs_0_), channel_id=1, source_target_pairs={{0,2},{1,3},{2,0},{3,1},{4,6},{5,7},{6,4},{7,5},{8,10},{9,11},{10,... | collective-permute-start | bytes 135176 | tf_op jit(solution)/shard_map/ppermute | solution.py:316

commit v5 on v4

--- a/solution.py
+++ b/solution.py
@@ -191,42 +191,70 @@
         pick.wait()
 
 
-def depth_kernel(blocks_ref, weight_ref, context_ref, slot_ref, gc_ref, gd_ref, wt_ref, st_ref, s_ref, m_ref, d_ref):
-    sources, cam, cells_of = blocks_ref.shape
+def turned_slots(slot_ref, wide):
     depth, pix = slot_ref.shape
-    wide = st_ref.shape[1]
+    return jnp.concatenate([slot_ref[...], jnp.full((wide - depth, pix), -1, jnp.int32)], axis=0).T
+
+
+def one_hots(slot, cells, places):
+    count = cells.shape[0]
+    at_cell = jnp.where(cells == (slot & (count - 1)), 1.0, 0.0).astype(bf16)
+    return at_cell, places == (slot >> (count.bit_length() - 1))
+
+
+def mass_kernel(weight_ref, slot_ref, out_ref, wt_ref, st_ref, m_ref):
+    sources, pix, cells_of = out_ref.shape
+    depth, wide = slot_ref.shape[0], st_ref.shape[1]
+    pitch = m_ref.shape[0] // sources
     wt_ref[...] = jnp.concatenate([weight_ref[...].astype(f32), jnp.zeros((wide - depth, pix), f32)], axis=0).T
-    st_ref[...] = jnp.concatenate([slot_ref[...], jnp.full((wide - depth, pix), -1, jnp.int32)], axis=0).T
-    context_t = context_ref[...].astype(f32).T.astype(bf16)
-    pitch = s_ref.shape[0] // sources
-    for s in range(sources):
-        s_ref[s * pitch : s * pitch + pix, :] = mm(context_t, blocks_ref[s], NN)
+    st_ref[...] = turned_slots(slot_ref, wide)
     cells = lax.broadcasted_iota(jnp.int32, (cells_of, wide), 0)
     places = lax.broadcasted_iota(jnp.int32, (sources, wide), 0)
-    shift = cells_of.bit_length() - 1
 
     def pixels(g, carry):
         base = pl.multiple_of(g * 8, 8)
         slots = st_ref[pl.ds(base, 8), :]
         weights = wt_ref[pl.ds(base, 8), :]
+        for k in range(8):
+            at_cell, here = one_hots(slots[k : k + 1], cells, places)
+            m_ref[pl.ds(base + k, sources, stride=pitch), :] = mm(
+                jnp.where(here, weights[k : k + 1], 0.0).astype(bf16), at_cell, NT
+            )
+        return carry
+
+    lax.fori_loop(0, pix // 8, pixels, 0)
+    for s in range(sources):
+        out_ref[s] = m_ref[s * pitch : s * pitch + pix, :].astype(bf16)
+
+
+def depth_kernel(blocks_ref, mass_ref, context_ref, slot_ref, gc_ref, gd_ref, st_ref, s_ref, d_ref):
+    sources, cam, cells_of = blocks_ref.shape
+    depth, pix = slot_ref.shape
+    wide = st_ref.shape[1]
+    pitch = s_ref.shape[0] // sources
+    st_ref[...] = turned_slots(slot_ref, wide)
+    context_t = context_ref[...].astype(f32).T.astype(bf16)
+    total = jnp.zeros((cam, pix), f32)
+    for s in range(sources):
+        s_ref[s * pitch : s * pitch + pix, :] = mm(context_t, blocks_ref[s], NN)
+        total += mm(blocks_ref[s], mass_ref[s], NT)
+    gc_ref[...] = total
+    cells = lax.broadcasted_iota(jnp.int32, (cells_of, wide), 0)
+    places = lax.broadcasted_iota(jnp.int32, (sources, wide), 0)
+
+    def pixels(g, carry):
+        base = pl.multiple_of(g * 8, 8)
+        slots = st_ref[pl.ds(base, 8), :]
         found_rows = []
         for k in range(8):
-            slot = slots[k : k + 1]
-            at_cell = jnp.where(cells == (slot & (cells_of - 1)), 1.0, 0.0).astype(bf16)
-            here = places == (slot >> shift)
-            every = pl.ds(base + k, sources, stride=pitch)
-            m_ref[every, :] = mm(jnp.where(here, weights[k : k + 1], 0.0).astype(bf16), at_cell, NT)
-            found = mm(s_ref[every, :].astype(bf16), at_cell, NN)
+            at_cell, here = one_hots(slots[k : k + 1], cells, places)
+            found = mm(s_ref[pl.ds(base + k, sources, stride=pitch), :].astype(bf16), at_cell, NN)
             found_rows.append(jnp.sum(jnp.where(here, found, 0.0), axis=0, keepdims=True))
         d_ref[pl.ds(base, 8), :] = jnp.concatenate(found_rows, axis=0)
         return carry
 
     lax.fori_loop(0, pix // 8, pixels, 0)
     gd_ref[...] = d_ref[...].T[:depth]
-    total = jnp.zeros((cam, pix), f32)
-    for s in range(sources):
-        total += mm(blocks_ref[s], m_ref[s * pitch : s * pitch + pix, :].astype(bf16), NT)
-    gc_ref[...] = total
 
 
 def added(keep_ref, other_ref, part, rows):
@@ -262,12 +290,15 @@
     out_ref[rows:] = (own_ref[rows:] + b_ref[...].astype(f32)).astype(bf16)
 
 
-def place_sum(parts_ref, out_ref):
-    out_ref[...] = jnp.sum(parts_ref[...].astype(f32), axis=0).astype(bf16)
-
-
-def pair_sum(one_ref, two_ref, out_ref):
-    out_ref[...] = one_ref[...].astype(f32) + two_ref[...].astype(f32)
+def y_sum(parts_ref, out_ref):
+    total = jnp.sum(parts_ref[...].astype(f32), axis=0).astype(bf16)
+    for z in range(out_ref.shape[1]):
+        for h in range(out_ref.shape[0]):
+            out_ref[h, z] = total[8 * z : 8 * z + 8]
+
+
+def z_sum(parts_ref, out_ref):
+    out_ref[...] = jnp.sum(parts_ref[...].astype(f32), axis=0)
 
 
 def last_sum(dims, scale, *refs):
@@ -333,9 +364,8 @@
     return part
 
 
-def over_scenes(part, dims, scale):
+def along_x(own, dims, scale):
     ch, lid, cam = dims
-    (own,) = small(pair_sum, [(part.shape, f32)], (part, swapped(part, "scene", lambda i: i ^ 1)))
     parts = [own]
     for k in range(1, 4):
         parts.append(swapped(own, "scene", lambda i: i ^ 2 * k))
@@ -429,29 +459,50 @@
         outs_at=[HB, HB, VM, HB],
     )
     incoming = exchanged(blocks, "space", None)
+    table = pltpu.VMEM((space * (pix + 8), cols), f32)
+    (mass,) = call(
+        mass_kernel,
+        [shape((space, pix, cols), bf16)],
+        [pltpu.VMEM((pix, 128), f32), pltpu.VMEM((pix, 128), jnp.int32), table],
+        (depth_weights[0], point_slot),
+        [VM] * 2,
+        500_000_000,
+        2_000_000,
+    )
     part = summed_along_x(keep, send)
     incoming, part = lax.optimization_barrier((incoming, part))
-    along_yz = exchanged(
-        part.reshape(place, 8, per_part), "space", [[2 * i + c for i in range(place)] for c in range(2)]
+    deep = place // reach
+    along_y = exchanged(
+        part.reshape(reach, deep * 8, per_part),
+        "space",
+        [[y * 2 * deep + r for y in range(reach)] for r in range(2 * deep)],
     )
     grad_context, grad_depth = call(
         depth_kernel,
         [shape((cam, pix), f32), shape(point_slot.shape, f32)],
-        [
-            pltpu.VMEM((pix, 128), f32),
-            pltpu.VMEM((pix, 128), jnp.int32),
-            pltpu.VMEM((space * (pix + 8), cols), f32),
-            pltpu.VMEM((space * (pix + 8), cols), f32),
-            pltpu.VMEM((pix, 128), f32),
+        [pltpu.VMEM((pix, 128), jnp.int32), table, pltpu.VMEM((pix, 128), f32)],
+        (incoming, mass, context[0], point_slot),
+        [VM] * 4,
+        1_500_000_000,
+        2_000_000,
+    )
+    along_y, grad_context, grad_depth = lax.optimization_barrier((along_y, grad_context, grad_depth))
+    (spread,) = small(y_sum, [((2, deep, 8, per_part), bf16)], (along_y,))
+    along_z = lax.all_to_all(
+        spread.reshape(2 * deep, 8, per_part),
+        ("space", "scene"),
+        0,
+        0,
+        axis_index_groups=[
+            [((y * deep + z) * 2 + c) * scenes + 2 * x + h for h in range(2) for z in range(deep)]
+            for y in range(reach)
+            for c in range(2)
+            for x in range(reach)
         ],
-        (incoming, depth_weights[0], context[0], point_slot),
-        [VM] * 4,
-        2_000_000_000,
-        2_000_000,
-    )
-    along_yz, grad_context, grad_depth = lax.optimization_barrier((along_yz, grad_context, grad_depth))
-    (part,) = small(place_sum, [((8, per_part), bf16)], (along_yz,))
-    grad_wa, grad_wb = over_scenes(part, (ch, lid, cam), scale)
+        tiled=True,
+    )
+    (own,) = small(z_sum, [((8, per_part), f32)], (along_z,))
+    grad_wa, grad_wb = along_x(own, (ch, lid, cam), scale)
     return grad_wa, grad_wb, lidar[None], grad_context[None], grad_depth[None]
 
 

time: 81.7 us -> 86.6 us (1.060)
  the two profiles are of different devices: /device:TPU:2 before, /device:TPU:8 now
where the time goes in v5:
time: 86.6 us; the launch traced here: 86.2 us
  starting transfers between devices  30 us (35%)
  waiting for transfers between devices  20.3 us (23%)
  Pallas kernels  18.9 us (22%)
  blocking collectives  15.5 us (18%)
    pallas_call x12, Pallas kernels, call(): pl.pallas_call(kernel, out_shape=outs, in_specs=specs, out_specs=outs_at...  18.9 us
    ppermute x9, waiting for transfers between devices, swapped(): lax.ppermute(x, axis, [(i, partner(i)) for i in range(lax.axis_size(axis))])  17.2 us
    all_to_all x1, blocking collectives, shards(): lax.all_to_all(spread.reshape(2 * deep, 8, per_part), ('space', 'scene'),...  15.5 us
    all_to_all x2, starting transfers between devices, exchanged(): return lax.all_to_all(x, axis, 0, 0, axis_index_groups=groups, tiled=True)  12.7 us
    ppermute x9, starting transfers between devices, swapped(): lax.ppermute(x, axis, [(i, partner(i)) for i in range(lax.axis_size(axis))])  10.8 us
    ppermute x1, starting transfers between devices, shards(): far = lax.ppermute(far, 'space', sides + [(j, i) for i, j in sides])  6.51 us
    ppermute x1, waiting for transfers between devices, shards(): far = lax.ppermute(far, 'space', sides + [(j, i) for i, j in sides])  3.1 us
  transfers between devices with their start and end apart: 12, of which 7 were waited for; matrix products, arithmetic and copies ran while one was open for 1% of the time, Pallas kernels for 14%

profile of v5, /device:TPU:8, one launch (start us, length us, event | category | flops | bytes accessed | tf_op | source)
XLA Modules:
  0.0 86.2 jit_solution(5981142845606290503)
XLA Ops:
  0.6 1.1 %shard_map.146 = (bf16[3,128,256]{2,1,0:T(8,128)(2,1)S(1)}, bf16[3,128,256]{2,1,0:T(8,128)(2,1)S(1)}) custom-call(bf16[2,128,256]{2,1,0:T(8,128)(2,1)} %bitcast.20, bf16[2,128,256]{2,1,0:T(8,128)(2,1)} %bitcast.22, bf16[2,128,256]{2,1,0:T(8,128)(2,1)} %bitcast.24), custom_call_target="tpu_custom_call" | custom-call | flops 1000000 | bytes 1000000 | tf_op jit(solution)/shard_map/pallas_call | solution.py:320
  1.8 6.5 %collective-permute-start.1 = (bf16[3,128,256]{2,1,0:T(8,128)(2,1)S(1)}, bf16[3,128,256]{2,1,0:T(8,128)(2,1)S(1)}, u32[]{:S(2)}, u32[]{:S(2)}) collective-permute-start(bf16[3,128,256]{2,1,0:T(8,128)(2,1)S(1)} %get-tuple-element.31), channel_id=1, source_target_pairs={{8,16},{24,32},{40,48},{56,64},{72,80},{88,96},{104,112},{120,128}... | collective-permute-start | bytes 589832 | tf_op jit(solution)/shard_map/ppermute | solution.py:406
  8.4 1.9 %shard_map.147 = (f32[512,256]{1,0:T(8,128)S(1)}, bf16[3,256,256]{2,1,0:T(8,128)(2,1)S(1)}, bf16[256,2304]{1,0:T(8,128)(2,1)S(1)}) custom-call(bf16[2,128,256]{2,1,0:T(8,128)(2,1)} %bitcast.21, bf16[2,128,256]{2,1,0:T(8,128)(2,1)} %bitcast.23, bf16[256,2304]{1,0:T(8,128)(2,1)} %wb_hbm.1), custom_call_target="tpu_custom_call" | custom-call | flops 300000000 | bytes 2500000 | tf_op jit(solution)/shard_map/pallas_call | solution.py:320
  10.3 3.1 %collective-permute-done.1.far_ref = bf16[3,128,256]{2,1,0:T(8,128)(2,1)S(1)} collective-permute-done((bf16[3,128,256]{2,1,0:T(8,128)(2,1)S(1)}, bf16[3,128,256]{2,1,0:T(8,128)(2,1)S(1)}, u32[]{:S(2)}, u32[]{:S(2)}) %collective-permute-start.1) | collective-permute-done | bytes 196640 | tf_op jit(solution)/shard_map/ppermute | solution.py:406
  13.4 4.8 %shard_map.148 = (bf16[2,128,256]{2,1,0:T(8,128)(2,1)}, bf16[32,80,128]{2,1,0:T(8,128)(2,1)}, bf16[4,128,1408]{2,1,0:T(8,128)(2,1)S(1)}, bf16[4,128,1408]{2,1,0:T(8,128)(2,1)}) custom-call(bf16[3,128,256]{2,1,0:T(8,128)(2,1)S(1)} %collective-permute-done.near_ref, bf16[3,128,256]{2,1,0:T(8,128)(2,1)S(1)} %collective-permute-done.1.far_ref, ...), custom_call_target="tpu_custom_call" | custom-call | flops 1500000000 | bytes 12000000 | tf_op jit(solution)/shard_map/pallas_call | solution.py:320
  18.3 7.7 %all-to-all-start = ((bf16[32,80,128]{2,1,0:T(8,128)(2,1)}), bf16[32,80,128]{2,1,0:T(8,128)(2,1)S(1)}, u32[]{:S(2)}, u32[]{:S(2)}) async-start(bf16[32,80,128]{2,1,0:T(8,128)(2,1)} %get-tuple-element.35), calls=%async_computation | async-start | bytes 1310720 | tf_op jit(solution)/shard_map/all_to_all | solution.py:343
  26.2 1.6 %collective-permute-start.3 = (bf16[2,64,1408]{2,1,0:T(8,128)(2,1)S(1)}, bf16[2,64,1408]{2,1,0:T(8,128)(2,1)S(1)}, u32[]{:S(2)}, u32[]{:S(2)}) collective-permute-start(bf16[2,64,1408]{2,1,0:T(8,128)(2,1)S(1)} %get-tuple-element.40), channel_id=1, source_target_pairs={{0,2},{1,3},{2,0},{3,1},{4,6},{5,7},{6,4},{7,5},{8,10},{9,11},{10,... | collective-permute-start | bytes 1081352 | tf_op jit(solution)/shard_map/ppermute | solution.py:347
  27.8 2.1 %collective-permute-start.4 = (bf16[2,64,1408]{2,1,0:T(8,128)(2,1)S(1)}, bf16[2,64,1408]{2,1,0:T(8,128)(2,1)S(1)}, u32[]{:S(2)}, u32[]{:S(2)}) collective-permute-start(bf16[2,64,1408]{2,1,0:T(8,128)(2,1)S(1)} %get-tuple-element.41), channel_id=1, source_target_pairs={{0,6},{1,7},{2,4},{3,5},{4,2},{5,3},{6,0},{7,1},{8,14},{9,15},{10,... | collective-permute-start | bytes 1081352 | tf_op jit(solution)/shard_map/ppermute | solution.py:347
  30.0 6.7 %collective-permute-done.3.a_ref = bf16[2,64,1408]{2,1,0:T(8,128)(2,1)S(1)} collective-permute-done((bf16[2,64,1408]{2,1,0:T(8,128)(2,1)S(1)}, bf16[2,64,1408]{2,1,0:T(8,128)(2,1)S(1)}, u32[]{:S(2)}, u32[]{:S(2)}) %collective-permute-start.3) | collective-permute-done | bytes 360480 | tf_op jit(solution)/shard_map/ppermute | solution.py:347
  36.7 2.4 %collective-permute-done.4.b_ref = bf16[2,64,1408]{2,1,0:T(8,128)(2,1)S(1)} collective-permute-done((bf16[2,64,1408]{2,1,0:T(8,128)(2,1)S(1)}, bf16[2,64,1408]{2,1,0:T(8,128)(2,1)S(1)}, u32[]{:S(2)}, u32[]{:S(2)}) %collective-permute-start.4) | collective-permute-done | bytes 360480 | tf_op jit(solution)/shard_map/ppermute | solution.py:347
  39.3 2.2 %collective-permute-start.5 = (bf16[64,1408]{1,0:T(8,128)(2,1)S(1)}, bf16[64,1408]{1,0:T(8,128)(2,1)S(1)}, u32[]{:S(2)}, u32[]{:S(2)}) collective-permute-start(bf16[64,1408]{1,0:T(8,128)(2,1)S(1)} %get-tuple-element.43), channel_id=1, source_target_pairs={{0,6},{1,7},{2,4},{3,5},{4,2},{5,3},{6,0},{7,1},{8,14},{9,15},{10,... | collective-permute-start | bytes 540680 | tf_op jit(solution)/shard_map/ppermute | solution.py:347
  41.5 4.6 %collective-permute-done.5.a_ref = bf16[64,1408]{1,0:T(8,128)(2,1)S(1)} collective-permute-done((bf16[64,1408]{1,0:T(8,128)(2,1)S(1)}, bf16[64,1408]{1,0:T(8,128)(2,1)S(1)}, u32[]{:S(2)}, u32[]{:S(2)}) %collective-permute-start.5) | collective-permute-done | bytes 180256 | tf_op jit(solution)/shard_map/ppermute | solution.py:347
  46.1 0.9 %collective-permute-done.6.b_ref = bf16[64,1408]{1,0:T(8,128)(2,1)S(1)} collective-permute-done((bf16[64,1408]{1,0:T(8,128)(2,1)S(1)}, bf16[64,1408]{1,0:T(8,128)(2,1)S(1)}, u32[]{:S(2)}, u32[]{:S(2)}) %collective-permute-start.6) | collective-permute-done | bytes 180256 | tf_op jit(solution)/shard_map/ppermute | solution.py:347
  47.0 0.8 shard_map.152
  47.8 4.9 %all-to-all-start.1 = ((bf16[4,32,1408]{2,1,0:T(8,128)(2,1)}), bf16[4,32,1408]{2,1,0:T(8,128)(2,1)S(1)}, u32[]{:S(2)}, u32[]{:S(2)}) async-start(bf16[4,32,1408]{2,1,0:T(8,128)(2,1)} %bitcast.8), calls=%async_computation.1 | async-start | bytes 720896 | tf_op jit(solution)/shard_map/all_to_all | solution.py:343
  52.7 4.3 %shard_map.153.mass_ref = bf16[32,128,128]{2,1,0:T(8,128)(2,1)S(1)} custom-call(bf16[118,128]{1,0:T(8,128)(2,1)S(1)} %bitcast.18, s32[118,128]{1,0:T(8,128)S(1)} %copy-done), custom_call_target="tpu_custom_call" | custom-call | flops 500000000 | bytes 2000000 | tf_op jit(solution)/shard_map/pallas_call | solution.py:320
  57.0 4.7 %shard_map.154 = (f32[80,128]{1,0:T(8,128)}, f32[118,128]{1,0:T(8,128)S(1)}) custom-call(bf16[32,80,128]{2,1,0:T(8,128)(2,1)S(1)} %all-to-all-done.blocks_ref, bf16[32,128,128]{2,1,0:T(8,128)(2,1)S(1)} %shard_map.153.mass_ref, bf16[80,128]{1,0:T(8,128)(2,1)S(1)} %bitcast.19, s32[118,128]{1,0:T(8,128)S(1)} %copy-done), custom_call_target="tpu_custom_call" | custom-call | flops 1500000000 | bytes 2000000 | tf_op jit(solution)/shard_map/pallas_call | solution.py:320
  61.8 15.5 %all_to_all.15.parts_ref = bf16[8,8,1408]{2,1,0:T(8,128)(2,1)S(1)} all-to-all(bf16[8,8,1408]{2,1,0:T(8,128)(2,1)S(1)} %bitcast.16), channel_id=1, replica_groups={{0,16,32,48,1,17,33,49},{2,18,34,50,3,19,35,51},{4,20,36,52,5,21,37,53}..., dimensions={0} | all-to-all | bytes 360448 | tf_op jit(solution)/shard_map/all_to_all | solution.py:491
  77.5 2.7 %collective-permute-start.8 = (f32[8,1408]{1,0:T(8,128)S(1)}, f32[8,1408]{1,0:T(8,128)S(1)}, u32[]{:S(2)}, u32[]{:S(2)}) collective-permute-start(f32[8,1408]{1,0:T(8,128)S(1)} %shard_map.156.refs_0_), channel_id=1, source_target_pairs={{0,4},{1,5},{2,6},{3,7},{4,0},{5,1},{6,2},{7,3},{8,12},{9,13},{10,... | collective-permute-start | bytes 135176 | tf_op jit(solution)/shard_map/ppermute | solution.py:347
  80.2 2.0 %collective-permute-start.9 = (f32[8,1408]{1,0:T(8,128)S(1)}, f32[8,1408]{1,0:T(8,128)S(1)}, u32[]{:S(2)}, u32[]{:S(2)}) collective-permute-start(f32[8,1408]{1,0:T(8,128)S(1)} %shard_map.156.refs_0_), channel_id=1, source_target_pairs={{0,6},{1,7},{2,4},{3,5},{4,2},{5,3},{6,0},{7,1},{8,14},{9,15},{10,... | collective-permute-start | bytes 135176 | tf_op jit(solution)/shard_map/ppermute | solution.py:347
  82.2 0.7 copy.16
  82.9 0.3 collective-permute-done.8.refs_2_
  83.1 2.3 %collective-permute-done.9.refs_3_ = f32[8,1408]{1,0:T(8,128)S(1)} collective-permute-done((f32[8,1408]{1,0:T(8,128)S(1)}, f32[8,1408]{1,0:T(8,128)S(1)}, u32[]{:S(2)}, u32[]{:S(2)}) %collective-permute-start.9) | collective-permute-done | bytes 45088 | tf_op jit(solution)/shard_map/ppermute | solution.py:347
  85.4 0.7 shard_map.157
  (20 shorter events, 0.8 us)
Async XLA Ops:
  1.7 8.6 %collective-permute-start = (bf16[3,128,256]{2,1,0:T(8,128)(2,1)S(1)}, bf16[3,128,256]{2,1,0:T(8,128)(2,1)S(1)}, u32[]{:S(2)}, u32[]{:S(2)}) collective-permute-start(bf16[3,128,256]{2,1,0:T(8,128)(2,1)S(1)} %get-tuple-element.30), channel_id=1, source_target_pairs={{0,8},{8,0},{16,24},{24,16},{32,40},{40,32},{48,56},{56,48},{64,72... | collective-permute-start | bytes 589832 | tf_op jit(solution)/shard_map/ppermute | solution.py:347
  1.8 11.6 %collective-permute-start.1 = (bf16[3,128,256]{2,1,0:T(8,128)(2,1)S(1)}, bf16[3,128,256]{2,1,0:T(8,128)(2,1)S(1)}, u32[]{:S(2)}, u32[]{:S(2)}) collective-permute-start(bf16[3,128,256]{2,1,0:T(8,128)(2,1)S(1)} %get-tuple-element.31), channel_id=1, source_target_pairs={{8,16},{24,32},{40,48},{56,64},{72,80},{88,96},{104,112},{120,128}... | collective-permute-start | bytes 589832 | tf_op jit(solution)/shard_map/ppermute | solution.py:406
  18.2 7.8 %collective-permute-start.2 = (bf16[4,128,1408]{2,1,0:T(8,128)(2,1)}, bf16[4,128,1408]{2,1,0:T(8,128)(2,1)S(1)}, u32[]{:S(2)}, u32[]{:S(2)}) collective-permute-start(bf16[4,128,1408]{2,1,0:T(8,128)(2,1)} %get-tuple-element.37), channel_id=1, source_target_pairs={{0,8},{8,0},{16,24},{24,16},{32,40},{40,32},{48,56},{56,48},{64,72... | collective-permute-start | bytes 4325384 | tf_op jit(solution)/shard_map/ppermute | solution.py:347
  18.3 29.5 %all-to-all-start = ((bf16[32,80,128]{2,1,0:T(8,128)(2,1)}), bf16[32,80,128]{2,1,0:T(8,128)(2,1)S(1)}, u32[]{:S(2)}, u32[]{:S(2)}) async-start(bf16[32,80,128]{2,1,0:T(8,128)(2,1)} %get-tuple-element.35), calls=%async_computation | async-start | bytes 1310720 | tf_op jit(solution)/shard_map/all_to_all | solution.py:343
  26.2 10.5 %collective-permute-start.3 = (bf16[2,64,1408]{2,1,0:T(8,128)(2,1)S(1)}, bf16[2,64,1408]{2,1,0:T(8,128)(2,1)S(1)}, u32[]{:S(2)}, u32[]{:S(2)}) collective-permute-start(bf16[2,64,1408]{2,1,0:T(8,128)(2,1)S(1)} %get-tuple-element.40), channel_id=1, source_target_pairs={{0,2},{1,3},{2,0},{3,1},{4,6},{5,7},{6,4},{7,5},{8,10},{9,11},{10,... | collective-permute-start | bytes 1081352 | tf_op jit(solution)/shard_map/ppermute | solution.py:347
  27.8 11.4 %collective-permute-start.4 = (bf16[2,64,1408]{2,1,0:T(8,128)(2,1)S(1)}, bf16[2,64,1408]{2,1,0:T(8,128)(2,1)S(1)}, u32[]{:S(2)}, u32[]{:S(2)}) collective-permute-start(bf16[2,64,1408]{2,1,0:T(8,128)(2,1)S(1)} %get-tuple-element.41), channel_id=1, source_target_pairs={{0,6},{1,7},{2,4},{3,5},{4,2},{5,3},{6,0},{7,1},{8,14},{9,15},{10,... | collective-permute-start | bytes 1081352 | tf_op jit(solution)/shard_map/ppermute | solution.py:347
  39.3 13.4 %copy-start = (s32[118,128]{1,0:T(8,128)S(1)}, s32[118,128]{1,0:T(8,128)}, u32[]{:S(2)}) copy-start(s32[118,128]{1,0:T(8,128)} %slot_ref.3) | copy-start | bytes 181252
  39.3 13.4 %copy-start.1 = (bf16[1,118,128]{2,1,0:T(8,128)(2,1)S(1)}, bf16[1,118,128]{2,1,0:T(8,128)(2,1)}, u32[]{:S(2)}) copy-start(bf16[1,118,128]{2,1,0:T(8,128)(2,1)} %param.18) | copy-start | bytes 90628
  39.3 6.8 %collective-permute-start.5 = (bf16[64,1408]{1,0:T(8,128)(2,1)S(1)}, bf16[64,1408]{1,0:T(8,128)(2,1)S(1)}, u32[]{:S(2)}, u32[]{:S(2)}) collective-permute-start(bf16[64,1408]{1,0:T(8,128)(2,1)S(1)} %get-tuple-element.43), channel_id=1, source_target_pairs={{0,6},{1,7},{2,4},{3,5},{4,2},{5,3},{6,0},{7,1},{8,14},{9,15},{10,... | collective-permute-start | bytes 540680 | tf_op jit(solution)/shard_map/ppermute | solution.py:347
  41.5 5.5 %collective-permute-start.6 = (bf16[64,1408]{1,0:T(8,128)(2,1)S(1)}, bf16[64,1408]{1,0:T(8,128)(2,1)S(1)}, u32[]{:S(2)}, u32[]{:S(2)}) collective-permute-start(bf16[64,1408]{1,0:T(8,128)(2,1)S(1)} %get-tuple-element.44), channel_id=1, source_target_pairs={{0,2},{1,3},{2,0},{3,1},{4,6},{5,7},{6,4},{7,5},{8,10},{9,11},{10,... | collective-permute-start | bytes 540680 | tf_op jit(solution)/shard_map/ppermute | solution.py:347
  47.8 9.3 %copy-start.2 = (bf16[1,80,128]{2,1,0:T(8,128)(2,1)S(1)}, bf16[1,80,128]{2,1,0:T(8,128)(2,1)}, u32[]{:S(2)}) copy-start(bf16[1,80,128]{2,1,0:T(8,128)(2,1)} %param.19) | copy-start | bytes 61444
  47.8 14.0 %all-to-all-start.1 = ((bf16[4,32,1408]{2,1,0:T(8,128)(2,1)}), bf16[4,32,1408]{2,1,0:T(8,128)(2,1)S(1)}, u32[]{:S(2)}, u32[]{:S(2)}) async-start(bf16[4,32,1408]{2,1,0:T(8,128)(2,1)} %bitcast.8), calls=%async_computation.1 | async-start | bytes 720896 | tf_op jit(solution)/shard_map/all_to_all | solution.py:343
  77.4 5.5 %collective-permute-start.7 = (f32[8,1408]{1,0:T(8,128)S(1)}, f32[8,1408]{1,0:T(8,128)S(1)}, u32[]{:S(2)}, u32[]{:S(2)}) collective-permute-start(f32[8,1408]{1,0:T(8,128)S(1)} %shard_map.156.refs_0_), channel_id=1, source_target_pairs={{0,2},{1,3},{2,0},{3,1},{4,6},{5,7},{6,4},{7,5},{8,10},{9,11},{10,... | collective-permute-start | bytes 135176 | tf_op jit(solution)/shard_map/ppermute | solution.py:347
  77.5 5.6 %collective-permute-start.8 = (f32[8,1408]{1,0:T(8,128)S(1)}, f32[8,1408]{1,0:T(8,128)S(1)}, u32[]{:S(2)}, u32[]{:S(2)}) collective-permute-start(f32[8,1408]{1,0:T(8,128)S(1)} %shard_map.156.refs_0_), channel_id=1, source_target_pairs={{0,4},{1,5},{2,6},{3,7},{4,0},{5,1},{6,2},{7,3},{8,12},{9,13},{10,... | collective-permute-start | bytes 135176 | tf_op jit(solution)/shard_map/ppermute | solution.py:347
  80.2 5.3 %collective-permute-start.9 = (f32[8,1408]{1,0:T(8,128)S(1)}, f32[8,1408]{1,0:T(8,128)S(1)}, u32[]{:S(2)}, u32[]{:S(2)}) collective-permute-start(f32[8,1408]{1,0:T(8,128)S(1)} %shard_map.156.refs_0_), channel_id=1, source_target_pairs={{0,6},{1,7},{2,4},{3,5},{4,2},{5,3},{6,0},{7,1},{8,14},{9,15},{10,... | collective-permute-start | bytes 135176 | tf_op jit(solution)/shard_map/ppermute | solution.py:347

commit v6 on v5

--- a/solution.py
+++ b/solution.py
@@ -284,14 +284,26 @@
     out_ref[lower] = own_ref[lower] + b_ref[0].astype(f32)
 
 
-def third_sum(own_ref, a_ref, b_ref, out_ref):
+def third_sum(y_shift, own_ref, a_ref, b_ref, a_out_ref, b_out_ref, own_out_ref, next_ref, all_ref):
     rows = a_ref.shape[0]
-    out_ref[:rows] = (own_ref[:rows] + a_ref[...].astype(f32)).astype(bf16)
-    out_ref[rows:] = (own_ref[rows:] + b_ref[...].astype(f32)).astype(bf16)
-
-
-def y_sum(parts_ref, out_ref):
-    total = jnp.sum(parts_ref[...].astype(f32), axis=0).astype(bf16)
+    count, deep = all_ref.shape[:2]
+    me = lax.axis_index("space") >> y_shift
+    for y in range(count):
+        came = a_ref if y * deep < rows else b_ref
+        at = y * deep % rows
+        all_ref[y ^ me] = own_ref[y * deep : (y + 1) * deep] + came[at : at + deep].astype(f32)
+    upper, lower = slice(0, deep // 2), slice(deep // 2, deep)
+    for k, (one, two) in enumerate([(1, 3), (2, 2)]):
+        a_out_ref[k] = all_ref[one, upper].astype(bf16)
+        b_out_ref[k] = all_ref[two, lower].astype(bf16)
+    own_out_ref[...] = all_ref[0]
+    next_ref[upper] = all_ref[3, upper]
+    next_ref[lower] = all_ref[1, lower]
+
+
+def y_sum(own_ref, a_ref, b_ref, out_ref):
+    came = jnp.concatenate([a_ref[...].astype(f32), b_ref[...].astype(f32)], axis=0)
+    total = (own_ref[...] + came).astype(bf16)
     for z in range(out_ref.shape[1]):
         for h in range(out_ref.shape[0]):
             out_ref[h, z] = total[8 * z : 8 * z + 8]
@@ -360,8 +372,31 @@
         (*kept, a, b),
     )
     a, b = swapped(a, "scene", lambda i: i ^ 6), swapped(b, "scene", lambda i: i ^ 2)
-    (part,) = small(third_sum, [((2 * deep, per_part), bf16)], (own, a, b))
-    return part
+    return own, a, b
+
+
+def summed_along_y(own, a, b, row):
+    rows, per_part = own.shape
+    deep = rows // 4
+    halves = [((2, deep // 2, per_part), bf16)] * 2 + [((deep, per_part), f32)] * 2
+    a, b, *kept = call(
+        functools.partial(third_sum, row.bit_length() - 1),
+        [jax.ShapeDtypeStruct(*spec) for spec in halves],
+        [pltpu.VMEM((4, deep, per_part), f32)],
+        (own, a, b),
+        [VM] * 3,
+        2_000_000,
+        2_000_000,
+    )
+    a, b = swapped(a, "space", lambda i: i ^ row), swapped(b, "space", lambda i: i ^ 3 * row)
+    own, a, b = small(
+        second_sum,
+        [((deep, per_part), f32), ((deep // 2, per_part), bf16), ((deep // 2, per_part), bf16)],
+        (*kept, a, b),
+    )
+    a, b = swapped(a, "space", lambda i: i ^ 3 * row), swapped(b, "space", lambda i: i ^ row)
+    (spread,) = small(y_sum, [((2, deep // 8, 8, per_part), bf16)], (own, a, b))
+    return spread
 
 
 def along_x(own, dims, scale):
@@ -469,14 +504,9 @@
         500_000_000,
         2_000_000,
     )
-    part = summed_along_x(keep, send)
-    incoming, part = lax.optimization_barrier((incoming, part))
     deep = place // reach
-    along_y = exchanged(
-        part.reshape(reach, deep * 8, per_part),
-        "space",
-        [[y * 2 * deep + r for y in range(reach)] for r in range(2 * deep)],
-    )
+    spread = summed_along_y(*summed_along_x(keep, send), 2 * deep)
+    incoming, spread = lax.optimization_barrier((incoming, spread))
     grad_context, grad_depth = call(
         depth_kernel,
         [shape((cam, pix), f32), shape(point_slot.shape, f32)],
@@ -486,8 +516,6 @@
         1_500_000_000,
         2_000_000,
     )
-    along_y, grad_context, grad_depth = lax.optimization_barrier((along_y, grad_context, grad_depth))
-    (spread,) = small(y_sum, [((2, deep, 8, per_part), bf16)], (along_y,))
     along_z = lax.all_to_all(
         spread.reshape(2 * deep, 8, per_part),
         ("space", "scene"),
@@ -501,6 +529,7 @@
         ],
         tiled=True,
     )
+    along_z, grad_context, grad_depth = lax.optimization_barrier((along_z, grad_context, grad_depth))
     (own,) = small(z_sum, [((8, per_part), f32)], (along_z,))
     grad_wa, grad_wb = along_x(own, (ch, lid, cam), scale)
     return grad_wa, grad_wb, lidar[None], grad_context[None], grad_depth[None]

time: 86.6 us -> 85.1 us (0.983)
  the two profiles are of different devices: /device:TPU:8 before, /device:TPU:32 now
where the time goes in v6:
time: 85.1 us; the launch traced here: 84.8 us
  starting transfers between devices  37.4 us (44%)
  waiting for transfers between devices  27 us (32%)
  Pallas kernels  18.9 us (22%)
    ppermute x13, waiting for transfers between devices, swapped(): lax.ppermute(x, axis, [(i, partner(i)) for i in range(lax.axis_size(axis))])  24.1 us
    pallas_call x13, Pallas kernels, call(): pl.pallas_call(kernel, out_shape=outs, in_specs=specs, out_specs=outs_at...  18.9 us
    ppermute x13, starting transfers between devices, swapped(): lax.ppermute(x, axis, [(i, partner(i)) for i in range(lax.axis_size(axis))])  16.9 us
    all_to_all x1, starting transfers between devices, exchanged(): return lax.all_to_all(x, axis, 0, 0, axis_index_groups=groups, tiled=True)  9.96 us
    all_to_all x1, starting transfers between devices, shards(): lax.all_to_all(spread.reshape(2 * deep, 8, per_part), ('space', 'scene'),...  6.68 us
    ppermute x1, starting transfers between devices, shards(): far = lax.ppermute(far, 'space', sides + [(j, i) for i, j in sides])  3.81 us
    ppermute x1, waiting for transfers between devices, shards(): far = lax.ppermute(far, 'space', sides + [(j, i) for i, j in sides])  2.95 us
  transfers between devices with their start and end apart: 16, of which 11 were waited for; matrix products, arithmetic and copies ran while one was open for 1% of the time, Pallas kernels for 14%

profile of v6, /device:TPU:32, one launch (start us, length us, event | category | flops | bytes accessed | tf_op | source)
XLA Modules:
  0.0 84.8 jit_solution(5557438202363150207)
XLA Ops:
  0.6 1.1 %shard_map.146 = (bf16[3,128,256]{2,1,0:T(8,128)(2,1)S(1)}, bf16[3,128,256]{2,1,0:T(8,128)(2,1)S(1)}) custom-call(bf16[2,128,256]{2,1,0:T(8,128)(2,1)} %bitcast.18, bf16[2,128,256]{2,1,0:T(8,128)(2,1)} %bitcast.20, bf16[2,128,256]{2,1,0:T(8,128)(2,1)} %bitcast.22), custom_call_target="tpu_custom_call" | custom-call | flops 1000000 | bytes 1000000 | tf_op jit(solution)/shard_map/pallas_call | solution.py:332
  1.8 3.8 %collective-permute-start.1 = (bf16[3,128,256]{2,1,0:T(8,128)(2,1)S(1)}, bf16[3,128,256]{2,1,0:T(8,128)(2,1)S(1)}, u32[]{:S(2)}, u32[]{:S(2)}) collective-permute-start(bf16[3,128,256]{2,1,0:T(8,128)(2,1)S(1)} %get-tuple-element.38), channel_id=1, source_target_pairs={{8,16},{24,32},{40,48},{56,64},{72,80},{88,96},{104,112},{120,128}... | collective-permute-start | bytes 589832 | tf_op jit(solution)/shard_map/ppermute | solution.py:441
  5.7 1.9 %shard_map.147 = (f32[512,256]{1,0:T(8,128)S(1)}, bf16[3,256,256]{2,1,0:T(8,128)(2,1)S(1)}, bf16[256,2304]{1,0:T(8,128)(2,1)S(1)}) custom-call(bf16[2,128,256]{2,1,0:T(8,128)(2,1)} %bitcast.19, bf16[2,128,256]{2,1,0:T(8,128)(2,1)} %bitcast.21, bf16[256,2304]{1,0:T(8,128)(2,1)} %wb_hbm.1), custom_call_target="tpu_custom_call" | custom-call | flops 300000000 | bytes 2500000 | tf_op jit(solution)/shard_map/pallas_call | solution.py:332
  7.6 3.0 %collective-permute-done.1.far_ref = bf16[3,128,256]{2,1,0:T(8,128)(2,1)S(1)} collective-permute-done((bf16[3,128,256]{2,1,0:T(8,128)(2,1)S(1)}, bf16[3,128,256]{2,1,0:T(8,128)(2,1)S(1)}, u32[]{:S(2)}, u32[]{:S(2)}) %collective-permute-start.1) | collective-permute-done | bytes 196640 | tf_op jit(solution)/shard_map/ppermute | solution.py:441
  10.6 4.8 %shard_map.148 = (bf16[2,128,256]{2,1,0:T(8,128)(2,1)}, bf16[32,80,128]{2,1,0:T(8,128)(2,1)}, bf16[4,128,1408]{2,1,0:T(8,128)(2,1)S(1)}, bf16[4,128,1408]{2,1,0:T(8,128)(2,1)}) custom-call(bf16[3,128,256]{2,1,0:T(8,128)(2,1)S(1)} %collective-permute-done.near_ref, bf16[3,128,256]{2,1,0:T(8,128)(2,1)S(1)} %collective-permute-done.1.far_ref, ...), custom_call_target="tpu_custom_call" | custom-call | flops 1500000000 | bytes 12000000 | tf_op jit(solution)/shard_map/pallas_call | solution.py:332
  15.7 10.0 %all-to-all-start = ((bf16[32,80,128]{2,1,0:T(8,128)(2,1)}), bf16[32,80,128]{2,1,0:T(8,128)(2,1)S(1)}, u32[]{:S(2)}, u32[]{:S(2)}) async-start(bf16[32,80,128]{2,1,0:T(8,128)(2,1)} %get-tuple-element.42), calls=%async_computation | async-start | bytes 1310720 | tf_op jit(solution)/shard_map/all_to_all | solution.py:355
  25.9 1.6 %collective-permute-start.3 = (bf16[2,64,1408]{2,1,0:T(8,128)(2,1)S(1)}, bf16[2,64,1408]{2,1,0:T(8,128)(2,1)S(1)}, u32[]{:S(2)}, u32[]{:S(2)}) collective-permute-start(bf16[2,64,1408]{2,1,0:T(8,128)(2,1)S(1)} %get-tuple-element.47), channel_id=1, source_target_pairs={{0,2},{1,3},{2,0},{3,1},{4,6},{5,7},{6,4},{7,5},{8,10},{9,11},{10,... | collective-permute-start | bytes 1081352 | tf_op jit(solution)/shard_map/ppermute | solution.py:359
  27.5 2.1 %collective-permute-start.4 = (bf16[2,64,1408]{2,1,0:T(8,128)(2,1)S(1)}, bf16[2,64,1408]{2,1,0:T(8,128)(2,1)S(1)}, u32[]{:S(2)}, u32[]{:S(2)}) collective-permute-start(bf16[2,64,1408]{2,1,0:T(8,128)(2,1)S(1)} %get-tuple-element.48), channel_id=1, source_target_pairs={{0,6},{1,7},{2,4},{3,5},{4,2},{5,3},{6,0},{7,1},{8,14},{9,15},{10,... | collective-permute-start | bytes 1081352 | tf_op jit(solution)/shard_map/ppermute | solution.py:359
  29.7 6.7 %collective-permute-done.3.a_ref = bf16[2,64,1408]{2,1,0:T(8,128)(2,1)S(1)} collective-permute-done((bf16[2,64,1408]{2,1,0:T(8,128)(2,1)S(1)}, bf16[2,64,1408]{2,1,0:T(8,128)(2,1)S(1)}, u32[]{:S(2)}, u32[]{:S(2)}) %collective-permute-start.3) | collective-permute-done | bytes 360480 | tf_op jit(solution)/shard_map/ppermute | solution.py:359
  36.4 2.5 %collective-permute-done.4.b_ref = bf16[2,64,1408]{2,1,0:T(8,128)(2,1)S(1)} collective-permute-done((bf16[2,64,1408]{2,1,0:T(8,128)(2,1)S(1)}, bf16[2,64,1408]{2,1,0:T(8,128)(2,1)S(1)}, u32[]{:S(2)}, u32[]{:S(2)}) %collective-permute-start.4) | collective-permute-done | bytes 360480 | tf_op jit(solution)/shard_map/ppermute | solution.py:359
  39.0 2.1 %collective-permute-start.5 = (bf16[64,1408]{1,0:T(8,128)(2,1)S(1)}, bf16[64,1408]{1,0:T(8,128)(2,1)S(1)}, u32[]{:S(2)}, u32[]{:S(2)}) collective-permute-start(bf16[64,1408]{1,0:T(8,128)(2,1)S(1)} %get-tuple-element.50), channel_id=1, source_target_pairs={{0,6},{1,7},{2,4},{3,5},{4,2},{5,3},{6,0},{7,1},{8,14},{9,15},{10,... | collective-permute-start | bytes 540680 | tf_op jit(solution)/shard_map/ppermute | solution.py:359
  41.1 4.6 %collective-permute-done.5.a_ref = bf16[64,1408]{1,0:T(8,128)(2,1)S(1)} collective-permute-done((bf16[64,1408]{1,0:T(8,128)(2,1)S(1)}, bf16[64,1408]{1,0:T(8,128)(2,1)S(1)}, u32[]{:S(2)}, u32[]{:S(2)}) %collective-permute-start.5) | collective-permute-done | bytes 180256 | tf_op jit(solution)/shard_map/ppermute | solution.py:359
  46.7 1.6 %collective-permute-start.7 = (bf16[2,16,1408]{2,1,0:T(8,128)(2,1)S(1)}, bf16[2,16,1408]{2,1,0:T(8,128)(2,1)S(1)}, u32[]{:S(2)}, u32[]{:S(2)}) collective-permute-start(bf16[2,16,1408]{2,1,0:T(8,128)(2,1)S(1)} %get-tuple-element.54), channel_id=1, source_target_pairs={{0,64},{8,72},{16,80},{24,88},{32,96},{40,104},{48,112},{56,120},{... | collective-permute-start | bytes 270344 | tf_op jit(solution)/shard_map/ppermute | solution.py:359
  48.3 2.1 %collective-permute-start.8 = (bf16[2,16,1408]{2,1,0:T(8,128)(2,1)S(1)}, bf16[2,16,1408]{2,1,0:T(8,128)(2,1)S(1)}, u32[]{:S(2)}, u32[]{:S(2)}) collective-permute-start(bf16[2,16,1408]{2,1,0:T(8,128)(2,1)S(1)} %get-tuple-element.55), channel_id=1, source_target_pairs={{0,192},{8,200},{16,208},{24,216},{32,224},{40,232},{48,240},{56,2... | collective-permute-start | bytes 270344 | tf_op jit(solution)/shard_map/ppermute | solution.py:359
  51.3 2.7 %collective-permute-done.8.b_ref = bf16[2,16,1408]{2,1,0:T(8,128)(2,1)S(1)} collective-permute-done((bf16[2,16,1408]{2,1,0:T(8,128)(2,1)S(1)}, bf16[2,16,1408]{2,1,0:T(8,128)(2,1)S(1)}, u32[]{:S(2)}, u32[]{:S(2)}) %collective-permute-start.8) | collective-permute-done | bytes 90144 | tf_op jit(solution)/shard_map/ppermute | solution.py:359
  54.2 2.2 %collective-permute-start.9 = (bf16[16,1408]{1,0:T(8,128)(2,1)S(1)}, bf16[16,1408]{1,0:T(8,128)(2,1)S(1)}, u32[]{:S(2)}, u32[]{:S(2)}) collective-permute-start(bf16[16,1408]{1,0:T(8,128)(2,1)S(1)} %get-tuple-element.57), channel_id=1, source_target_pairs={{0,192},{8,200},{16,208},{24,216},{32,224},{40,232},{48,240},{56,2... | collective-permute-start | bytes 135176 | tf_op jit(solution)/shard_map/ppermute | solution.py:359
  56.3 1.9 %collective-permute-done.10.b_ref = bf16[16,1408]{1,0:T(8,128)(2,1)S(1)} collective-permute-done((bf16[16,1408]{1,0:T(8,128)(2,1)S(1)}, bf16[16,1408]{1,0:T(8,128)(2,1)S(1)}, u32[]{:S(2)}, u32[]{:S(2)}) %collective-permute-start.10) | collective-permute-done | bytes 45088 | tf_op jit(solution)/shard_map/ppermute | solution.py:359
  58.2 1.3 %collective-permute-done.9.a_ref = bf16[16,1408]{1,0:T(8,128)(2,1)S(1)} collective-permute-done((bf16[16,1408]{1,0:T(8,128)(2,1)S(1)}, bf16[16,1408]{1,0:T(8,128)(2,1)S(1)}, u32[]{:S(2)}, u32[]{:S(2)}) %collective-permute-start.9) | collective-permute-done | bytes 45088 | tf_op jit(solution)/shard_map/ppermute | solution.py:359
  60.2 6.7 %all-to-all-start.1 = ((bf16[8,8,1408]{2,1,0:T(8,128)(2,1)}), bf16[8,8,1408]{2,1,0:T(8,128)(2,1)S(1)}, u32[]{:S(2)}, u32[]{:S(2)}) async-start(bf16[8,8,1408]{2,1,0:T(8,128)(2,1)} %bitcast.8), calls=%async_computation.1 | async-start | bytes 360448 | tf_op jit(solution)/shard_map/all_to_all | solution.py:519
  66.9 4.3 %shard_map.155.mass_ref = bf16[32,128,128]{2,1,0:T(8,128)(2,1)S(1)} custom-call(bf16[118,128]{1,0:T(8,128)(2,1)S(1)} %bitcast.16, s32[118,128]{1,0:T(8,128)S(1)} %copy-done), custom_call_target="tpu_custom_call" | custom-call | flops 500000000 | bytes 2000000 | tf_op jit(solution)/shard_map/pallas_call | solution.py:332
  71.2 4.7 %shard_map.156 = (f32[80,128]{1,0:T(8,128)}, f32[118,128]{1,0:T(8,128)S(1)}) custom-call(bf16[32,80,128]{2,1,0:T(8,128)(2,1)S(1)} %all-to-all-done.blocks_ref, bf16[32,128,128]{2,1,0:T(8,128)(2,1)S(1)} %shard_map.155.mass_ref, bf16[80,128]{1,0:T(8,128)(2,1)S(1)} %bitcast.17, s32[118,128]{1,0:T(8,128)S(1)} %copy-done), custom_call_target="tpu_custom_call" | custom-call | flops 1500000000 | bytes 2000000 | tf_op jit(solution)/shard_map/pallas_call | solution.py:332
  76.1 2.7 %collective-permute-start.12 = (f32[8,1408]{1,0:T(8,128)S(1)}, f32[8,1408]{1,0:T(8,128)S(1)}, u32[]{:S(2)}, u32[]{:S(2)}) collective-permute-start(f32[8,1408]{1,0:T(8,128)S(1)} %shard_map.157.refs_0_), channel_id=1, source_target_pairs={{0,4},{1,5},{2,6},{3,7},{4,0},{5,1},{6,2},{7,3},{8,12},{9,13},{10,... | collective-permute-start | bytes 135176 | tf_op jit(solution)/shard_map/ppermute | solution.py:359
  78.8 2.0 %collective-permute-start.13 = (f32[8,1408]{1,0:T(8,128)S(1)}, f32[8,1408]{1,0:T(8,128)S(1)}, u32[]{:S(2)}, u32[]{:S(2)}) collective-permute-start(f32[8,1408]{1,0:T(8,128)S(1)} %shard_map.157.refs_0_), channel_id=1, source_target_pairs={{0,6},{1,7},{2,4},{3,5},{4,2},{5,3},{6,0},{7,1},{8,14},{9,15},{10,... | collective-permute-start | bytes 135176 | tf_op jit(solution)/shard_map/ppermute | solution.py:359
  81.7 2.3 %collective-permute-done.13.refs_3_ = f32[8,1408]{1,0:T(8,128)S(1)} collective-permute-done((f32[8,1408]{1,0:T(8,128)S(1)}, f32[8,1408]{1,0:T(8,128)S(1)}, u32[]{:S(2)}, u32[]{:S(2)}) %collective-permute-start.13) | collective-permute-done | bytes 45088 | tf_op jit(solution)/shard_map/ppermute | solution.py:359
  (28 shorter events, 5.5 us)
Async XLA Ops:
  1.7 5.9 %collective-permute-start = (bf16[3,128,256]{2,1,0:T(8,128)(2,1)S(1)}, bf16[3,128,256]{2,1,0:T(8,128)(2,1)S(1)}, u32[]{:S(2)}, u32[]{:S(2)}) collective-permute-start(bf16[3,128,256]{2,1,0:T(8,128)(2,1)S(1)} %get-tuple-element.37), channel_id=1, source_target_pairs={{0,8},{8,0},{16,24},{24,16},{32,40},{40,32},{48,56},{56,48},{64,72... | collective-permute-start | bytes 589832 | tf_op jit(solution)/shard_map/ppermute | solution.py:359
  1.8 8.7 %collective-permute-start.1 = (bf16[3,128,256]{2,1,0:T(8,128)(2,1)S(1)}, bf16[3,128,256]{2,1,0:T(8,128)(2,1)S(1)}, u32[]{:S(2)}, u32[]{:S(2)}) collective-permute-start(bf16[3,128,256]{2,1,0:T(8,128)(2,1)S(1)} %get-tuple-element.38), channel_id=1, source_target_pairs={{8,16},{24,32},{40,48},{56,64},{72,80},{88,96},{104,112},{120,128}... | collective-permute-start | bytes 589832 | tf_op jit(solution)/shard_map/ppermute | solution.py:441
  15.3 10.3 %collective-permute-start.2 = (bf16[4,128,1408]{2,1,0:T(8,128)(2,1)}, bf16[4,128,1408]{2,1,0:T(8,128)(2,1)S(1)}, u32[]{:S(2)}, u32[]{:S(2)}) collective-permute-start(bf16[4,128,1408]{2,1,0:T(8,128)(2,1)} %get-tuple-element.44), channel_id=1, source_target_pairs={{0,8},{8,0},{16,24},{24,16},{32,40},{40,32},{48,56},{56,48},{64,72... | collective-permute-start | bytes 4325384 | tf_op jit(solution)/shard_map/ppermute | solution.py:359
  15.7 44.5 %all-to-all-start = ((bf16[32,80,128]{2,1,0:T(8,128)(2,1)}), bf16[32,80,128]{2,1,0:T(8,128)(2,1)S(1)}, u32[]{:S(2)}, u32[]{:S(2)}) async-start(bf16[32,80,128]{2,1,0:T(8,128)(2,1)} %get-tuple-element.42), calls=%async_computation | async-start | bytes 1310720 | tf_op jit(solution)/shard_map/all_to_all | solution.py:355
  25.9 10.5 %collective-permute-start.3 = (bf16[2,64,1408]{2,1,0:T(8,128)(2,1)S(1)}, bf16[2,64,1408]{2,1,0:T(8,128)(2,1)S(1)}, u32[]{:S(2)}, u32[]{:S(2)}) collective-permute-start(bf16[2,64,1408]{2,1,0:T(8,128)(2,1)S(1)} %get-tuple-element.47), channel_id=1, source_target_pairs={{0,2},{1,3},{2,0},{3,1},{4,6},{5,7},{6,4},{7,5},{8,10},{9,11},{10,... | collective-permute-start | bytes 1081352 | tf_op jit(solution)/shard_map/ppermute | solution.py:359
  27.5 11.4 %collective-permute-start.4 = (bf16[2,64,1408]{2,1,0:T(8,128)(2,1)S(1)}, bf16[2,64,1408]{2,1,0:T(8,128)(2,1)S(1)}, u32[]{:S(2)}, u32[]{:S(2)}) collective-permute-start(bf16[2,64,1408]{2,1,0:T(8,128)(2,1)S(1)} %get-tuple-element.48), channel_id=1, source_target_pairs={{0,6},{1,7},{2,4},{3,5},{4,2},{5,3},{6,0},{7,1},{8,14},{9,15},{10,... | collective-permute-start | bytes 1081352 | tf_op jit(solution)/shard_map/ppermute | solution.py:359
  38.9 27.9 %copy-start = (s32[118,128]{1,0:T(8,128)S(1)}, s32[118,128]{1,0:T(8,128)}, u32[]{:S(2)}) copy-start(s32[118,128]{1,0:T(8,128)} %slot_ref.3) | copy-start | bytes 181252
  39.0 27.9 %copy-start.1 = (bf16[1,118,128]{2,1,0:T(8,128)(2,1)S(1)}, bf16[1,118,128]{2,1,0:T(8,128)(2,1)}, u32[]{:S(2)}) copy-start(bf16[1,118,128]{2,1,0:T(8,128)(2,1)} %param.18) | copy-start | bytes 90628
  39.0 6.8 %collective-permute-start.5 = (bf16[64,1408]{1,0:T(8,128)(2,1)S(1)}, bf16[64,1408]{1,0:T(8,128)(2,1)S(1)}, u32[]{:S(2)}, u32[]{:S(2)}) collective-permute-start(bf16[64,1408]{1,0:T(8,128)(2,1)S(1)} %get-tuple-element.50), channel_id=1, source_target_pairs={{0,6},{1,7},{2,4},{3,5},{4,2},{5,3},{6,0},{7,1},{8,14},{9,15},{10,... | collective-permute-start | bytes 540680 | tf_op jit(solution)/shard_map/ppermute | solution.py:359
  41.1 5.5 %collective-permute-start.6 = (bf16[64,1408]{1,0:T(8,128)(2,1)S(1)}, bf16[64,1408]{1,0:T(8,128)(2,1)S(1)}, u32[]{:S(2)}, u32[]{:S(2)}) collective-permute-start(bf16[64,1408]{1,0:T(8,128)(2,1)S(1)} %get-tuple-element.51), channel_id=1, source_target_pairs={{0,2},{1,3},{2,0},{3,1},{4,6},{5,7},{6,4},{7,5},{8,10},{9,11},{10,... | collective-permute-start | bytes 540680 | tf_op jit(solution)/shard_map/ppermute | solution.py:359
  46.7 4.6 %collective-permute-start.7 = (bf16[2,16,1408]{2,1,0:T(8,128)(2,1)S(1)}, bf16[2,16,1408]{2,1,0:T(8,128)(2,1)S(1)}, u32[]{:S(2)}, u32[]{:S(2)}) collective-permute-start(bf16[2,16,1408]{2,1,0:T(8,128)(2,1)S(1)} %get-tuple-element.54), channel_id=1, source_target_pairs={{0,64},{8,72},{16,80},{24,88},{32,96},{40,104},{48,112},{56,120},{... | collective-permute-start | bytes 270344 | tf_op jit(solution)/shard_map/ppermute | solution.py:359
  48.3 5.7 %collective-permute-start.8 = (bf16[2,16,1408]{2,1,0:T(8,128)(2,1)S(1)}, bf16[2,16,1408]{2,1,0:T(8,128)(2,1)S(1)}, u32[]{:S(2)}, u32[]{:S(2)}) collective-permute-start(bf16[2,16,1408]{2,1,0:T(8,128)(2,1)S(1)} %get-tuple-element.55), channel_id=1, source_target_pairs={{0,192},{8,200},{16,208},{24,216},{32,224},{40,232},{48,240},{56,2... | collective-permute-start | bytes 270344 | tf_op jit(solution)/shard_map/ppermute | solution.py:359
  54.1 17.2 %copy-start.2 = (bf16[1,80,128]{2,1,0:T(8,128)(2,1)S(1)}, bf16[1,80,128]{2,1,0:T(8,128)(2,1)}, u32[]{:S(2)}) copy-start(bf16[1,80,128]{2,1,0:T(8,128)(2,1)} %param.19) | copy-start | bytes 61444
  54.1 4.1 %collective-permute-start.10 = (bf16[16,1408]{1,0:T(8,128)(2,1)S(1)}, bf16[16,1408]{1,0:T(8,128)(2,1)S(1)}, u32[]{:S(2)}, u32[]{:S(2)}) collective-permute-start(bf16[16,1408]{1,0:T(8,128)(2,1)S(1)} %get-tuple-element.58), channel_id=1, source_target_pairs={{0,64},{8,72},{16,80},{24,88},{32,96},{40,104},{48,112},{56,120},{... | collective-permute-start | bytes 135176 | tf_op jit(solution)/shard_map/ppermute | solution.py:359
  54.2 5.3 %collective-permute-start.9 = (bf16[16,1408]{1,0:T(8,128)(2,1)S(1)}, bf16[16,1408]{1,0:T(8,128)(2,1)S(1)}, u32[]{:S(2)}, u32[]{:S(2)}) collective-permute-start(bf16[16,1408]{1,0:T(8,128)(2,1)S(1)} %get-tuple-element.57), channel_id=1, source_target_pairs={{0,192},{8,200},{16,208},{24,216},{32,224},{40,232},{48,240},{56,2... | collective-permute-start | bytes 135176 | tf_op jit(solution)/shard_map/ppermute | solution.py:359
  60.2 15.7 %all-to-all-start.1 = ((bf16[8,8,1408]{2,1,0:T(8,128)(2,1)}), bf16[8,8,1408]{2,1,0:T(8,128)(2,1)S(1)}, u32[]{:S(2)}, u32[]{:S(2)}) async-start(bf16[8,8,1408]{2,1,0:T(8,128)(2,1)} %bitcast.8), calls=%async_computation.1 | async-start | bytes 360448 | tf_op jit(solution)/shard_map/all_to_all | solution.py:519
  76.0 5.5 %collective-permute-start.11 = (f32[8,1408]{1,0:T(8,128)S(1)}, f32[8,1408]{1,0:T(8,128)S(1)}, u32[]{:S(2)}, u32[]{:S(2)}) collective-permute-start(f32[8,1408]{1,0:T(8,128)S(1)} %shard_map.157.refs_0_), channel_id=1, source_target_pairs={{0,2},{1,3},{2,0},{3,1},{4,6},{5,7},{6,4},{7,5},{8,10},{9,11},{10,... | collective-permute-start | bytes 135176 | tf_op jit(solution)/shard_map/ppermute | solution.py:359
  76.1 5.6 %collective-permute-start.12 = (f32[8,1408]{1,0:T(8,128)S(1)}, f32[8,1408]{1,0:T(8,128)S(1)}, u32[]{:S(2)}, u32[]{:S(2)}) collective-permute-start(f32[8,1408]{1,0:T(8,128)S(1)} %shard_map.157.refs_0_), channel_id=1, source_target_pairs={{0,4},{1,5},{2,6},{3,7},{4,0},{5,1},{6,2},{7,3},{8,12},{9,13},{10,... | collective-permute-start | bytes 135176 | tf_op jit(solution)/shard_map/ppermute | solution.py:359
  78.8 5.3 %collective-permute-start.13 = (f32[8,1408]{1,0:T(8,128)S(1)}, f32[8,1408]{1,0:T(8,128)S(1)}, u32[]{:S(2)}, u32[]{:S(2)}) collective-permute-start(f32[8,1408]{1,0:T(8,128)S(1)} %shard_map.157.refs_0_), channel_id=1, source_target_pairs={{0,6},{1,7},{2,4},{3,5},{4,2},{5,3},{6,0},{7,1},{8,14},{9,15},{10,... | collective-permute-start | bytes 135176 | tf_op jit(solution)/shard_map/ppermute | solution.py:359

commit v7 on v4

--- a/solution.py
+++ b/solution.py
@@ -221,7 +221,7 @@
         d_ref[pl.ds(base, 8), :] = jnp.concatenate(found_rows, axis=0)
         return carry
 
-    lax.fori_loop(0, pix // 8, pixels, 0)
+    lax.fori_loop(0, pix // 8, pixels, 0, unroll=2)
     gd_ref[...] = d_ref[...].T[:depth]
     total = jnp.zeros((cam, pix), f32)
     for s in range(sources):
@@ -247,19 +247,16 @@
         next_ref[here] = added(keep_ref, other_ref, part, here)
 
 
-def second_sum(own_ref, next_ref, a_ref, b_ref, out_ref, a_out_ref, b_out_ref):
-    rows = a_ref.shape[1]
-    upper, lower = slice(0, rows), slice(rows, 2 * rows)
-    a_out_ref[...] = (next_ref[upper] + a_ref[1].astype(f32)).astype(bf16)
-    b_out_ref[...] = (next_ref[lower] + b_ref[1].astype(f32)).astype(bf16)
-    out_ref[upper] = own_ref[upper] + a_ref[0].astype(f32)
-    out_ref[lower] = own_ref[lower] + b_ref[0].astype(f32)
-
-
-def third_sum(own_ref, a_ref, b_ref, out_ref):
+def second_sum(first_row, own_ref, next_ref, came_ref, out_ref, send_ref):
+    here = slice(first_row, first_row + out_ref.shape[0])
+    send_ref[...] = (next_ref[here] + came_ref[1].astype(f32)).astype(bf16)
+    out_ref[...] = own_ref[here] + came_ref[0].astype(f32)
+
+
+def third_sum(own_a_ref, own_b_ref, a_ref, b_ref, out_ref):
     rows = a_ref.shape[0]
-    out_ref[:rows] = (own_ref[:rows] + a_ref[...].astype(f32)).astype(bf16)
-    out_ref[rows:] = (own_ref[rows:] + b_ref[...].astype(f32)).astype(bf16)
+    out_ref[:rows] = (own_a_ref[...] + a_ref[...].astype(f32)).astype(bf16)
+    out_ref[rows:] = (own_b_ref[...] + b_ref[...].astype(f32)).astype(bf16)
 
 
 def place_sum(parts_ref, out_ref):
@@ -321,15 +318,15 @@
     deep = rows // 2
     other = swapped(send, "space", lambda i: i ^ 1)
     a, b = small(first_sum, [((2, deep, per_part), bf16)] * 2, (keep, other))
-    a, b = swapped(a, "scene", lambda i: i ^ 2), swapped(b, "scene", lambda i: i ^ 6)
+    a = swapped(a, "scene", lambda i: i ^ 2)
+    b = swapped(b, "scene", lambda i: i ^ 6)
     kept = small(kept_sum, [((2 * deep, per_part), f32)] * 2, (keep, other))
-    own, a, b = small(
-        second_sum,
-        [((2 * deep, per_part), f32), ((deep, per_part), bf16), ((deep, per_part), bf16)],
-        (*kept, a, b),
-    )
-    a, b = swapped(a, "scene", lambda i: i ^ 6), swapped(b, "scene", lambda i: i ^ 2)
-    (part,) = small(third_sum, [((2 * deep, per_part), bf16)], (own, a, b))
+    halves = [((deep, per_part), f32), ((deep, per_part), bf16)]
+    own_a, a = small(functools.partial(second_sum, 0), halves, (*kept, a))
+    a = swapped(a, "scene", lambda i: i ^ 6)
+    own_b, b = small(functools.partial(second_sum, deep), halves, (*kept, b))
+    b = swapped(b, "scene", lambda i: i ^ 2)
+    (part,) = small(third_sum, [((2 * deep, per_part), bf16)], (own_a, own_b, a, b))
     return part
 
 

time: 81.7 us -> 80.3 us (0.983)
  starting transfers between devices: 40.9 us -> 39.4 us
  waiting for transfers between devices: 21.7 us -> 22.8 us
  Pallas kernels: 17.3 us -> 16.3 us
    all_to_all x2, waiting for transfers between devices: 3.69 us -> 5.19 us  [exchanged(): return lax.all_to_all(x, axis, 0, 0, axis_index_groups=groups, tiled=True)]
    ppermute x10, starting transfers between devices: 21.4 us -> 20.3 us  [swapped(): lax.ppermute(x, axis, [(i, partner(i)) for i in range(lax.axis_size(axis))])]
    pallas_call x11 -> x12, Pallas kernels: 17.3 us -> 16.3 us  [call(): pl.pallas_call(kernel, out_shape=outs, in_specs=specs, out_specs=outs_at...]
  transfers between devices with their start and end apart: 13 -> 13, of which waited for: 8 -> 8; matrix products, arithmetic and copies ran while one was open for 1% -> 1% of each run, Pallas kernels for 13% -> 12%
where the time goes in v7:
time: 80.3 us; the launch traced here: 79.9 us
  starting transfers between devices  39.4 us (49%)
  waiting for transfers between devices  22.8 us (28%)
  Pallas kernels  16.3 us (20%)
    ppermute x10, starting transfers between devices, swapped(): lax.ppermute(x, axis, [(i, partner(i)) for i in range(lax.axis_size(axis))])  20.3 us
    all_to_all x2, starting transfers between devices, exchanged(): return lax.all_to_all(x, axis, 0, 0, axis_index_groups=groups, tiled=True)  18.4 us
    ppermute x10, waiting for transfers between devices, swapped(): lax.ppermute(x, axis, [(i, partner(i)) for i in range(lax.axis_size(axis))])  17.6 us
    pallas_call x12, Pallas kernels, call(): pl.pallas_call(kernel, out_shape=outs, in_specs=specs, out_specs=outs_at...  16.3 us
    all_to_all x2, waiting for transfers between devices, exchanged(): return lax.all_to_all(x, axis, 0, 0, axis_index_groups=groups, tiled=True)  5.19 us
  transfers between devices with their start and end apart: 13, of which 8 were waited for; matrix products, arithmetic and copies ran while one was open for 1% of the time, Pallas kernels for 12%

profile of v7, /device:TPU:2, one launch (start us, length us, event | category | flops | bytes accessed | tf_op | source)
XLA Modules:
  0.0 79.9 jit_solution(2851851566216652077)
XLA Ops:
  0.6 1.1 %shard_map.146 = (bf16[3,128,256]{2,1,0:T(8,128)(2,1)S(1)}, bf16[3,128,256]{2,1,0:T(8,128)(2,1)S(1)}) custom-call(bf16[2,128,256]{2,1,0:T(8,128)(2,1)} %bitcast.18, bf16[2,128,256]{2,1,0:T(8,128)(2,1)} %bitcast.20, bf16[2,128,256]{2,1,0:T(8,128)(2,1)} %bitcast.22), custom_call_target="tpu_custom_call" | custom-call | flops 1000000 | bytes 1000000 | tf_op jit(solution)/shard_map/pallas_call | solution.py:286
  1.8 0.7 collective-permute-start.1
  2.5 1.9 %shard_map.147 = (f32[512,256]{1,0:T(8,128)S(1)}, bf16[3,256,256]{2,1,0:T(8,128)(2,1)S(1)}, bf16[256,2304]{1,0:T(8,128)(2,1)S(1)}) custom-call(bf16[2,128,256]{2,1,0:T(8,128)(2,1)} %bitcast.19, bf16[2,128,256]{2,1,0:T(8,128)(2,1)} %bitcast.21, bf16[256,2304]{1,0:T(8,128)(2,1)} %wb_hbm.1), custom_call_target="tpu_custom_call" | custom-call | flops 300000000 | bytes 2500000 | tf_op jit(solution)/shard_map/pallas_call | solution.py:286
  4.5 4.8 %shard_map.148 = (bf16[2,128,256]{2,1,0:T(8,128)(2,1)}, bf16[32,80,128]{2,1,0:T(8,128)(2,1)}, bf16[4,128,1408]{2,1,0:T(8,128)(2,1)S(1)}, bf16[4,128,1408]{2,1,0:T(8,128)(2,1)}) custom-call(bf16[3,128,256]{2,1,0:T(8,128)(2,1)S(1)} %collective-permute-done.near_ref, bf16[3,128,256]{2,1,0:T(8,128)(2,1)S(1)} %collective-permute-done.1.far_ref, ...), custom_call_target="tpu_custom_call" | custom-call | flops 1500000000 | bytes 12000000 | tf_op jit(solution)/shard_map/pallas_call | solution.py:286
  9.3 4.9 %collective-permute-start.2 = (bf16[4,128,1408]{2,1,0:T(8,128)(2,1)}, bf16[4,128,1408]{2,1,0:T(8,128)(2,1)S(1)}, u32[]{:S(2)}, u32[]{:S(2)}) collective-permute-start(bf16[4,128,1408]{2,1,0:T(8,128)(2,1)} %get-tuple-element.38), channel_id=1, source_target_pairs={{0,8},{8,0},{16,24},{24,16},{32,40},{40,32},{48,56},{56,48},{64,72... | collective-permute-start | bytes 4325384 | tf_op jit(solution)/shard_map/ppermute | solution.py:313
  14.2 11.6 %all-to-all-start = ((bf16[32,80,128]{2,1,0:T(8,128)(2,1)}), bf16[32,80,128]{2,1,0:T(8,128)(2,1)S(1)}, u32[]{:S(2)}, u32[]{:S(2)}) async-start(bf16[32,80,128]{2,1,0:T(8,128)(2,1)} %get-tuple-element.36), calls=%async_computation | async-start | bytes 1310720 | tf_op jit(solution)/shard_map/all_to_all | solution.py:309
  26.6 2.1 %collective-permute-start.4 = (bf16[2,64,1408]{2,1,0:T(8,128)(2,1)S(1)}, bf16[2,64,1408]{2,1,0:T(8,128)(2,1)S(1)}, u32[]{:S(2)}, u32[]{:S(2)}) collective-permute-start(bf16[2,64,1408]{2,1,0:T(8,128)(2,1)S(1)} %get-tuple-element.43), channel_id=1, source_target_pairs={{0,6},{1,7},{2,4},{3,5},{4,2},{5,3},{6,0},{7,1},{8,14},{9,15},{10,... | collective-permute-start | bytes 1081352 | tf_op jit(solution)/shard_map/ppermute | solution.py:313
  28.9 7.8 %collective-permute-done.3.came_ref = bf16[2,64,1408]{2,1,0:T(8,128)(2,1)S(1)} collective-permute-done((bf16[2,64,1408]{2,1,0:T(8,128)(2,1)S(1)}, bf16[2,64,1408]{2,1,0:T(8,128)(2,1)S(1)}, u32[]{:S(2)}, u32[]{:S(2)}) %collective-permute-start.3) | collective-permute-done | bytes 360480 | tf_op jit(solution)/shard_map/ppermute | solution.py:313
  36.8 1.6 %collective-permute-start.5 = (bf16[64,1408]{1,0:T(8,128)(2,1)S(1)}, bf16[64,1408]{1,0:T(8,128)(2,1)S(1)}, u32[]{:S(2)}, u32[]{:S(2)}) collective-permute-start(bf16[64,1408]{1,0:T(8,128)(2,1)S(1)} %get-tuple-element.45), channel_id=1, source_target_pairs={{0,6},{1,7},{2,4},{3,5},{4,2},{5,3},{6,0},{7,1},{8,14},{9,15},{10,... | collective-permute-start | bytes 540680 | tf_op jit(solution)/shard_map/ppermute | solution.py:313
  38.4 1.9 %collective-permute-start.6 = (bf16[64,1408]{1,0:T(8,128)(2,1)S(1)}, bf16[64,1408]{1,0:T(8,128)(2,1)S(1)}, u32[]{:S(2)}, u32[]{:S(2)}) collective-permute-start(bf16[64,1408]{1,0:T(8,128)(2,1)S(1)} %get-tuple-element.46), channel_id=1, source_target_pairs={{0,2},{1,3},{2,0},{3,1},{4,6},{5,7},{6,4},{7,5},{8,10},{9,11},{10,... | collective-permute-start | bytes 540680 | tf_op jit(solution)/shard_map/ppermute | solution.py:313
  40.3 2.4 %collective-permute-done.5.a_ref = bf16[64,1408]{1,0:T(8,128)(2,1)S(1)} collective-permute-done((bf16[64,1408]{1,0:T(8,128)(2,1)S(1)}, bf16[64,1408]{1,0:T(8,128)(2,1)S(1)}, u32[]{:S(2)}, u32[]{:S(2)}) %collective-permute-start.5) | collective-permute-done | bytes 180256 | tf_op jit(solution)/shard_map/ppermute | solution.py:313
  42.7 1.4 %collective-permute-done.6.b_ref = bf16[64,1408]{1,0:T(8,128)(2,1)S(1)} collective-permute-done((bf16[64,1408]{1,0:T(8,128)(2,1)S(1)}, bf16[64,1408]{1,0:T(8,128)(2,1)S(1)}, u32[]{:S(2)}, u32[]{:S(2)}) %collective-permute-start.6) | collective-permute-done | bytes 180256 | tf_op jit(solution)/shard_map/ppermute | solution.py:313
  44.1 0.8 shard_map.153
  45.2 6.8 %all-to-all-start.1 = ((bf16[16,8,1408]{2,1,0:T(8,128)(2,1)}), bf16[16,8,1408]{2,1,0:T(8,128)(2,1)S(1)}, u32[]{:S(2)}, u32[]{:S(2)}) async-start(bf16[16,8,1408]{2,1,0:T(8,128)(2,1)} %bitcast.8), calls=%async_computation.1 | async-start | bytes 720896 | tf_op jit(solution)/shard_map/all_to_all | solution.py:309
  52.1 6.4 %shard_map.154 = (f32[80,128]{1,0:T(8,128)}, f32[118,128]{1,0:T(8,128)S(1)}) custom-call(bf16[32,80,128]{2,1,0:T(8,128)(2,1)S(1)} %all-to-all-done.blocks_ref, bf16[118,128]{1,0:T(8,128)(2,1)S(1)} %bitcast.16, bf16[80,128]{1,0:T(8,128)(2,1)S(1)} %bitcast.17, s32[118,128]{1,0:T(8,128)S(1)} %copy-done), custom_call_target="tpu_custom_call" | custom-call | flops 2000000000 | bytes 2000000 | tf_op jit(solution)/shard_map/pallas_call | solution.py:286
  58.5 4.9 %all-to-all-done.1.parts_ref = bf16[16,8,1408]{2,1,0:T(8,128)(2,1)S(1)} async-done(((bf16[16,8,1408]{2,1,0:T(8,128)(2,1)}), bf16[16,8,1408]{2,1,0:T(8,128)(2,1)S(1)}, u32[]{:S(2)}, u32[]{:S(2)}) %all-to-all-start.1) | async-done | bytes 360480 | tf_op jit(solution)/shard_map/all_to_all | solution.py:309
  63.4 4.9 %collective-permute-start.7 = (bf16[8,1408]{1,0:T(8,128)(2,1)S(1)}, bf16[8,1408]{1,0:T(8,128)(2,1)S(1)}, u32[]{:S(2)}, u32[]{:S(2)}) collective-permute-start(bf16[8,1408]{1,0:T(8,128)(2,1)S(1)} %shard_map.155.one_ref), channel_id=1, source_target_pairs={{0,1},{1,0},{2,3},{3,2},{4,5},{5,4},{6,7},{7,6},{8,9},{9,8},{10,11... | collective-permute-start | bytes 67592 | tf_op jit(solution)/shard_map/ppermute | solution.py:313
  68.4 2.9 %collective-permute-done.7.two_ref = bf16[8,1408]{1,0:T(8,128)(2,1)S(1)} collective-permute-done((bf16[8,1408]{1,0:T(8,128)(2,1)S(1)}, bf16[8,1408]{1,0:T(8,128)(2,1)S(1)}, u32[]{:S(2)}, u32[]{:S(2)}) %collective-permute-start.7) | collective-permute-done | bytes 22560 | tf_op jit(solution)/shard_map/ppermute | solution.py:313
  71.3 1.3 %collective-permute-start.10 = (f32[8,1408]{1,0:T(8,128)S(1)}, f32[8,1408]{1,0:T(8,128)S(1)}, u32[]{:S(2)}, u32[]{:S(2)}) collective-permute-start(f32[8,1408]{1,0:T(8,128)S(1)} %shard_map.156.refs_0_), channel_id=1, source_target_pairs={{0,6},{1,7},{2,4},{3,5},{4,2},{5,3},{6,0},{7,1},{8,14},{9,15},{10,... | collective-permute-start | bytes 135176 | tf_op jit(solution)/shard_map/ppermute | solution.py:313
  72.6 2.5 %collective-permute-start.9 = (f32[8,1408]{1,0:T(8,128)S(1)}, f32[8,1408]{1,0:T(8,128)S(1)}, u32[]{:S(2)}, u32[]{:S(2)}) collective-permute-start(f32[8,1408]{1,0:T(8,128)S(1)} %shard_map.156.refs_0_), channel_id=1, source_target_pairs={{0,4},{1,5},{2,6},{3,7},{4,0},{5,1},{6,2},{7,3},{8,12},{9,13},{10,... | collective-permute-start | bytes 135176 | tf_op jit(solution)/shard_map/ppermute | solution.py:313
  75.4 0.7 copy.16
  76.1 2.0 %collective-permute-done.9.refs_2_ = f32[8,1408]{1,0:T(8,128)S(1)} collective-permute-done((f32[8,1408]{1,0:T(8,128)S(1)}, f32[8,1408]{1,0:T(8,128)S(1)}, u32[]{:S(2)}, u32[]{:S(2)}) %collective-permute-start.9) | collective-permute-done | bytes 45088 | tf_op jit(solution)/shard_map/ppermute | solution.py:313
  78.2 1.0 %collective-permute-done.8.refs_1_ = f32[8,1408]{1,0:T(8,128)S(1)} collective-permute-done((f32[8,1408]{1,0:T(8,128)S(1)}, f32[8,1408]{1,0:T(8,128)S(1)}, u32[]{:S(2)}, u32[]{:S(2)}) %collective-permute-start.8) | collective-permute-done | bytes 45088 | tf_op jit(solution)/shard_map/ppermute | solution.py:313
  79.2 0.8 shard_map.157
  (21 shorter events, 1.8 us)
Async XLA Ops:
  1.7 2.7 %collective-permute-start = (bf16[3,128,256]{2,1,0:T(8,128)(2,1)S(1)}, bf16[3,128,256]{2,1,0:T(8,128)(2,1)S(1)}, u32[]{:S(2)}, u32[]{:S(2)}) collective-permute-start(bf16[3,128,256]{2,1,0:T(8,128)(2,1)S(1)} %get-tuple-element.31), channel_id=1, source_target_pairs={{0,8},{8,0},{16,24},{24,16},{32,40},{40,32},{48,56},{56,48},{64,72... | collective-permute-start | bytes 589832 | tf_op jit(solution)/shard_map/ppermute | solution.py:313
  1.8 2.6 %collective-permute-start.1 = (bf16[3,128,256]{2,1,0:T(8,128)(2,1)S(1)}, bf16[3,128,256]{2,1,0:T(8,128)(2,1)S(1)}, u32[]{:S(2)}, u32[]{:S(2)}) collective-permute-start(bf16[3,128,256]{2,1,0:T(8,128)(2,1)S(1)} %get-tuple-element.32), channel_id=1, source_target_pairs={{8,16},{24,32},{40,48},{56,64},{72,80},{88,96},{104,112},{120,128}... | collective-permute-start | bytes 589832 | tf_op jit(solution)/shard_map/ppermute | solution.py:373
  9.3 16.5 %collective-permute-start.2 = (bf16[4,128,1408]{2,1,0:T(8,128)(2,1)}, bf16[4,128,1408]{2,1,0:T(8,128)(2,1)S(1)}, u32[]{:S(2)}, u32[]{:S(2)}) collective-permute-start(bf16[4,128,1408]{2,1,0:T(8,128)(2,1)} %get-tuple-element.38), channel_id=1, source_target_pairs={{0,8},{8,0},{16,24},{24,16},{32,40},{40,32},{48,56},{56,48},{64,72... | collective-permute-start | bytes 4325384 | tf_op jit(solution)/shard_map/ppermute | solution.py:313
  14.2 31.0 %all-to-all-start = ((bf16[32,80,128]{2,1,0:T(8,128)(2,1)}), bf16[32,80,128]{2,1,0:T(8,128)(2,1)S(1)}, u32[]{:S(2)}, u32[]{:S(2)}) async-start(bf16[32,80,128]{2,1,0:T(8,128)(2,1)} %get-tuple-element.36), calls=%async_computation | async-start | bytes 1310720 | tf_op jit(solution)/shard_map/all_to_all | solution.py:309
  26.0 10.7 %collective-permute-start.3 = (bf16[2,64,1408]{2,1,0:T(8,128)(2,1)S(1)}, bf16[2,64,1408]{2,1,0:T(8,128)(2,1)S(1)}, u32[]{:S(2)}, u32[]{:S(2)}) collective-permute-start(bf16[2,64,1408]{2,1,0:T(8,128)(2,1)S(1)} %get-tuple-element.41), channel_id=1, source_target_pairs={{0,2},{1,3},{2,0},{3,1},{4,6},{5,7},{6,4},{7,5},{8,10},{9,11},{10,... | collective-permute-start | bytes 1081352 | tf_op jit(solution)/shard_map/ppermute | solution.py:313
  26.6 11.7 %collective-permute-start.4 = (bf16[2,64,1408]{2,1,0:T(8,128)(2,1)S(1)}, bf16[2,64,1408]{2,1,0:T(8,128)(2,1)S(1)}, u32[]{:S(2)}, u32[]{:S(2)}) collective-permute-start(bf16[2,64,1408]{2,1,0:T(8,128)(2,1)S(1)} %get-tuple-element.43), channel_id=1, source_target_pairs={{0,6},{1,7},{2,4},{3,5},{4,2},{5,3},{6,0},{7,1},{8,14},{9,15},{10,... | collective-permute-start | bytes 1081352 | tf_op jit(solution)/shard_map/ppermute | solution.py:313
  36.8 6.0 %collective-permute-start.5 = (bf16[64,1408]{1,0:T(8,128)(2,1)S(1)}, bf16[64,1408]{1,0:T(8,128)(2,1)S(1)}, u32[]{:S(2)}, u32[]{:S(2)}) collective-permute-start(bf16[64,1408]{1,0:T(8,128)(2,1)S(1)} %get-tuple-element.45), channel_id=1, source_target_pairs={{0,6},{1,7},{2,4},{3,5},{4,2},{5,3},{6,0},{7,1},{8,14},{9,15},{10,... | collective-permute-start | bytes 540680 | tf_op jit(solution)/shard_map/ppermute | solution.py:313
  38.4 13.7 %copy-start = (s32[118,128]{1,0:T(8,128)S(1)}, s32[118,128]{1,0:T(8,128)}, u32[]{:S(2)}) copy-start(s32[118,128]{1,0:T(8,128)} %slot_ref.1) | copy-start | bytes 181252
  38.4 13.7 %copy-start.1 = (bf16[1,118,128]{2,1,0:T(8,128)(2,1)S(1)}, bf16[1,118,128]{2,1,0:T(8,128)(2,1)}, u32[]{:S(2)}) copy-start(bf16[1,118,128]{2,1,0:T(8,128)(2,1)} %param.18) | copy-start | bytes 90628
  38.4 13.7 %copy-start.2 = (bf16[1,80,128]{2,1,0:T(8,128)(2,1)S(1)}, bf16[1,80,128]{2,1,0:T(8,128)(2,1)}, u32[]{:S(2)}) copy-start(bf16[1,80,128]{2,1,0:T(8,128)(2,1)} %param.19) | copy-start | bytes 61444
  38.4 5.7 %collective-permute-start.6 = (bf16[64,1408]{1,0:T(8,128)(2,1)S(1)}, bf16[64,1408]{1,0:T(8,128)(2,1)S(1)}, u32[]{:S(2)}, u32[]{:S(2)}) collective-permute-start(bf16[64,1408]{1,0:T(8,128)(2,1)S(1)} %get-tuple-element.46), channel_id=1, source_target_pairs={{0,2},{1,3},{2,0},{3,1},{4,6},{5,7},{6,4},{7,5},{8,10},{9,11},{10,... | collective-permute-start | bytes 540680 | tf_op jit(solution)/shard_map/ppermute | solution.py:313
  45.2 18.2 %all-to-all-start.1 = ((bf16[16,8,1408]{2,1,0:T(8,128)(2,1)}), bf16[16,8,1408]{2,1,0:T(8,128)(2,1)S(1)}, u32[]{:S(2)}, u32[]{:S(2)}) async-start(bf16[16,8,1408]{2,1,0:T(8,128)(2,1)} %bitcast.8), calls=%async_computation.1 | async-start | bytes 720896 | tf_op jit(solution)/shard_map/all_to_all | solution.py:309
  63.4 7.8 %collective-permute-start.7 = (bf16[8,1408]{1,0:T(8,128)(2,1)S(1)}, bf16[8,1408]{1,0:T(8,128)(2,1)S(1)}, u32[]{:S(2)}, u32[]{:S(2)}) collective-permute-start(bf16[8,1408]{1,0:T(8,128)(2,1)S(1)} %shard_map.155.one_ref), channel_id=1, source_target_pairs={{0,1},{1,0},{2,3},{3,2},{4,5},{5,4},{6,7},{7,6},{8,9},{9,8},{10,11... | collective-permute-start | bytes 67592 | tf_op jit(solution)/shard_map/ppermute | solution.py:313
  71.3 4.9 %collective-permute-start.10 = (f32[8,1408]{1,0:T(8,128)S(1)}, f32[8,1408]{1,0:T(8,128)S(1)}, u32[]{:S(2)}, u32[]{:S(2)}) collective-permute-start(f32[8,1408]{1,0:T(8,128)S(1)} %shard_map.156.refs_0_), channel_id=1, source_target_pairs={{0,6},{1,7},{2,4},{3,5},{4,2},{5,3},{6,0},{7,1},{8,14},{9,15},{10,... | collective-permute-start | bytes 135176 | tf_op jit(solution)/shard_map/ppermute | solution.py:313
  72.6 5.6 %collective-permute-start.9 = (f32[8,1408]{1,0:T(8,128)S(1)}, f32[8,1408]{1,0:T(8,128)S(1)}, u32[]{:S(2)}, u32[]{:S(2)}) collective-permute-start(f32[8,1408]{1,0:T(8,128)S(1)} %shard_map.156.refs_0_), channel_id=1, source_target_pairs={{0,4},{1,5},{2,6},{3,7},{4,0},{5,1},{6,2},{7,3},{8,12},{9,13},{10,... | collective-permute-start | bytes 135176 | tf_op jit(solution)/shard_map/ppermute | solution.py:313
  75.1 4.0 %collective-permute-start.8 = (f32[8,1408]{1,0:T(8,128)S(1)}, f32[8,1408]{1,0:T(8,128)S(1)}, u32[]{:S(2)}, u32[]{:S(2)}) collective-permute-start(f32[8,1408]{1,0:T(8,128)S(1)} %shard_map.156.refs_0_), channel_id=1, source_target_pairs={{0,2},{1,3},{2,0},{3,1},{4,6},{5,7},{6,4},{7,5},{8,10},{9,11},{10,... | collective-permute-start | bytes 135176 | tf_op jit(solution)/shard_map/ppermute | solution.py:313
